TPU v7x, 128 devices: a whole 4x4x4 slice. The times are simulated.
128 devices in a mesh: section: 8 (over y, z_lo), seq: 2 (over core), tensor: 8 (over z_hi, x).
Axes of the slice: x: 4, y: 4, z: 4 (z_hi: 2, z_lo: 2; z = z_hi * 2 + z_lo), core: 2. Of those that a mesh axis runs over, the one named last changes fastest.
Arguments:
- states_in: bfloat16 [1, 256, 4608], P(None, 'seq', 'tensor'), may hold values from -100 to 100
- span_order: int32 [4], replicated, may hold values from 0 to 3, each once
- pre_gain: bfloat16 [8, 4608], P('section'), may hold values from 0.25 to 1.75
- w_query: bfloat16 [8, 4608, 4096], P('section', None, 'tensor'), may hold values from -0.09375 to 0.09375
- w_key: bfloat16 [8, 4608, 2048], P('section', None, 'tensor'), may hold values from -0.09375 to 0.09375
- w_value: bfloat16 [8, 4608, 2048], P('section', None, 'tensor'), may hold values from -0.09375 to 0.09375
- w_out: bfloat16 [8, 4096, 4608], P('section', 'tensor'), may hold values from -0.125 to 0.125
- post_gain: bfloat16 [8, 4608], P('section'), may hold values from 0.25 to 1.75
Outputs:
- states: bfloat16 [8, 1, 256, 4608], P('section', None, 'seq', 'tensor')
Inputs may be any that keep to these rules, and one draw needn't show every extreme that they name: Each span number appears once; row block j of 64 rows holds the tokens from position span_order[j] * 64 on.
All inputs are finite; a program needn't handle non-finite values.
Results may differ from a plain program's by a relative error of at most 0.024.
Values may be sent and summed in bfloat16 or wider, within the bound.
No kernel may reach another device: no remote copies, remote signals or barrier semaphores. Data moves between devices by JAX's collectives and lax.ppermute only.
A program may use at most 64 MiB of HBM per device.

v0:
```python
import jax
import jax.numpy as jnp
from jax import lax
from jax.sharding import PartitionSpec as P

HEAD_DIM = 128


softcap_limit = 50.0
query_scale = 144.0 ** (-0.5)
epsilon = 1e-06
rotary_base = 10000.0


def sent_together(arrays, axis, dim, along):
    ends, at = ([], 0)
    for a in arrays[:-1]:
        at += a.shape[along]
        ends.append(at)
    both = jnp.concatenate(arrays, axis=along)
    return tuple(jnp.split(lax.all_gather(both, axis, axis=dim, tiled=True), ends, axis=along))


def in_blocks(x, dim, size):
    lengths = x.shape
    pieces = x.reshape(*lengths[:dim], size, lengths[dim] // size, *lengths[dim + 1 :])
    return jnp.moveaxis(pieces, dim, 0)


def sent_and_summed(x, axis, dim):
    pieces = in_blocks(x, dim, lax.axis_size(axis))
    arrived = lax.all_to_all(pieces, axis, split_axis=0, concat_axis=0, tiled=True)
    return arrived.astype(jnp.float32).sum(axis=0)


def from_everyone(x, axis):
    size = lax.axis_size(axis)
    return lax.all_to_all(jnp.broadcast_to(x[None], (size, *x.shape)), axis, 0, 0, tiled=True)


def of_everyone(x, axis):
    return from_everyone(x, axis).sum(axis=0)


def from_behind(value, axis, steps):
    count = lax.axis_size(axis)
    first, last = (max(0, -steps), min(count, count - steps))
    return lax.ppermute(value, axis, [(source, source + steps) for source in range(first, last)])


def in_order(pieces, dim):
    lengths = list(pieces.shape[1:])
    lengths[dim] *= pieces.shape[0]
    return jnp.moveaxis(pieces, 0, dim).reshape(lengths)


def gather_directly(x, axis, dim):
    return in_order(from_everyone(x, axis), dim)


def rotate(vectors, places):
    half_dim = vectors.shape[-1] // 2
    inverse = rotary_base ** (-(jnp.arange(half_dim, dtype=jnp.float32) * 2.0 / vectors.shape[-1]))
    angles = places.astype(jnp.float32)[:, None] * inverse[None, :]
    cos_part = jnp.cos(angles)[:, None, :]
    sin_part = jnp.sin(angles)[:, None, :]
    lower_half = vectors[..., :half_dim]
    upper_half = vectors[..., half_dim:]
    return jnp.concatenate(
        [
            lower_half * cos_part - upper_half * sin_part,
            upper_half * cos_part + lower_half * sin_part,
        ],
        axis=-1,
    )


def span_positions(first_row, row_total, order_table, span_rows):
    row_ids = first_row + jnp.arange(row_total, dtype=jnp.int32)
    blocks = row_ids // span_rows
    matches = blocks[:, None] == jnp.arange(order_table.shape[0], dtype=jnp.int32)[None, :]
    starts = jnp.sum(jnp.where(matches, order_table[None, :], 0), axis=1)
    return starts * span_rows + row_ids % span_rows


def body(states_in, span_order, pre_gain, w_query, w_key, w_value, w_out, post_gain):
    micro_count, row_count, width_part = states_in.shape
    model_width = pre_gain.shape[1]
    head_size = HEAD_DIM
    kv_local = w_key.shape[2] // head_size
    q_local = w_query.shape[2] // head_size
    group_size = q_local // kv_local
    span_rows = row_count // 2
    section_count = lax.axis_size("section")
    section_rank = lax.axis_index("section")
    seq_rank = lax.axis_index("seq")
    tensor_rank = lax.axis_index("tensor")
    tick_total = section_count + micro_count - 1
    query_places = span_positions(seq_rank * row_count, row_count, span_order, span_rows)
    gain_in = pre_gain[0].astype(jnp.float32)
    gain_out = post_gain[0].astype(jnp.float32)
    gain_part = lax.dynamic_slice_in_dim(gain_out, tensor_rank * width_part, width_part, 0)

    def layer(full_rows):
        stream = full_rows.astype(jnp.float32)
        normed = (
            stream * lax.rsqrt(jnp.mean(stream * stream, axis=1, keepdims=True) + epsilon) * gain_in
        ).astype(jnp.bfloat16)
        queries = jnp.dot(normed, w_query[0], preferred_element_type=jnp.float32).reshape(
            row_count, q_local, head_size
        )
        queries = (
            (rotate(queries, query_places) * query_scale)
            .astype(jnp.bfloat16)
            .reshape(row_count, kv_local, group_size, head_size)
        )
        key_rows = jnp.dot(normed, w_key[0], preferred_element_type=jnp.float32).reshape(
            row_count, kv_local, head_size
        )
        key_rows = (
            rotate(key_rows, query_places)
            .astype(jnp.bfloat16)
            .reshape(row_count, kv_local * head_size)
        )
        values = jnp.dot(normed, w_value[0], preferred_element_type=jnp.float32).astype(
            jnp.bfloat16
        )
        key_piece, value_piece = sent_together((key_rows, values), "seq", 0, 1)
        key_count = key_piece.shape[0]
        key_places = span_positions(jnp.int32(0), key_count, span_order, span_rows)
        scores = jnp.einsum(
            "tkgd,pkd->kgtp",
            queries,
            key_piece.reshape(key_count, kv_local, head_size),
            preferred_element_type=jnp.float32,
        )
        capped = softcap_limit * jnp.tanh(scores / softcap_limit)
        allowed = key_places[None, :] <= query_places[:, None]
        weight = jnp.where(allowed[None, None], jnp.exp(capped), jnp.float32(0.0))
        totals = jnp.sum(weight, axis=3)
        numerator = jnp.einsum(
            "kgtp,pkd->tkgd",
            weight.astype(jnp.bfloat16),
            value_piece.reshape(key_count, kv_local, head_size),
            preferred_element_type=jnp.float32,
        )
        numerator, totals = (numerator, totals)
        attended = (
            (numerator / jnp.transpose(totals, (2, 0, 1))[..., None])
            .astype(jnp.bfloat16)
            .reshape(row_count, q_local * head_size)
        )
        partial_value = jnp.dot(attended, w_out[0], preferred_element_type=jnp.float32)
        own_part = lax.dynamic_slice_in_dim(stream, tensor_rank * width_part, width_part, 1)
        projected = sent_and_summed(partial_value.astype(jnp.bfloat16), "tensor", 1)
        squares = of_everyone(jnp.sum(projected * projected, axis=1), "tensor")
        scaling = lax.rsqrt(squares / model_width + epsilon)[:, None]
        new_part = (own_part + projected * scaling * gain_part).astype(jnp.bfloat16)
        return (new_part, new_part)

    def take_micro(tick_index):
        return lax.dynamic_index_in_dim(
            states_in, jnp.minimum(tick_index, micro_count - 1), 0, keepdims=False
        )

    def tick(carried, tick_index):
        outgoing, record = carried
        arrived = from_behind(outgoing, "section", 1)
        incoming = jnp.where(section_rank == 0, take_micro(tick_index), arrived)
        full_rows = gather_directly(incoming, "tensor", 1)
        new_part, new_full = layer(full_rows)
        slot_index = tick_index - section_rank
        is_valid = jnp.logical_and(slot_index >= 0, slot_index < micro_count)
        placed = lax.dynamic_update_index_in_dim(
            record, new_part, jnp.clip(slot_index, 0, micro_count - 1), 0
        )
        record = jnp.where(is_valid, placed, record)
        outgoing = new_part
        return ((outgoing, record), None)

    first_out = jnp.zeros((row_count, width_part), jnp.bfloat16)
    first_record = jnp.zeros((micro_count, row_count, width_part), jnp.bfloat16)
    (last_out, record), unused = lax.scan(
        tick, (first_out, first_record), jnp.arange(tick_total, dtype=jnp.int32)
    )
    return record[None]


def solution(mesh):
    in_specs = (
        P(None, "seq", "tensor"),
        P(),
        P("section", None),
        P("section", None, "tensor"),
        P("section", None, "tensor"),
        P("section", None, "tensor"),
        P("section", "tensor", None),
        P("section", None),
    )
    out_specs = P("section", None, "seq", "tensor")
    return jax.shard_map(body, mesh=mesh, in_specs=in_specs, out_specs=out_specs, check_vma=False)
```

profile of v0, /device:TPU:57, one launch (start us, length us, event | category | flops | bytes accessed | tf_op | source)
XLA Modules:
  0.0 668.1 jit_solution(18189864824074889298)
XLA Ops:
  3.6 4.3 copy.51
  7.9 6.7 %copy.52 = bf16[1,4608,512]{1,2,0:T(8,128)(2,1)} copy(bf16[1,4608,512]{2,1,0:T(8,128)(2,1)} %param.13) | data formatting | bytes 9437184
  14.6 653.5 %while.16 = (s32[]{:T(128)}, bf16[128,576]{0,1:T(8,128)(2,1)S(1)}, bf16[1,128,576]{1,2,0:T(8,128)(2,1)}, pred[]{:T(512)}, bf16[1,128,576]{1,2,0:T(8,128)(2,1)}, ...) while((s32[]{:T(128)}, bf16[128,576]{0,1:T(8,128)(2,1)S(1)}, ...), condition=%wide.wide.region_8.9_spmd.clone, body=%wide.wide.region_1.8_spmd.clone.sunk | while | flops 1887985152 | bytes 65021264 | solution.py:183
  15.9 5.3 collective-permute-done
  23.3 6.4 all-to-all-start
  30.8 17.7 %all-to-all-done = bf16[8,128,576]{1,2,0:T(8,128)(2,1)S(1)} async-done(((bf16[8,128,576]{1,2,0:T(8,128)(2,1)}), bf16[8,128,576]{1,2,0:T(8,128)(2,1)S(1)}, u32[]{:S(2)}, u32[]{:S(2)}) %all-to-all-start) | async-done | bytes 1179680 | tf_op jit(solution)/shard_map/while/body/eval_jaxpr/all_to_all | solution.py:38
  60.7 3.1 convolution_convert_fusion.3
  64.6 20.8 %all_to_all.34 = bf16[8,128,576]{1,2,0:T(8,128)(2,1)S(1)} all-to-all(bf16[8,128,576]{1,2,0:T(8,128)(2,1)S(1)} %bitcast.162), channel_id=1, replica_groups=mesh['section'=8,'seq'=2,'tensor'=8] {'tensor'}, dimensions={0} | all-to-all | bytes 2359296 | tf_op jit(solution)/shard_map/while/body/eval_jaxpr/all_to_all | solution.py:32
  87.1 3.3 all-to-all-start.2
  91.9 5.0 all-to-all-done.2
  100.0 4.8 collective-permute-done
  106.8 3.6 all-to-all-start
  111.5 17.6 %all-to-all-done = bf16[8,128,576]{1,2,0:T(8,128)(2,1)S(1)} async-done(((bf16[8,128,576]{1,2,0:T(8,128)(2,1)}), bf16[8,128,576]{1,2,0:T(8,128)(2,1)S(1)}, u32[]{:S(2)}, u32[]{:S(2)}) %all-to-all-start) | async-done | bytes 1179680 | tf_op jit(solution)/shard_map/while/body/eval_jaxpr/all_to_all | solution.py:38
  131.4 2.4 fusion.85
  137.8 2.4 all_gather.9
  141.3 3.1 convolution_convert_fusion.3
  145.2 20.8 %all_to_all.34 = bf16[8,128,576]{1,2,0:T(8,128)(2,1)S(1)} all-to-all(bf16[8,128,576]{1,2,0:T(8,128)(2,1)S(1)} %bitcast.162), channel_id=1, replica_groups=mesh['section'=8,'seq'=2,'tensor'=8] {'tensor'}, dimensions={0} | all-to-all | bytes 2359296 | tf_op jit(solution)/shard_map/while/body/eval_jaxpr/all_to_all | solution.py:32
  167.6 3.3 all-to-all-start.2
  172.4 5.0 all-to-all-done.2
  180.6 5.6 collective-permute-done
  188.3 3.6 all-to-all-start
  192.9 17.6 %all-to-all-done = bf16[8,128,576]{1,2,0:T(8,128)(2,1)S(1)} async-done(((bf16[8,128,576]{1,2,0:T(8,128)(2,1)}), bf16[8,128,576]{1,2,0:T(8,128)(2,1)S(1)}, u32[]{:S(2)}, u32[]{:S(2)}) %all-to-all-start) | async-done | bytes 1179680 | tf_op jit(solution)/shard_map/while/body/eval_jaxpr/all_to_all | solution.py:38
  222.8 3.1 convolution_convert_fusion.3
  226.7 20.8 %all_to_all.34 = bf16[8,128,576]{1,2,0:T(8,128)(2,1)S(1)} all-to-all(bf16[8,128,576]{1,2,0:T(8,128)(2,1)S(1)} %bitcast.162), channel_id=1, replica_groups=mesh['section'=8,'seq'=2,'tensor'=8] {'tensor'}, dimensions={0} | all-to-all | bytes 2359296 | tf_op jit(solution)/shard_map/while/body/eval_jaxpr/all_to_all | solution.py:32
  249.1 3.3 all-to-all-start.2
  253.9 5.0 all-to-all-done.2
  262.1 5.6 collective-permute-done
  269.8 3.6 all-to-all-start
  274.4 17.6 %all-to-all-done = bf16[8,128,576]{1,2,0:T(8,128)(2,1)S(1)} async-done(((bf16[8,128,576]{1,2,0:T(8,128)(2,1)}), bf16[8,128,576]{1,2,0:T(8,128)(2,1)S(1)}, u32[]{:S(2)}, u32[]{:S(2)}) %all-to-all-start) | async-done | bytes 1179680 | tf_op jit(solution)/shard_map/while/body/eval_jaxpr/all_to_all | solution.py:38
  294.4 2.4 fusion.85
  304.2 3.1 convolution_convert_fusion.3
  308.1 20.8 %all_to_all.34 = bf16[8,128,576]{1,2,0:T(8,128)(2,1)S(1)} all-to-all(bf16[8,128,576]{1,2,0:T(8,128)(2,1)S(1)} %bitcast.162), channel_id=1, replica_groups=mesh['section'=8,'seq'=2,'tensor'=8] {'tensor'}, dimensions={0} | all-to-all | bytes 2359296 | tf_op jit(solution)/shard_map/while/body/eval_jaxpr/all_to_all | solution.py:32
  330.6 3.3 all-to-all-start.2
  335.4 5.0 all-to-all-done.2
  343.5 5.6 collective-permute-done
  351.2 3.6 all-to-all-start
  355.9 17.6 %all-to-all-done = bf16[8,128,576]{1,2,0:T(8,128)(2,1)S(1)} async-done(((bf16[8,128,576]{1,2,0:T(8,128)(2,1)}), bf16[8,128,576]{1,2,0:T(8,128)(2,1)S(1)}, u32[]{:S(2)}, u32[]{:S(2)}) %all-to-all-start) | async-done | bytes 1179680 | tf_op jit(solution)/shard_map/while/body/eval_jaxpr/all_to_all | solution.py:38
  375.8 2.4 fusion.85
  385.7 3.1 convolution_convert_fusion.3
  389.6 20.8 %all_to_all.34 = bf16[8,128,576]{1,2,0:T(8,128)(2,1)S(1)} all-to-all(bf16[8,128,576]{1,2,0:T(8,128)(2,1)S(1)} %bitcast.162), channel_id=1, replica_groups=mesh['section'=8,'seq'=2,'tensor'=8] {'tensor'}, dimensions={0} | all-to-all | bytes 2359296 | tf_op jit(solution)/shard_map/while/body/eval_jaxpr/all_to_all | solution.py:32
  412.0 3.3 all-to-all-start.2
  416.8 5.0 all-to-all-done.2
  425.0 5.6 collective-permute-done
  432.7 3.6 all-to-all-start
  437.4 17.6 %all-to-all-done = bf16[8,128,576]{1,2,0:T(8,128)(2,1)S(1)} async-done(((bf16[8,128,576]{1,2,0:T(8,128)(2,1)}), bf16[8,128,576]{1,2,0:T(8,128)(2,1)S(1)}, u32[]{:S(2)}, u32[]{:S(2)}) %all-to-all-start) | async-done | bytes 1179680 | tf_op jit(solution)/shard_map/while/body/eval_jaxpr/all_to_all | solution.py:38
  467.2 3.1 convolution_convert_fusion.3
  471.1 20.8 %all_to_all.34 = bf16[8,128,576]{1,2,0:T(8,128)(2,1)S(1)} all-to-all(bf16[8,128,576]{1,2,0:T(8,128)(2,1)S(1)} %bitcast.162), channel_id=1, replica_groups=mesh['section'=8,'seq'=2,'tensor'=8] {'tensor'}, dimensions={0} | all-to-all | bytes 2359296 | tf_op jit(solution)/shard_map/while/body/eval_jaxpr/all_to_all | solution.py:32
  493.5 3.3 all-to-all-start.2
  498.3 5.0 all-to-all-done.2
  506.5 5.6 collective-permute-done
  514.2 3.6 all-to-all-start
  518.8 17.6 %all-to-all-done = bf16[8,128,576]{1,2,0:T(8,128)(2,1)S(1)} async-done(((bf16[8,128,576]{1,2,0:T(8,128)(2,1)}), bf16[8,128,576]{1,2,0:T(8,128)(2,1)S(1)}, u32[]{:S(2)}, u32[]{:S(2)}) %all-to-all-start) | async-done | bytes 1179680 | tf_op jit(solution)/shard_map/while/body/eval_jaxpr/all_to_all | solution.py:38
  538.8 2.4 fusion.85
  548.7 3.1 convolution_convert_fusion.3
  552.6 20.8 %all_to_all.34 = bf16[8,128,576]{1,2,0:T(8,128)(2,1)S(1)} all-to-all(bf16[8,128,576]{1,2,0:T(8,128)(2,1)S(1)} %bitcast.162), channel_id=1, replica_groups=mesh['section'=8,'seq'=2,'tensor'=8] {'tensor'}, dimensions={0} | all-to-all | bytes 2359296 | tf_op jit(solution)/shard_map/while/body/eval_jaxpr/all_to_all | solution.py:32
  575.0 3.3 all-to-all-start.2
  579.8 5.0 all-to-all-done.2
  588.0 5.6 collective-permute-done
  595.7 3.6 all-to-all-start
  600.3 17.6 %all-to-all-done = bf16[8,128,576]{1,2,0:T(8,128)(2,1)S(1)} async-done(((bf16[8,128,576]{1,2,0:T(8,128)(2,1)}), bf16[8,128,576]{1,2,0:T(8,128)(2,1)S(1)}, u32[]{:S(2)}, u32[]{:S(2)}) %all-to-all-start) | async-done | bytes 1179680 | tf_op jit(solution)/shard_map/while/body/eval_jaxpr/all_to_all | solution.py:38
  630.1 3.1 convolution_convert_fusion.3
  634.0 20.8 %all_to_all.34 = bf16[8,128,576]{1,2,0:T(8,128)(2,1)S(1)} all-to-all(bf16[8,128,576]{1,2,0:T(8,128)(2,1)S(1)} %bitcast.162), channel_id=1, replica_groups=mesh['section'=8,'seq'=2,'tensor'=8] {'tensor'}, dimensions={0} | all-to-all | bytes 2359296 | tf_op jit(solution)/shard_map/while/body/eval_jaxpr/all_to_all | solution.py:32
  656.5 3.3 all-to-all-start.2
  661.3 5.0 all-to-all-done.2
  (359 shorter events, 163.6 us)
Async XLA Ops:
  2.9 0.7 copy-start.2
  14.6 6.6 collective-permute-start
  23.3 25.2 %all-to-all-start = ((bf16[8,128,576]{1,2,0:T(8,128)(2,1)}), bf16[8,128,576]{1,2,0:T(8,128)(2,1)S(1)}, u32[]{:S(2)}, u32[]{:S(2)}) async-start(bf16[8,128,576]{1,2,0:T(8,128)(2,1)} %broadcast_in_dim.130), calls=%async_computation | async-start | bytes 2359296 | tf_op jit(solution)/shard_map/while/body/eval_jaxpr/all_to_all | solution.py:38
  49.2 4.1 copy-start
  64.6 25.7 %copy-start.3 = (s32[8]{0:T(128)S(1)}, s32[8]{0:T(128)}, u32[]{:S(2)}) copy-start(s32[8]{0:T(128)} %get-tuple-element.652) | copy-start | bytes 100 | tf_op jit(solution)/shard_map/while
  85.6 0.7 copy-start.1
  87.1 9.8 %all-to-all-start.2 = ((f32[8,1,128]{2,1,0:T(1,128)}), f32[8,1,128]{2,1,0:T(1,128)S(1)}, u32[]{:S(2)}, u32[]{:S(2)}) async-start(f32[8,1,128]{2,1,0:T(1,128)} %broadcast_in_dim.131), calls=%async_computation.2 | async-start | bytes 8192 | tf_op jit(solution)/shard_map/while/body/eval_jaxpr/all_to_all | solution.py:38
  98.7 6.1 collective-permute-start
  106.8 22.3 %all-to-all-start = ((bf16[8,128,576]{1,2,0:T(8,128)(2,1)}), bf16[8,128,576]{1,2,0:T(8,128)(2,1)S(1)}, u32[]{:S(2)}, u32[]{:S(2)}) async-start(bf16[8,128,576]{1,2,0:T(8,128)(2,1)} %broadcast_in_dim.130), calls=%async_computation | async-start | bytes 2359296 | tf_op jit(solution)/shard_map/while/body/eval_jaxpr/all_to_all | solution.py:38
  129.7 4.1 copy-start
  145.2 25.7 %copy-start.3 = (s32[8]{0:T(128)S(1)}, s32[8]{0:T(128)}, u32[]{:S(2)}) copy-start(s32[8]{0:T(128)} %get-tuple-element.652) | copy-start | bytes 100 | tf_op jit(solution)/shard_map/while
  166.2 0.7 copy-start.1
  167.6 9.8 %all-to-all-start.2 = ((f32[8,1,128]{2,1,0:T(1,128)}), f32[8,1,128]{2,1,0:T(1,128)S(1)}, u32[]{:S(2)}, u32[]{:S(2)}) async-start(f32[8,1,128]{2,1,0:T(1,128)} %broadcast_in_dim.131), calls=%async_computation.2 | async-start | bytes 8192 | tf_op jit(solution)/shard_map/while/body/eval_jaxpr/all_to_all | solution.py:38
  179.3 6.9 %collective-permute-start = (bf16[128,576]{0,1:T(8,128)(2,1)S(1)}, bf16[128,576]{0,1:T(8,128)(2,1)S(1)}, u32[]{:S(2)}, u32[]{:S(2)}) collective-permute-start(bf16[128,576]{0,1:T(8,128)(2,1)S(1)} %broadcast_select_fusion.3), channel_id=1, source_target_pairs={{0,16},{16,32},{32,48},{48,64},{64,80},{80,96},{96,112},{1,17},{17... | collective-permute-start | bytes 442376 | tf_op jit(solution)/shard_map/while/body/eval_jaxpr/ppermute | solution.py:48
  188.3 22.3 %all-to-all-start = ((bf16[8,128,576]{1,2,0:T(8,128)(2,1)}), bf16[8,128,576]{1,2,0:T(8,128)(2,1)S(1)}, u32[]{:S(2)}, u32[]{:S(2)}) async-start(bf16[8,128,576]{1,2,0:T(8,128)(2,1)} %broadcast_in_dim.130), calls=%async_computation | async-start | bytes 2359296 | tf_op jit(solution)/shard_map/while/body/eval_jaxpr/all_to_all | solution.py:38
  211.2 4.1 copy-start
  226.7 25.7 %copy-start.3 = (s32[8]{0:T(128)S(1)}, s32[8]{0:T(128)}, u32[]{:S(2)}) copy-start(s32[8]{0:T(128)} %get-tuple-element.652) | copy-start | bytes 100 | tf_op jit(solution)/shard_map/while
  247.7 0.7 copy-start.1
  249.1 9.8 %all-to-all-start.2 = ((f32[8,1,128]{2,1,0:T(1,128)}), f32[8,1,128]{2,1,0:T(1,128)S(1)}, u32[]{:S(2)}, u32[]{:S(2)}) async-start(f32[8,1,128]{2,1,0:T(1,128)} %broadcast_in_dim.131), calls=%async_computation.2 | async-start | bytes 8192 | tf_op jit(solution)/shard_map/while/body/eval_jaxpr/all_to_all | solution.py:38
  260.8 6.9 %collective-permute-start = (bf16[128,576]{0,1:T(8,128)(2,1)S(1)}, bf16[128,576]{0,1:T(8,128)(2,1)S(1)}, u32[]{:S(2)}, u32[]{:S(2)}) collective-permute-start(bf16[128,576]{0,1:T(8,128)(2,1)S(1)} %broadcast_select_fusion.3), channel_id=1, source_target_pairs={{0,16},{16,32},{32,48},{48,64},{64,80},{80,96},{96,112},{1,17},{17... | collective-permute-start | bytes 442376 | tf_op jit(solution)/shard_map/while/body/eval_jaxpr/ppermute | solution.py:48
  269.8 22.3 %all-to-all-start = ((bf16[8,128,576]{1,2,0:T(8,128)(2,1)}), bf16[8,128,576]{1,2,0:T(8,128)(2,1)S(1)}, u32[]{:S(2)}, u32[]{:S(2)}) async-start(bf16[8,128,576]{1,2,0:T(8,128)(2,1)} %broadcast_in_dim.130), calls=%async_computation | async-start | bytes 2359296 | tf_op jit(solution)/shard_map/while/body/eval_jaxpr/all_to_all | solution.py:38
  292.7 4.1 copy-start
  308.1 25.7 %copy-start.3 = (s32[8]{0:T(128)S(1)}, s32[8]{0:T(128)}, u32[]{:S(2)}) copy-start(s32[8]{0:T(128)} %get-tuple-element.652) | copy-start | bytes 100 | tf_op jit(solution)/shard_map/while
  329.1 0.7 copy-start.1
  330.6 9.8 %all-to-all-start.2 = ((f32[8,1,128]{2,1,0:T(1,128)}), f32[8,1,128]{2,1,0:T(1,128)S(1)}, u32[]{:S(2)}, u32[]{:S(2)}) async-start(f32[8,1,128]{2,1,0:T(1,128)} %broadcast_in_dim.131), calls=%async_computation.2 | async-start | bytes 8192 | tf_op jit(solution)/shard_map/while/body/eval_jaxpr/all_to_all | solution.py:38
  342.2 6.9 %collective-permute-start = (bf16[128,576]{0,1:T(8,128)(2,1)S(1)}, bf16[128,576]{0,1:T(8,128)(2,1)S(1)}, u32[]{:S(2)}, u32[]{:S(2)}) collective-permute-start(bf16[128,576]{0,1:T(8,128)(2,1)S(1)} %broadcast_select_fusion.3), channel_id=1, source_target_pairs={{0,16},{16,32},{32,48},{48,64},{64,80},{80,96},{96,112},{1,17},{17... | collective-permute-start | bytes 442376 | tf_op jit(solution)/shard_map/while/body/eval_jaxpr/ppermute | solution.py:48
  351.2 22.3 %all-to-all-start = ((bf16[8,128,576]{1,2,0:T(8,128)(2,1)}), bf16[8,128,576]{1,2,0:T(8,128)(2,1)S(1)}, u32[]{:S(2)}, u32[]{:S(2)}) async-start(bf16[8,128,576]{1,2,0:T(8,128)(2,1)} %broadcast_in_dim.130), calls=%async_computation | async-start | bytes 2359296 | tf_op jit(solution)/shard_map/while/body/eval_jaxpr/all_to_all | solution.py:38
  374.2 4.1 copy-start
  389.6 25.7 %copy-start.3 = (s32[8]{0:T(128)S(1)}, s32[8]{0:T(128)}, u32[]{:S(2)}) copy-start(s32[8]{0:T(128)} %get-tuple-element.652) | copy-start | bytes 100 | tf_op jit(solution)/shard_map/while
  410.6 0.7 copy-start.1
  412.0 9.8 %all-to-all-start.2 = ((f32[8,1,128]{2,1,0:T(1,128)}), f32[8,1,128]{2,1,0:T(1,128)S(1)}, u32[]{:S(2)}, u32[]{:S(2)}) async-start(f32[8,1,128]{2,1,0:T(1,128)} %broadcast_in_dim.131), calls=%async_computation.2 | async-start | bytes 8192 | tf_op jit(solution)/shard_map/while/body/eval_jaxpr/all_to_all | solution.py:38
  423.7 6.9 %collective-permute-start = (bf16[128,576]{0,1:T(8,128)(2,1)S(1)}, bf16[128,576]{0,1:T(8,128)(2,1)S(1)}, u32[]{:S(2)}, u32[]{:S(2)}) collective-permute-start(bf16[128,576]{0,1:T(8,128)(2,1)S(1)} %broadcast_select_fusion.3), channel_id=1, source_target_pairs={{0,16},{16,32},{32,48},{48,64},{64,80},{80,96},{96,112},{1,17},{17... | collective-permute-start | bytes 442376 | tf_op jit(solution)/shard_map/while/body/eval_jaxpr/ppermute | solution.py:48
  432.7 22.3 %all-to-all-start = ((bf16[8,128,576]{1,2,0:T(8,128)(2,1)}), bf16[8,128,576]{1,2,0:T(8,128)(2,1)S(1)}, u32[]{:S(2)}, u32[]{:S(2)}) async-start(bf16[8,128,576]{1,2,0:T(8,128)(2,1)} %broadcast_in_dim.130), calls=%async_computation | async-start | bytes 2359296 | tf_op jit(solution)/shard_map/while/body/eval_jaxpr/all_to_all | solution.py:38
  455.6 4.1 copy-start
  471.1 25.7 %copy-start.3 = (s32[8]{0:T(128)S(1)}, s32[8]{0:T(128)}, u32[]{:S(2)}) copy-start(s32[8]{0:T(128)} %get-tuple-element.652) | copy-start | bytes 100 | tf_op jit(solution)/shard_map/while
  492.1 0.7 copy-start.1
  493.5 9.8 %all-to-all-start.2 = ((f32[8,1,128]{2,1,0:T(1,128)}), f32[8,1,128]{2,1,0:T(1,128)S(1)}, u32[]{:S(2)}, u32[]{:S(2)}) async-start(f32[8,1,128]{2,1,0:T(1,128)} %broadcast_in_dim.131), calls=%async_computation.2 | async-start | bytes 8192 | tf_op jit(solution)/shard_map/while/body/eval_jaxpr/all_to_all | solution.py:38
  505.2 6.9 %collective-permute-start = (bf16[128,576]{0,1:T(8,128)(2,1)S(1)}, bf16[128,576]{0,1:T(8,128)(2,1)S(1)}, u32[]{:S(2)}, u32[]{:S(2)}) collective-permute-start(bf16[128,576]{0,1:T(8,128)(2,1)S(1)} %broadcast_select_fusion.3), channel_id=1, source_target_pairs={{0,16},{16,32},{32,48},{48,64},{64,80},{80,96},{96,112},{1,17},{17... | collective-permute-start | bytes 442376 | tf_op jit(solution)/shard_map/while/body/eval_jaxpr/ppermute | solution.py:48
  514.2 22.3 %all-to-all-start = ((bf16[8,128,576]{1,2,0:T(8,128)(2,1)}), bf16[8,128,576]{1,2,0:T(8,128)(2,1)S(1)}, u32[]{:S(2)}, u32[]{:S(2)}) async-start(bf16[8,128,576]{1,2,0:T(8,128)(2,1)} %broadcast_in_dim.130), calls=%async_computation | async-start | bytes 2359296 | tf_op jit(solution)/shard_map/while/body/eval_jaxpr/all_to_all | solution.py:38
  537.1 4.1 copy-start
  552.5 25.7 %copy-start.3 = (s32[8]{0:T(128)S(1)}, s32[8]{0:T(128)}, u32[]{:S(2)}) copy-start(s32[8]{0:T(128)} %get-tuple-element.652) | copy-start | bytes 100 | tf_op jit(solution)/shard_map/while
  573.6 0.7 copy-start.1
  575.0 9.8 %all-to-all-start.2 = ((f32[8,1,128]{2,1,0:T(1,128)}), f32[8,1,128]{2,1,0:T(1,128)S(1)}, u32[]{:S(2)}, u32[]{:S(2)}) async-start(f32[8,1,128]{2,1,0:T(1,128)} %broadcast_in_dim.131), calls=%async_computation.2 | async-start | bytes 8192 | tf_op jit(solution)/shard_map/while/body/eval_jaxpr/all_to_all | solution.py:38
  586.7 6.9 %collective-permute-start = (bf16[128,576]{0,1:T(8,128)(2,1)S(1)}, bf16[128,576]{0,1:T(8,128)(2,1)S(1)}, u32[]{:S(2)}, u32[]{:S(2)}) collective-permute-start(bf16[128,576]{0,1:T(8,128)(2,1)S(1)} %broadcast_select_fusion.3), channel_id=1, source_target_pairs={{0,16},{16,32},{32,48},{48,64},{64,80},{80,96},{96,112},{1,17},{17... | collective-permute-start | bytes 442376 | tf_op jit(solution)/shard_map/while/body/eval_jaxpr/ppermute | solution.py:48
  595.7 22.3 %all-to-all-start = ((bf16[8,128,576]{1,2,0:T(8,128)(2,1)}), bf16[8,128,576]{1,2,0:T(8,128)(2,1)S(1)}, u32[]{:S(2)}, u32[]{:S(2)}) async-start(bf16[8,128,576]{1,2,0:T(8,128)(2,1)} %broadcast_in_dim.130), calls=%async_computation | async-start | bytes 2359296 | tf_op jit(solution)/shard_map/while/body/eval_jaxpr/all_to_all | solution.py:38
  618.6 4.1 copy-start
  634.0 25.7 %copy-start.3 = (s32[8]{0:T(128)S(1)}, s32[8]{0:T(128)}, u32[]{:S(2)}) copy-start(s32[8]{0:T(128)} %get-tuple-element.652) | copy-start | bytes 100 | tf_op jit(solution)/shard_map/while
  655.0 0.7 copy-start.1
  656.5 9.8 %all-to-all-start.2 = ((f32[8,1,128]{2,1,0:T(1,128)}), f32[8,1,128]{2,1,0:T(1,128)S(1)}, u32[]{:S(2)}, u32[]{:S(2)}) async-start(f32[8,1,128]{2,1,0:T(1,128)} %broadcast_in_dim.131), calls=%async_computation.2 | async-start | bytes 8192 | tf_op jit(solution)/shard_map/while/body/eval_jaxpr/all_to_all | solution.py:38
where the time goes:
time: 675 us; the launch traced here: 668 us
  waiting for transfers between devices  224 us (33%)
  blocking collectives  186 us (28%)
  matrix products  79.2 us (12%)
  starting transfers between devices  68 us (10%)
  other arithmetic  55.7 us (8%)
  local copies, waits for them, and re-layouts  47.4 us (7%)
  loops' own time  7.24 us (1%)
    all_to_all x16, waiting for transfers between devices, from_everyone(): lax.all_to_all(jnp.broadcast_to(x[None], (size, *x.shape)), axis, 0, 0, t...  181 us
    all_to_all x8, blocking collectives, sent_and_summed(): lax.all_to_all(pieces, axis, split_axis=0, concat_axis=0, tiled=True)  167 us
    all_to_all x16, starting transfers between devices, from_everyone(): lax.all_to_all(jnp.broadcast_to(x[None], (size, *x.shape)), axis, 0, 0, t...  57.7 us
    ppermute x8, waiting for transfers between devices, from_behind(): lax.ppermute(value, axis, [(source, source + steps) for source in range(f...  43.7 us
    dot_general x8, matrix products, layer(): jnp.dot(attended, w_out[0], preferred_element_type=jnp.float32)  25.1 us
    dot_general x8, matrix products, layer(): jnp.dot(normed, w_key[0], preferred_element_type=jnp.float32)  19.5 us
    all_gather x8, blocking collectives, sent_together(): lax.all_gather(both, axis, axis=dim, tiled=True)  19.3 us
    dot_general x8, matrix products, layer(): jnp.dot(normed, w_value[0], preferred_element_type=jnp.float32)  18.4 us
  transfers between devices with their start and end apart: 24, of which 24 were waited for; matrix products, arithmetic and copies ran while one was open for 2% of the time, Pallas kernels for 0%

commit v1 on v0

v1 whole, which is shorter than its diff:
```python
import jax
import jax.numpy as jnp
from jax import lax
from jax.sharding import PartitionSpec as P

HEAD_DIM = 128
CHUNKS = 2

softcap_limit = 50.0
query_scale = 144.0 ** (-0.5)
epsilon = 1e-06
rotary_base = 10000.0
f32 = jnp.float32
bf16 = jnp.bfloat16


def rotate(vectors, cos_part, sin_part):
    half_dim = vectors.shape[-1] // 2
    lower_half = vectors[..., :half_dim]
    upper_half = vectors[..., half_dim:]
    return jnp.concatenate(
        [
            lower_half * cos_part - upper_half * sin_part,
            upper_half * cos_part + lower_half * sin_part,
        ],
        axis=-1,
    )


def exchange(pieces):
    return lax.all_to_all(pieces, "tensor", split_axis=0, concat_axis=0, tiled=True)


def spread(x, size):
    return exchange(jnp.broadcast_to(x[None], (size, *x.shape)))


def body(states_in, span_order, pre_gain, w_query, w_key, w_value, w_out, post_gain):
    _, row_count, width_part = states_in.shape
    width = pre_gain.shape[1]
    q_width = w_query.shape[2]
    kv_width = w_key.shape[2]
    kv_heads = kv_width // HEAD_DIM
    group = q_width // kv_width
    sections = lax.axis_size("section")
    tensors = lax.axis_size("tensor")
    section_rank = lax.axis_index("section")
    seq_rank = lax.axis_index("seq")
    tensor_rank = lax.axis_index("tensor")
    seqs = lax.axis_size("seq")
    spans = span_order.shape[0]
    rows = row_count // CHUNKS
    own = rows // tensors
    chunk_len = rows * seqs
    total_len = chunk_len * CHUNKS
    gain_in = pre_gain[0].astype(f32)
    gain_out = post_gain[0].astype(f32)
    ids = jnp.arange(spans, dtype=jnp.int32)

    blocks = lax.all_gather(states_in[0], "seq", axis=0).reshape(spans, rows, width_part)
    block_of = jnp.sum(jnp.where(span_order[None, :] == ids[:, None], ids[None, :], 0), axis=1)
    picked = jnp.stack(
        [
            lax.dynamic_index_in_dim(
                blocks,
                lax.dynamic_index_in_dim(block_of, c * seqs + seq_rank, 0, keepdims=False),
                0,
                keepdims=False,
            )
            for c in range(CHUNKS)
        ]
    )
    first_rows = spread(picked, tensors)
    first_rows = jnp.moveaxis(first_rows, 0, 2).reshape(CHUNKS, rows, width)

    places = (
        jnp.arange(CHUNKS, dtype=jnp.int32)[:, None] * chunk_len
        + seq_rank * rows
        + jnp.arange(rows, dtype=jnp.int32)[None, :]
    )
    half = HEAD_DIM // 2
    inverse = rotary_base ** (-(jnp.arange(half, dtype=f32) * 2.0 / HEAD_DIM))
    angles = places.astype(f32)[..., None] * inverse
    cos_all, sin_all = (jnp.cos(angles), jnp.sin(angles))

    def layer(full, slot, keys, values_held):
        stream = full.astype(f32)
        normed = (
            stream * lax.rsqrt(jnp.mean(stream * stream, axis=1, keepdims=True) + epsilon) * gain_in
        ).astype(bf16)
        cos_part = lax.dynamic_index_in_dim(cos_all, slot, 0, keepdims=False)[:, None, :]
        sin_part = lax.dynamic_index_in_dim(sin_all, slot, 0, keepdims=False)[:, None, :]
        queries = jnp.dot(normed, w_query[0], preferred_element_type=f32)
        queries = rotate(queries.reshape(rows, -1, HEAD_DIM), cos_part, sin_part) * query_scale
        queries = queries.astype(bf16).reshape(rows, kv_heads, group, HEAD_DIM)
        key_rows = jnp.dot(normed, w_key[0], preferred_element_type=f32)
        key_rows = rotate(key_rows.reshape(rows, -1, HEAD_DIM), cos_part, sin_part)
        key_rows = key_rows.astype(bf16).reshape(rows, kv_width)
        value_rows = jnp.dot(normed, w_value[0], preferred_element_type=f32).astype(bf16)
        both = lax.all_gather(jnp.concatenate([key_rows, value_rows], axis=1), "seq", axis=0)
        both = both.reshape(chunk_len, 2 * kv_width)
        keys = lax.dynamic_update_slice_in_dim(keys, both[:, :kv_width], slot * chunk_len, 0)
        values_held = lax.dynamic_update_slice_in_dim(
            values_held, both[:, kv_width:], slot * chunk_len, 0
        )
        scores = jnp.einsum(
            "tkgd,pkd->kgtp",
            queries,
            keys.reshape(total_len, kv_heads, HEAD_DIM),
            preferred_element_type=f32,
        )
        capped = softcap_limit * jnp.tanh(scores / softcap_limit)
        my_places = lax.dynamic_index_in_dim(places, slot, 0, keepdims=False)
        allowed = jnp.arange(total_len, dtype=jnp.int32)[None, :] <= my_places[:, None]
        weight = jnp.where(allowed[None, None], jnp.exp(capped), f32(0.0))
        totals = jnp.sum(weight, axis=3)
        numerator = jnp.einsum(
            "kgtp,pkd->tkgd",
            weight.astype(bf16),
            values_held.reshape(total_len, kv_heads, HEAD_DIM),
            preferred_element_type=f32,
        )
        attended = (numerator / jnp.transpose(totals, (2, 0, 1))[..., None]).astype(bf16)
        partial_value = jnp.dot(
            attended.reshape(rows, q_width), w_out[0], preferred_element_type=f32
        ).astype(bf16)
        arrived = exchange(partial_value.reshape(tensors, own, width))
        projected = arrived.astype(f32).sum(axis=0)
        scaling = lax.rsqrt(jnp.mean(projected * projected, axis=1, keepdims=True) + epsilon)
        held = lax.dynamic_slice_in_dim(full, tensor_rank * own, own, 0).astype(f32)
        return (held + projected * scaling * gain_out).astype(bf16), keys, values_held

    def work(carried, tick_index):
        full, keys, values_held, record = carried
        slot_index = tick_index - section_rank
        slot = jnp.clip(slot_index, 0, CHUNKS - 1)
        new_rows, keys, values_held = layer(full, slot, keys, values_held)
        is_valid = slot_index == slot
        placed = lax.dynamic_update_index_in_dim(record, new_rows, slot, 0)
        record = jnp.where(is_valid, placed, record)
        return new_rows, keys, values_held, record

    def tick(carried, tick_index):
        new_rows, keys, values_held, record = work(carried, tick_index)
        moved = lax.ppermute(new_rows, "section", [(i, i + 1) for i in range(sections - 1)])
        full = spread(moved, tensors).reshape(rows, width)
        following = lax.dynamic_index_in_dim(
            first_rows, jnp.minimum(tick_index + 1, CHUNKS - 1), 0, keepdims=False
        )
        full = jnp.where(section_rank == 0, following, full)
        return (full, keys, values_held, record), None

    tick_total = sections + CHUNKS - 1
    start = (
        first_rows[0],
        jnp.zeros((total_len, kv_width), bf16),
        jnp.zeros((total_len, kv_width), bf16),
        jnp.zeros((CHUNKS, own, width), bf16),
    )
    carried, _ = lax.scan(tick, start, jnp.arange(tick_total - 1, dtype=jnp.int32))
    record = work(carried, jnp.int32(tick_total - 1))[3]

    pieces = record.reshape(CHUNKS, own, tensors, width_part)
    pieces = exchange(jnp.moveaxis(pieces, 2, 0))
    pieces = jnp.moveaxis(pieces, 0, 1).reshape(CHUNKS, rows, width_part)
    ordered = lax.all_gather(pieces, "seq", axis=1).reshape(spans, rows, width_part)
    mine = lax.dynamic_slice_in_dim(span_order, seq_rank * CHUNKS, CHUNKS, 0)
    out = [lax.dynamic_index_in_dim(ordered, mine[j], 0, keepdims=False) for j in range(CHUNKS)]
    return jnp.concatenate(out, axis=0)[None, None]


def solution(mesh):
    in_specs = (
        P(None, "seq", "tensor"),
        P(),
        P("section", None),
        P("section", None, "tensor"),
        P("section", None, "tensor"),
        P("section", None, "tensor"),
        P("section", "tensor", None),
        P("section", None),
    )
    out_specs = P("section", None, "seq", "tensor")
    return jax.shard_map(body, mesh=mesh, in_specs=in_specs, out_specs=out_specs, check_vma=False)
```

time: 675 us -> 616 us (0.913)
  blocking collectives: 186 us -> 28.8 us
  local copies, waits for them, and re-layouts: 47.4 us -> 90.1 us
  matrix products: 79.2 us -> 111 us
  other arithmetic: 55.7 us -> 32.9 us
  waiting for transfers between devices: 224 us -> 242 us
  starting transfers between devices: 68 us -> 83.7 us
  between operations: 0.02 us -> 7.49 us
    all_to_all x8 -> x0, blocking collectives: 167 us -> none  [sent_and_summed(): lax.all_to_all(pieces, axis, split_axis=0, concat_axis=0, tiled=True)]
    dot_general x48 -> x54, matrix products: 79.2 us -> 111 us  [the longest x9 37 us: layer(): jnp.dot(attended.reshape(rows, q_width), w_out[0], preferred_element_type...]
    all_to_all x16 -> x19, waiting for transfers between devices: 181 us -> 206 us  [exchange(): lax.all_to_all(pieces, 'tensor', split_axis=0, concat_axis=0, tiled=True)]
    reshape x16 -> x29, local copies, waits for them, and re-layouts: 1.09 us -> 19.1 us  [the longest x9 8.46 us: layer(): values_held.reshape(total_len, kv_heads, HEAD_DIM)]
    all_to_all x16 -> x19, starting transfers between devices: 57.7 us -> 73.4 us  [exchange(): lax.all_to_all(pieces, 'tensor', split_axis=0, concat_axis=0, tiled=True)]
    another operation x16 -> x10, other arithmetic: 13.6 us -> 0.8 us
    unnamed x4 -> x20, local copies, waits for them, and re-layouts: 11 us -> 0.04 us
    all_gather x8 -> x11, blocking collectives: 19.3 us -> 28.8 us  [the longest x9 22.7 us: layer(): lax.all_gather(jnp.concatenate([key_rows, value_rows], axis=1), 'seq', ax...]
  transfers between devices with their start and end apart: 24 -> 27, of which waited for: 24 -> 26; matrix products, arithmetic and copies ran while one was open for 2% -> 4% of each run, Pallas kernels for 0% -> 0%
where the time goes in v1:
time: 616 us; the launch traced here: 608 us
  waiting for transfers between devices  242 us (39%)
  matrix products  111 us (18%)
  local copies, waits for them, and re-layouts  90.1 us (15%)
  starting transfers between devices  83.7 us (14%)
  other arithmetic  32.9 us (5%)
  blocking collectives  28.8 us (5%)
  loops' own time  12.1 us (2%)
  between operations  7.49 us (1%)
    all_to_all x19, waiting for transfers between devices, exchange(): lax.all_to_all(pieces, 'tensor', split_axis=0, concat_axis=0, tiled=True)  206 us
    all_to_all x19, starting transfers between devices, exchange(): lax.all_to_all(pieces, 'tensor', split_axis=0, concat_axis=0, tiled=True)  73.4 us
    dot_general x9, matrix products, layer(): jnp.dot(attended.reshape(rows, q_width), w_out[0], preferred_element_type...  37 us
    ppermute x8, waiting for transfers between devices, tick(): lax.ppermute(new_rows, 'section', [(i, i + 1) for i in range(sections - 1)])  35.9 us
    dot_general x9, matrix products, layer(): queries = jnp.dot(normed, w_query[0], preferred_element_type=f32)  35.2 us
    all_gather x9, blocking collectives, layer(): lax.all_gather(jnp.concatenate([key_rows, value_rows], axis=1), 'seq', ax...  22.7 us
    dot_general x9, matrix products, layer(): key_rows = jnp.dot(normed, w_key[0], preferred_element_type=f32)  21.8 us
    select_n x9, other arithmetic, work(): record = jnp.where(is_valid, placed, record)  13.2 us
  transfers between devices with their start and end apart: 27, of which 26 were waited for; matrix products, arithmetic and copies ran while one was open for 4% of the time, Pallas kernels for 0%

profile of v1, /device:TPU:57, one launch (start us, length us, event | category | flops | bytes accessed | tf_op | source)
XLA Modules:
  0.0 607.7 jit_solution(9915214565211291957)
XLA Ops:
  9.0 6.4 %all-to-all-start.2 = ((bf16[8,2,64,576]{3,2,1,0:T(8,128)(2,1)}), bf16[8,2,64,576]{3,2,1,0:T(8,128)(2,1)}, u32[]{:S(2)}, u32[]{:S(2)}) async-start(bf16[8,2,64,576]{3,2,1,0:T(8,128)(2,1)} %broadcast_in_dim.95), calls=%async_computation.2 | async-start | bytes 2621440 | tf_op jit(solution)/shard_map/all_to_all | solution.py:31
  15.5 6.9 %copy.105 = bf16[1,4608,512]{1,2,0:T(8,128)(2,1)} copy(bf16[1,4608,512]{2,1,0:T(8,128)(2,1)} %param.13) | data formatting | bytes 9437184 | tf_op jit(solution)/shard_map/while | solution.py:160
  24.9 6.7 %copy.129 = bf16[512,4608]{1,0:T(8,128)(2,1)} copy(bf16[512,4608]{0,1:T(8,128)(2,1)} %bitcast.198) | data formatting | bytes 9437184 | tf_op jit(solution)/shard_map/dot_general | solution.py:93
  51.0 507.2 %while.18 = (s32[]{:T(128)}, bf16[64,4608]{1,0:T(8,128)(2,1)S(1)}, bf16[256,256]{1,0:T(8,128)(2,1)}, bf16[256,256]{1,0:T(8,128)(2,1)}, bf16[2,8,4608]{2,1,0:T(8,...) while((s32[]{:T(128)}, bf16[64,4608]{1,0:T(8,128)(2,1)S(1)}, ...), condition=%wide.region_6.7_spmd, body=%wide.region_1.6_spmd.sunk | while | flops 946270016 | bytes 27762032 | solution.py:160
  61.8 3.9 fusion.115
  68.2 4.1 fusion.119
  72.3 6.9 %all-to-all-start = ((bf16[8,8,4608]{2,1,0:T(8,128)(2,1)}), bf16[8,8,4608]{2,1,0:T(8,128)(2,1)S(1)}, u32[]{:S(2)}, u32[]{:S(2)}) async-start(bf16[8,8,4608]{2,1,0:T(8,128)(2,1)} %fusion.119), calls=%async_computation | async-start | bytes 1179648 | tf_op jit(solution)/shard_map/while/body/eval_jaxpr/all_to_all | solution.py:31
  79.2 12.5 %all-to-all-done = bf16[8,8,4608]{2,1,0:T(8,128)(2,1)S(1)} async-done(((bf16[8,8,4608]{2,1,0:T(8,128)(2,1)}), bf16[8,8,4608]{2,1,0:T(8,128)(2,1)S(1)}, u32[]{:S(2)}, u32[]{:S(2)}) %all-to-all-start) | async-done | bytes 589856 | tf_op jit(solution)/shard_map/while/body/eval_jaxpr/all_to_all | solution.py:31
  94.8 3.8 collective-permute-done
  99.5 3.5 all-to-all-start.1
  103.7 11.0 %all-to-all-done.1 = bf16[8,8,4608]{2,1,0:T(8,128)(2,1)S(1)} async-done(((bf16[8,8,4608]{2,1,0:T(8,128)(2,1)}), bf16[8,8,4608]{2,1,0:T(8,128)(2,1)S(1)}, u32[]{:S(2)}, u32[]{:S(2)}) %all-to-all-start.1) | async-done | bytes 589856 | tf_op jit(solution)/shard_map/while/body/eval_jaxpr/all_to_all | solution.py:31
  127.5 3.9 fusion.115
  133.9 4.1 fusion.119
  138.0 3.5 all-to-all-start
  141.6 12.4 %all-to-all-done = bf16[8,8,4608]{2,1,0:T(8,128)(2,1)S(1)} async-done(((bf16[8,8,4608]{2,1,0:T(8,128)(2,1)}), bf16[8,8,4608]{2,1,0:T(8,128)(2,1)S(1)}, u32[]{:S(2)}, u32[]{:S(2)}) %all-to-all-start) | async-done | bytes 589856 | tf_op jit(solution)/shard_map/while/body/eval_jaxpr/all_to_all | solution.py:31
  157.1 4.0 collective-permute-done
  162.0 3.5 all-to-all-start.1
  166.2 11.5 %all-to-all-done.1 = bf16[8,8,4608]{2,1,0:T(8,128)(2,1)S(1)} async-done(((bf16[8,8,4608]{2,1,0:T(8,128)(2,1)}), bf16[8,8,4608]{2,1,0:T(8,128)(2,1)S(1)}, u32[]{:S(2)}, u32[]{:S(2)}) %all-to-all-start.1) | async-done | bytes 589856 | tf_op jit(solution)/shard_map/while/body/eval_jaxpr/all_to_all | solution.py:31
  190.0 3.9 fusion.115
  196.4 4.1 fusion.119
  200.5 3.5 all-to-all-start
  204.1 12.4 %all-to-all-done = bf16[8,8,4608]{2,1,0:T(8,128)(2,1)S(1)} async-done(((bf16[8,8,4608]{2,1,0:T(8,128)(2,1)}), bf16[8,8,4608]{2,1,0:T(8,128)(2,1)S(1)}, u32[]{:S(2)}, u32[]{:S(2)}) %all-to-all-start) | async-done | bytes 589856 | tf_op jit(solution)/shard_map/while/body/eval_jaxpr/all_to_all | solution.py:31
  219.6 4.7 collective-permute-done
  225.2 3.5 all-to-all-start.1
  229.4 11.6 %all-to-all-done.1 = bf16[8,8,4608]{2,1,0:T(8,128)(2,1)S(1)} async-done(((bf16[8,8,4608]{2,1,0:T(8,128)(2,1)}), bf16[8,8,4608]{2,1,0:T(8,128)(2,1)S(1)}, u32[]{:S(2)}, u32[]{:S(2)}) %all-to-all-start.1) | async-done | bytes 589856 | tf_op jit(solution)/shard_map/while/body/eval_jaxpr/all_to_all | solution.py:31
  253.2 3.9 fusion.115
  259.6 4.1 fusion.119
  263.7 3.5 all-to-all-start
  267.3 12.4 %all-to-all-done = bf16[8,8,4608]{2,1,0:T(8,128)(2,1)S(1)} async-done(((bf16[8,8,4608]{2,1,0:T(8,128)(2,1)}), bf16[8,8,4608]{2,1,0:T(8,128)(2,1)S(1)}, u32[]{:S(2)}, u32[]{:S(2)}) %all-to-all-start) | async-done | bytes 589856 | tf_op jit(solution)/shard_map/while/body/eval_jaxpr/all_to_all | solution.py:31
  282.8 4.7 collective-permute-done
  288.4 3.5 all-to-all-start.1
  292.6 11.6 %all-to-all-done.1 = bf16[8,8,4608]{2,1,0:T(8,128)(2,1)S(1)} async-done(((bf16[8,8,4608]{2,1,0:T(8,128)(2,1)}), bf16[8,8,4608]{2,1,0:T(8,128)(2,1)S(1)}, u32[]{:S(2)}, u32[]{:S(2)}) %all-to-all-start.1) | async-done | bytes 589856 | tf_op jit(solution)/shard_map/while/body/eval_jaxpr/all_to_all | solution.py:31
  316.5 3.9 fusion.115
  322.8 4.1 fusion.119
  326.9 3.5 all-to-all-start
  330.5 12.4 %all-to-all-done = bf16[8,8,4608]{2,1,0:T(8,128)(2,1)S(1)} async-done(((bf16[8,8,4608]{2,1,0:T(8,128)(2,1)}), bf16[8,8,4608]{2,1,0:T(8,128)(2,1)S(1)}, u32[]{:S(2)}, u32[]{:S(2)}) %all-to-all-start) | async-done | bytes 589856 | tf_op jit(solution)/shard_map/while/body/eval_jaxpr/all_to_all | solution.py:31
  346.1 4.7 collective-permute-done
  351.6 3.5 all-to-all-start.1
  355.9 11.6 %all-to-all-done.1 = bf16[8,8,4608]{2,1,0:T(8,128)(2,1)S(1)} async-done(((bf16[8,8,4608]{2,1,0:T(8,128)(2,1)}), bf16[8,8,4608]{2,1,0:T(8,128)(2,1)S(1)}, u32[]{:S(2)}, u32[]{:S(2)}) %all-to-all-start.1) | async-done | bytes 589856 | tf_op jit(solution)/shard_map/while/body/eval_jaxpr/all_to_all | solution.py:31
  379.7 3.9 fusion.115
  386.1 4.1 fusion.119
  390.2 3.5 all-to-all-start
  393.7 12.4 %all-to-all-done = bf16[8,8,4608]{2,1,0:T(8,128)(2,1)S(1)} async-done(((bf16[8,8,4608]{2,1,0:T(8,128)(2,1)}), bf16[8,8,4608]{2,1,0:T(8,128)(2,1)S(1)}, u32[]{:S(2)}, u32[]{:S(2)}) %all-to-all-start) | async-done | bytes 589856 | tf_op jit(solution)/shard_map/while/body/eval_jaxpr/all_to_all | solution.py:31
  409.3 4.7 collective-permute-done
  414.8 3.5 all-to-all-start.1
  419.1 11.6 %all-to-all-done.1 = bf16[8,8,4608]{2,1,0:T(8,128)(2,1)S(1)} async-done(((bf16[8,8,4608]{2,1,0:T(8,128)(2,1)}), bf16[8,8,4608]{2,1,0:T(8,128)(2,1)S(1)}, u32[]{:S(2)}, u32[]{:S(2)}) %all-to-all-start.1) | async-done | bytes 589856 | tf_op jit(solution)/shard_map/while/body/eval_jaxpr/all_to_all | solution.py:31
  442.9 3.9 fusion.115
  449.3 4.1 fusion.119
  453.4 3.5 all-to-all-start
  456.9 12.4 %all-to-all-done = bf16[8,8,4608]{2,1,0:T(8,128)(2,1)S(1)} async-done(((bf16[8,8,4608]{2,1,0:T(8,128)(2,1)}), bf16[8,8,4608]{2,1,0:T(8,128)(2,1)S(1)}, u32[]{:S(2)}, u32[]{:S(2)}) %all-to-all-start) | async-done | bytes 589856 | tf_op jit(solution)/shard_map/while/body/eval_jaxpr/all_to_all | solution.py:31
  472.5 4.7 collective-permute-done
  478.1 3.5 all-to-all-start.1
  482.3 11.6 %all-to-all-done.1 = bf16[8,8,4608]{2,1,0:T(8,128)(2,1)S(1)} async-done(((bf16[8,8,4608]{2,1,0:T(8,128)(2,1)}), bf16[8,8,4608]{2,1,0:T(8,128)(2,1)S(1)}, u32[]{:S(2)}, u32[]{:S(2)}) %all-to-all-start.1) | async-done | bytes 589856 | tf_op jit(solution)/shard_map/while/body/eval_jaxpr/all_to_all | solution.py:31
  506.1 3.9 fusion.115
  512.5 4.1 fusion.119
  516.6 3.5 all-to-all-start
  520.1 12.4 %all-to-all-done = bf16[8,8,4608]{2,1,0:T(8,128)(2,1)S(1)} async-done(((bf16[8,8,4608]{2,1,0:T(8,128)(2,1)}), bf16[8,8,4608]{2,1,0:T(8,128)(2,1)S(1)}, u32[]{:S(2)}, u32[]{:S(2)}) %all-to-all-start) | async-done | bytes 589856 | tf_op jit(solution)/shard_map/while/body/eval_jaxpr/all_to_all | solution.py:31
  535.7 4.7 collective-permute-done
  545.5 11.6 %all-to-all-done.1 = bf16[8,8,4608]{2,1,0:T(8,128)(2,1)S(1)} async-done(((bf16[8,8,4608]{2,1,0:T(8,128)(2,1)}), bf16[8,8,4608]{2,1,0:T(8,128)(2,1)S(1)}, u32[]{:S(2)}, u32[]{:S(2)}) %all-to-all-start.1) | async-done | bytes 589856 | tf_op jit(solution)/shard_map/while/body/eval_jaxpr/all_to_all | solution.py:31
  559.8 4.0 fusion.51
  571.4 4.1 fusion.34
  575.5 3.7 all-to-all-start.3
  579.2 12.4 %all-to-all-done.3 = bf16[8,8,4608]{2,1,0:T(8,128)(2,1)S(1)} async-done(((bf16[8,8,4608]{2,1,0:T(8,128)(2,1)}), bf16[8,8,4608]{2,1,0:T(8,128)(2,1)S(1)}, u32[]{:S(2)}, u32[]{:S(2)}) %all-to-all-start.3) | async-done | bytes 589856 | tf_op jit(solution)/shard_map/all_to_all | solution.py:31
  603.3 3.6 all_gather.25
  (295 shorter events, 193.0 us)
Async XLA Ops:
  9.0 29.6 %all-to-all-start.2 = ((bf16[8,2,64,576]{3,2,1,0:T(8,128)(2,1)}), bf16[8,2,64,576]{3,2,1,0:T(8,128)(2,1)}, u32[]{:S(2)}, u32[]{:S(2)}) async-start(bf16[8,2,64,576]{3,2,1,0:T(8,128)(2,1)} %broadcast_in_dim.95), calls=%async_computation.2 | async-start | bytes 2621440 | tf_op jit(solution)/shard_map/all_to_all | solution.py:31
  15.5 6.9 %copy-start.1 = (bf16[1,4608,256]{2,1,0:T(8,128)(2,1)S(1)}, bf16[1,4608,256]{2,1,0:T(8,128)(2,1)}, u32[]{:S(2)}) copy-start(bf16[1,4608,256]{2,1,0:T(8,128)(2,1)} %param.14) | copy-start | bytes 7077892
  31.6 6.2 %copy-start.7 = (bf16[1,4608]{1,0:T(2,128)(2,1)S(1)}, bf16[1,4608]{1,0:T(2,128)(2,1)}, u32[]{:S(2)}) copy-start(bf16[1,4608]{1,0:T(2,128)(2,1)} %param.17) | copy-start | bytes 27652
  31.6 6.2 %copy-start.8 = (bf16[1,4608]{1,0:T(2,128)(2,1)S(1)}, bf16[1,4608]{1,0:T(2,128)(2,1)}, u32[]{:S(2)}) copy-start(bf16[1,4608]{1,0:T(2,128)(2,1)} %param.12) | copy-start | bytes 27652
  44.4 6.6 %copy-start = (bf16[1,4608,256]{2,1,0:T(8,128)(2,1)S(1)}, bf16[1,4608,256]{2,1,0:T(8,128)(2,1)}, u32[]{:S(2)}) copy-start(bf16[1,4608,256]{2,1,0:T(8,128)(2,1)} %param.15) | copy-start | bytes 7077892
  72.3 19.4 %all-to-all-start = ((bf16[8,8,4608]{2,1,0:T(8,128)(2,1)}), bf16[8,8,4608]{2,1,0:T(8,128)(2,1)S(1)}, u32[]{:S(2)}, u32[]{:S(2)}) async-start(bf16[8,8,4608]{2,1,0:T(8,128)(2,1)} %fusion.119), calls=%async_computation | async-start | bytes 1179648 | tf_op jit(solution)/shard_map/while/body/eval_jaxpr/all_to_all | solution.py:31
  93.5 5.1 collective-permute-start
  99.5 15.2 %all-to-all-start.1 = ((bf16[8,8,4608]{2,1,0:T(8,128)(2,1)}), bf16[8,8,4608]{2,1,0:T(8,128)(2,1)S(1)}, u32[]{:S(2)}, u32[]{:S(2)}) async-start(bf16[8,8,4608]{2,1,0:T(8,128)(2,1)} %broadcast_in_dim.108), calls=%async_computation.1 | async-start | bytes 1179648 | tf_op jit(solution)/shard_map/while/body/eval_jaxpr/all_to_all | solution.py:31
  138.0 15.9 %all-to-all-start = ((bf16[8,8,4608]{2,1,0:T(8,128)(2,1)}), bf16[8,8,4608]{2,1,0:T(8,128)(2,1)S(1)}, u32[]{:S(2)}, u32[]{:S(2)}) async-start(bf16[8,8,4608]{2,1,0:T(8,128)(2,1)} %fusion.119), calls=%async_computation | async-start | bytes 1179648 | tf_op jit(solution)/shard_map/while/body/eval_jaxpr/all_to_all | solution.py:31
  155.8 5.3 collective-permute-start
  162.0 15.7 %all-to-all-start.1 = ((bf16[8,8,4608]{2,1,0:T(8,128)(2,1)}), bf16[8,8,4608]{2,1,0:T(8,128)(2,1)S(1)}, u32[]{:S(2)}, u32[]{:S(2)}) async-start(bf16[8,8,4608]{2,1,0:T(8,128)(2,1)} %broadcast_in_dim.108), calls=%async_computation.1 | async-start | bytes 1179648 | tf_op jit(solution)/shard_map/while/body/eval_jaxpr/all_to_all | solution.py:31
  200.5 15.9 %all-to-all-start = ((bf16[8,8,4608]{2,1,0:T(8,128)(2,1)}), bf16[8,8,4608]{2,1,0:T(8,128)(2,1)S(1)}, u32[]{:S(2)}, u32[]{:S(2)}) async-start(bf16[8,8,4608]{2,1,0:T(8,128)(2,1)} %fusion.119), calls=%async_computation | async-start | bytes 1179648 | tf_op jit(solution)/shard_map/while/body/eval_jaxpr/all_to_all | solution.py:31
  218.3 6.0 collective-permute-start
  225.2 15.8 %all-to-all-start.1 = ((bf16[8,8,4608]{2,1,0:T(8,128)(2,1)}), bf16[8,8,4608]{2,1,0:T(8,128)(2,1)S(1)}, u32[]{:S(2)}, u32[]{:S(2)}) async-start(bf16[8,8,4608]{2,1,0:T(8,128)(2,1)} %broadcast_in_dim.108), calls=%async_computation.1 | async-start | bytes 1179648 | tf_op jit(solution)/shard_map/while/body/eval_jaxpr/all_to_all | solution.py:31
  263.7 15.9 %all-to-all-start = ((bf16[8,8,4608]{2,1,0:T(8,128)(2,1)}), bf16[8,8,4608]{2,1,0:T(8,128)(2,1)S(1)}, u32[]{:S(2)}, u32[]{:S(2)}) async-start(bf16[8,8,4608]{2,1,0:T(8,128)(2,1)} %fusion.119), calls=%async_computation | async-start | bytes 1179648 | tf_op jit(solution)/shard_map/while/body/eval_jaxpr/all_to_all | solution.py:31
  281.5 6.0 collective-permute-start
  288.4 15.8 %all-to-all-start.1 = ((bf16[8,8,4608]{2,1,0:T(8,128)(2,1)}), bf16[8,8,4608]{2,1,0:T(8,128)(2,1)S(1)}, u32[]{:S(2)}, u32[]{:S(2)}) async-start(bf16[8,8,4608]{2,1,0:T(8,128)(2,1)} %broadcast_in_dim.108), calls=%async_computation.1 | async-start | bytes 1179648 | tf_op jit(solution)/shard_map/while/body/eval_jaxpr/all_to_all | solution.py:31
  326.9 15.9 %all-to-all-start = ((bf16[8,8,4608]{2,1,0:T(8,128)(2,1)}), bf16[8,8,4608]{2,1,0:T(8,128)(2,1)S(1)}, u32[]{:S(2)}, u32[]{:S(2)}) async-start(bf16[8,8,4608]{2,1,0:T(8,128)(2,1)} %fusion.119), calls=%async_computation | async-start | bytes 1179648 | tf_op jit(solution)/shard_map/while/body/eval_jaxpr/all_to_all | solution.py:31
  344.8 6.0 collective-permute-start
  351.6 15.8 %all-to-all-start.1 = ((bf16[8,8,4608]{2,1,0:T(8,128)(2,1)}), bf16[8,8,4608]{2,1,0:T(8,128)(2,1)S(1)}, u32[]{:S(2)}, u32[]{:S(2)}) async-start(bf16[8,8,4608]{2,1,0:T(8,128)(2,1)} %broadcast_in_dim.108), calls=%async_computation.1 | async-start | bytes 1179648 | tf_op jit(solution)/shard_map/while/body/eval_jaxpr/all_to_all | solution.py:31
  390.2 15.9 %all-to-all-start = ((bf16[8,8,4608]{2,1,0:T(8,128)(2,1)}), bf16[8,8,4608]{2,1,0:T(8,128)(2,1)S(1)}, u32[]{:S(2)}, u32[]{:S(2)}) async-start(bf16[8,8,4608]{2,1,0:T(8,128)(2,1)} %fusion.119), calls=%async_computation | async-start | bytes 1179648 | tf_op jit(solution)/shard_map/while/body/eval_jaxpr/all_to_all | solution.py:31
  408.0 6.0 collective-permute-start
  414.8 15.8 %all-to-all-start.1 = ((bf16[8,8,4608]{2,1,0:T(8,128)(2,1)}), bf16[8,8,4608]{2,1,0:T(8,128)(2,1)S(1)}, u32[]{:S(2)}, u32[]{:S(2)}) async-start(bf16[8,8,4608]{2,1,0:T(8,128)(2,1)} %broadcast_in_dim.108), calls=%async_computation.1 | async-start | bytes 1179648 | tf_op jit(solution)/shard_map/while/body/eval_jaxpr/all_to_all | solution.py:31
  453.4 15.9 %all-to-all-start = ((bf16[8,8,4608]{2,1,0:T(8,128)(2,1)}), bf16[8,8,4608]{2,1,0:T(8,128)(2,1)S(1)}, u32[]{:S(2)}, u32[]{:S(2)}) async-start(bf16[8,8,4608]{2,1,0:T(8,128)(2,1)} %fusion.119), calls=%async_computation | async-start | bytes 1179648 | tf_op jit(solution)/shard_map/while/body/eval_jaxpr/all_to_all | solution.py:31
  471.2 6.0 collective-permute-start
  478.1 15.8 %all-to-all-start.1 = ((bf16[8,8,4608]{2,1,0:T(8,128)(2,1)}), bf16[8,8,4608]{2,1,0:T(8,128)(2,1)S(1)}, u32[]{:S(2)}, u32[]{:S(2)}) async-start(bf16[8,8,4608]{2,1,0:T(8,128)(2,1)} %broadcast_in_dim.108), calls=%async_computation.1 | async-start | bytes 1179648 | tf_op jit(solution)/shard_map/while/body/eval_jaxpr/all_to_all | solution.py:31
  516.6 15.9 %all-to-all-start = ((bf16[8,8,4608]{2,1,0:T(8,128)(2,1)}), bf16[8,8,4608]{2,1,0:T(8,128)(2,1)S(1)}, u32[]{:S(2)}, u32[]{:S(2)}) async-start(bf16[8,8,4608]{2,1,0:T(8,128)(2,1)} %fusion.119), calls=%async_computation | async-start | bytes 1179648 | tf_op jit(solution)/shard_map/while/body/eval_jaxpr/all_to_all | solution.py:31
  534.4 6.0 collective-permute-start
  541.3 15.8 %all-to-all-start.1 = ((bf16[8,8,4608]{2,1,0:T(8,128)(2,1)}), bf16[8,8,4608]{2,1,0:T(8,128)(2,1)S(1)}, u32[]{:S(2)}, u32[]{:S(2)}) async-start(bf16[8,8,4608]{2,1,0:T(8,128)(2,1)} %broadcast_in_dim.108), calls=%async_computation.1 | async-start | bytes 1179648 | tf_op jit(solution)/shard_map/while/body/eval_jaxpr/all_to_all | solution.py:31
  559.8 4.1 copy-start.2
  563.8 1.6 copy-start.5
  563.8 1.6 copy-start.6
  575.5 16.3 %copy-start.3 = (bf16[2,8,4608]{2,1,0:T(8,128)(2,1)S(1)}, bf16[2,8,4608]{2,1,0:T(8,128)(2,1)}, u32[]{:S(2)}) copy-start(bf16[2,8,4608]{2,1,0:T(8,128)(2,1)} %get-tuple-element.221) | copy-start | bytes 442372
  575.5 16.3 %copy-start.4 = (f32[4608]{0:T(1024)S(1)}, f32[4608]{0:T(1024)}, u32[]{:S(2)}) copy-start(f32[4608]{0:T(1024)} %get-tuple-element.656) | copy-start | bytes 55300
  575.5 16.1 %all-to-all-start.3 = ((bf16[8,8,4608]{2,1,0:T(8,128)(2,1)}), bf16[8,8,4608]{2,1,0:T(8,128)(2,1)S(1)}, u32[]{:S(2)}, u32[]{:S(2)}) async-start(bf16[8,8,4608]{2,1,0:T(8,128)(2,1)} %fusion.34), calls=%async_computation.3 | async-start | bytes 1179648 | tf_op jit(solution)/shard_map/all_to_all | solution.py:31
  579.2 17.0 %copy-start.9 = (s32[4]{0:T(128)S(1)}, s32[4]{0:T(128)}, u32[]{:S(2)}) copy-start(s32[4]{0:T(128)} %param.11) | copy-start | bytes 52
  592.8 10.4 %all-to-all-start.4 = ((bf16[8,2,8,576]{3,2,1,0:T(8,128)(2,1)}), bf16[8,2,8,576]{3,2,1,0:T(8,128)(2,1)S(1)}, u32[]{:S(2)}, u32[]{:S(2)}) async-start(bf16[8,2,8,576]{3,2,1,0:T(8,128)(2,1)} %copy.112), calls=%async_computation.4 | async-start | bytes 327680 | tf_op jit(solution)/shard_map/all_to_all | solution.py:31

commit v2 on v1

v2 whole, which is shorter than its diff:
```python
import jax
import jax.numpy as jnp
from jax import lax
from jax.experimental import pallas as pl
from jax.experimental.pallas import tpu as pltpu
from jax.sharding import PartitionSpec as P

HEAD_DIM = 128
CHUNKS = 2

softcap_limit = 50.0
query_scale = 144.0 ** (-0.5)
epsilon = 1e-06
rotary_base = 10000.0
f32 = jnp.float32
bf16 = jnp.bfloat16

VMEM = pl.BlockSpec(memory_space=pltpu.VMEM)
SMEM = pl.BlockSpec(memory_space=pltpu.SMEM)
HBM = pl.BlockSpec(memory_space=pl.ANY)


def exchange(pieces):
    return lax.all_to_all(pieces, "tensor", split_axis=0, concat_axis=0, tiled=True)


def rope(u, cos_full, sin_full):
    return u * cos_full + pltpu.roll(u, HEAD_DIM // 2, 1) * sin_full


def key_value_kernel(place_ref, x_ref, gain_ref, cos_ref, sin_ref, wk_ref, wv_ref,
                     kv_ref, normed_ref, wk_buf, wv_buf, sems):
    steps, block, kv_width = wk_buf.shape
    rows, width = normed_ref.shape

    def copies(k):
        at = pl.ds(k * block, block)
        return (
            pltpu.make_async_copy(wk_ref.at[0, at], wk_buf.at[k], sems.at[0, k]),
            pltpu.make_async_copy(wv_ref.at[0, at], wv_buf.at[k], sems.at[1, k]),
        )

    for k in range(steps):
        for copy in copies(k):
            copy.start()
    squares = jnp.zeros((rows, 1), f32)
    for k in range(steps):
        x = x_ref[:, :, k * block:(k + 1) * block].astype(f32).reshape(rows, block)
        squares += jnp.sum(x * x, axis=1, keepdims=True)
    scaling = lax.rsqrt(squares / width + epsilon)
    for k in range(steps):
        at = slice(k * block, (k + 1) * block)
        x = x_ref[:, :, at].astype(f32).reshape(rows, block)
        normed_ref[:, at] = (x * scaling * gain_ref[:, at].astype(f32)).astype(bf16)
    key_sum = jnp.zeros((rows, kv_width), f32)
    value_sum = jnp.zeros((rows, kv_width), f32)
    for k in range(steps):
        for copy in copies(k):
            copy.wait()
        part = normed_ref[:, k * block:(k + 1) * block]
        key_sum += jnp.dot(part, wk_buf[k], preferred_element_type=f32)
        value_sum += jnp.dot(part, wv_buf[k], preferred_element_type=f32)
    slot = place_ref[0]
    cos_full, sin_full = cos_ref[slot], sin_ref[slot]
    for head in range(kv_width // HEAD_DIM):
        at = slice(head * HEAD_DIM, (head + 1) * HEAD_DIM)
        kv_ref[:, at] = rope(key_sum[:, at], cos_full, sin_full).astype(bf16)
    kv_ref[:, kv_width:] = value_sum.astype(bf16)


def query_kernel(place_ref, normed_ref, cos_ref, sin_ref, wq_ref, q_ref, wq_buf, sems):
    steps, block, q_width = wq_buf.shape
    rows = normed_ref.shape[0]

    def copy(k):
        return pltpu.make_async_copy(wq_ref.at[0, pl.ds(k * block, block)], wq_buf.at[k], sems.at[k])

    for k in range(steps):
        copy(k).start()
    total = jnp.zeros((rows, q_width), f32)
    for k in range(steps):
        copy(k).wait()
        total += jnp.dot(
            normed_ref[:, k * block:(k + 1) * block], wq_buf[k], preferred_element_type=f32
        )
    slot = place_ref[0]
    cos_full, sin_full = cos_ref[slot], sin_ref[slot]
    for head in range(q_width // HEAD_DIM):
        at = slice(head * HEAD_DIM, (head + 1) * HEAD_DIM)
        q_ref[:, at] = (rope(total[:, at], cos_full, sin_full) * query_scale).astype(bf16)


def attention_kernel(place_ref, q_ref, own_ref, other_ref, past_own_ref, past_other_ref, wo_ref,
                     out_ref, attended_ref, wo_buf, sems):
    steps, _, block = wo_buf.shape
    rows, q_width = q_ref.shape
    kv_width = own_ref.shape[1] // 2
    kv_heads = kv_width // HEAD_DIM
    group = q_width // kv_width

    def copy(n):
        return pltpu.make_async_copy(wo_ref.at[0, :, pl.ds(n * block, block)], wo_buf.at[n], sems.at[n])

    for n in range(steps):
        copy(n).start()
    has_past = place_ref[0] > 0
    is_later = place_ref[1] > 0
    row = lax.broadcasted_iota(jnp.int32, (group * rows, 4 * rows), 0) % rows
    col = lax.broadcasted_iota(jnp.int32, (group * rows, 4 * rows), 1)
    other_to = jnp.where(is_later, 2 * rows, rows)
    past_to = jnp.where(has_past, 4 * rows, 2 * rows)
    allowed = (
        ((col < rows) & (col <= row))
        | ((col >= rows) & (col < other_to))
        | ((col >= 2 * rows) & (col < past_to))
    )
    sources = (own_ref, other_ref, past_own_ref, past_other_ref)
    for head in range(kv_heads):
        at = slice(head * HEAD_DIM, (head + 1) * HEAD_DIM)
        value_at = slice(kv_width + head * HEAD_DIM, kv_width + (head + 1) * HEAD_DIM)
        keys = jnp.concatenate([s[:, at] for s in sources], axis=0)
        values = jnp.concatenate([s[:, value_at] for s in sources], axis=0)
        first = head * group * HEAD_DIM
        queries = jnp.concatenate(
            [q_ref[:, first + g * HEAD_DIM:first + (g + 1) * HEAD_DIM] for g in range(group)], axis=0
        )
        scores = lax.dot_general(
            queries, keys, (((1,), (1,)), ((), ())), preferred_element_type=f32
        )
        capped = softcap_limit * jnp.tanh(scores / softcap_limit)
        weight = jnp.where(allowed, jnp.exp(capped), f32(0.0))
        totals = jnp.sum(weight, axis=1, keepdims=True)
        numerator = jnp.dot(weight.astype(bf16), values, preferred_element_type=f32)
        attended = (numerator / totals).astype(bf16)
        for g in range(group):
            attended_ref[:, first + g * HEAD_DIM:first + (g + 1) * HEAD_DIM] = attended[
                g * rows:(g + 1) * rows
            ]
    owners, own = out_ref.shape[:2]
    for n in range(steps):
        copy(n).wait()
        part = jnp.dot(attended_ref[...], wo_buf[n], preferred_element_type=f32)
        out_ref[:, :, n * block:(n + 1) * block] = part.reshape(owners, own, block).astype(bf16)


def combine_kernel(arrived_ref, held_ref, gain_ref, out_ref):
    width = out_ref.shape[1]
    projected = jnp.sum(arrived_ref[...].astype(f32), axis=0)
    mean = jnp.sum(projected * projected, axis=1, keepdims=True) / width
    scaled = projected * lax.rsqrt(mean + epsilon) * gain_ref[...].astype(f32)
    out_ref[...] = (held_ref[...].astype(f32) + scaled).astype(bf16)


def body(states_in, span_order, pre_gain, w_query, w_key, w_value, w_out, post_gain):
    _, row_count, width_part = states_in.shape
    width = pre_gain.shape[1]
    q_width = w_query.shape[2]
    kv_width = w_key.shape[2]
    sections = lax.axis_size("section")
    tensors = lax.axis_size("tensor")
    seqs = lax.axis_size("seq")
    section_rank = lax.axis_index("section")
    seq_rank = lax.axis_index("seq")
    spans = span_order.shape[0]
    rows = row_count // CHUNKS
    own = rows // tensors
    chunk_len = rows * seqs
    in_steps, out_steps = 4, 4
    in_block, out_block = width // in_steps, width // out_steps
    ids = jnp.arange(spans, dtype=jnp.int32)

    blocks = lax.all_gather(states_in[0], "seq", axis=0).reshape(spans, rows, width_part)
    block_of = jnp.sum(jnp.where(span_order[None, :] == ids[:, None], ids[None, :], 0), axis=1)
    picked = jnp.stack(
        [
            lax.dynamic_index_in_dim(
                blocks,
                lax.dynamic_index_in_dim(block_of, c * seqs + seq_rank, 0, keepdims=False),
                0,
                keepdims=False,
            )
            for c in range(CHUNKS)
        ]
    )
    picked = jnp.moveaxis(picked.reshape(CHUNKS, tensors, own, width_part), 1, 0)
    first_rows = jnp.moveaxis(exchange(picked), 0, 2).reshape(CHUNKS, own, width)

    places = (
        jnp.arange(CHUNKS, dtype=jnp.int32)[:, None] * chunk_len
        + seq_rank * rows
        + jnp.arange(rows, dtype=jnp.int32)[None, :]
    )
    half = HEAD_DIM // 2
    inverse = rotary_base ** (-(jnp.arange(half, dtype=f32) * 2.0 / HEAD_DIM))
    angles = places.astype(f32)[..., None] * inverse
    cos_part, sin_part = jnp.cos(angles), jnp.sin(angles)
    cos_full = jnp.concatenate([cos_part, cos_part], axis=-1)
    sin_full = jnp.concatenate([-sin_part, sin_part], axis=-1)

    key_value = pl.pallas_call(
        key_value_kernel,
        out_shape=(
            jax.ShapeDtypeStruct((rows, 2 * kv_width), bf16),
            jax.ShapeDtypeStruct((rows, width), bf16),
        ),
        in_specs=[SMEM, VMEM, VMEM, VMEM, VMEM, HBM, HBM],
        out_specs=(VMEM, VMEM),
        scratch_shapes=[
            pltpu.VMEM((in_steps, in_block, kv_width), bf16),
            pltpu.VMEM((in_steps, in_block, kv_width), bf16),
            pltpu.SemaphoreType.DMA((2, in_steps)),
        ],
        name="key_value",
    )
    query = pl.pallas_call(
        query_kernel,
        out_shape=jax.ShapeDtypeStruct((rows, q_width), bf16),
        in_specs=[SMEM, VMEM, VMEM, VMEM, HBM],
        out_specs=VMEM,
        scratch_shapes=[
            pltpu.VMEM((in_steps, in_block, q_width), bf16),
            pltpu.SemaphoreType.DMA((in_steps,)),
        ],
        name="query",
    )
    attention = pl.pallas_call(
        attention_kernel,
        out_shape=jax.ShapeDtypeStruct((tensors, own, width), bf16),
        in_specs=[SMEM, VMEM, VMEM, VMEM, VMEM, VMEM, HBM],
        out_specs=VMEM,
        scratch_shapes=[
            pltpu.VMEM((rows, q_width), bf16),
            pltpu.VMEM((out_steps, q_width, out_block), bf16),
            pltpu.SemaphoreType.DMA((out_steps,)),
        ],
        name="attention",
    )
    combine = pl.pallas_call(
        combine_kernel,
        out_shape=jax.ShapeDtypeStruct((own, width), bf16),
        in_specs=[VMEM, VMEM, VMEM],
        out_specs=VMEM,
        name="combine",
    )

    def work(held, past_own, past_other, tick_index):
        slot = jnp.clip(tick_index - section_rank, 0, CHUNKS - 1)
        place = jnp.stack([slot, seq_rank]).astype(jnp.int32)
        full = exchange(jnp.broadcast_to(held[None], (tensors, own, width)))
        kv_own, normed = key_value(place, full, pre_gain, cos_full, sin_full, w_key, w_value)
        kv_other = lax.ppermute(kv_own, "seq", [(0, 1), (1, 0)])
        queries = query(place, normed, cos_full, sin_full, w_query)
        terms = attention(place, queries, kv_own, kv_other, past_own, past_other, w_out)
        return combine(exchange(terms), held, post_gain), kv_own, kv_other

    def tick(carried, tick_index):
        held, past_own, past_other = carried
        new_rows, past_own, past_other = work(held, past_own, past_other, tick_index)
        moved = lax.ppermute(new_rows, "section", [(i, i + 1) for i in range(sections - 1)])
        following = lax.dynamic_index_in_dim(
            first_rows, jnp.minimum(tick_index + 1, CHUNKS - 1), 0, keepdims=False
        )
        held = jnp.where(section_rank == 0, following, moved)
        return (held, past_own, past_other), new_rows

    tick_total = sections + CHUNKS - 1
    no_past = jnp.zeros((rows, 2 * kv_width), bf16)
    carried, made = lax.scan(
        tick, (first_rows[0], no_past, no_past), jnp.arange(tick_total - 1, dtype=jnp.int32)
    )
    last_rows = work(*carried, jnp.int32(tick_total - 1))[0]
    made = jnp.concatenate([made, last_rows[None]], axis=0)
    record = lax.dynamic_slice_in_dim(made, section_rank, CHUNKS, 0)

    pieces = jnp.moveaxis(record.reshape(CHUNKS, own, tensors, width_part), 2, 0)
    pieces = jnp.moveaxis(exchange(pieces), 0, 1).reshape(CHUNKS, rows, width_part)
    ordered = lax.all_gather(pieces, "seq", axis=1).reshape(spans, rows, width_part)
    mine = lax.dynamic_slice_in_dim(span_order, seq_rank * CHUNKS, CHUNKS, 0)
    out = [lax.dynamic_index_in_dim(ordered, mine[j], 0, keepdims=False) for j in range(CHUNKS)]
    return jnp.concatenate(out, axis=0)[None, None]


def solution(mesh):
    in_specs = (
        P(None, "seq", "tensor"),
        P(),
        P("section", None),
        P("section", None, "tensor"),
        P("section", None, "tensor"),
        P("section", None, "tensor"),
        P("section", "tensor", None),
        P("section", None),
    )
    out_specs = P("section", None, "seq", "tensor")
    return jax.shard_map(body, mesh=mesh, in_specs=in_specs, out_specs=out_specs, check_vma=False)
```

time: 616 us -> 558 us (0.906)
  Pallas kernels: 0 us -> 140 us
  matrix products: 111 us -> 0 us
  local copies, waits for them, and re-layouts: 90.1 us -> 50.8 us
  other arithmetic: 32.9 us -> 7.88 us
  blocking collectives: 28.8 us -> 6.14 us
  starting transfers between devices: 83.7 us -> 93.8 us
  waiting for transfers between devices: 242 us -> 235 us
    pallas_call x0 -> x36, Pallas kernels: none -> 140 us  [the longest x9 41.8 us: work(): attention(place, queries, kv_own, kv_other, past_own, past_other, w_out)]
    dot_general x54 -> x0, matrix products: 111 us -> none  [the longest x9 37 us: layer(): jnp.dot(attended.reshape(rows, q_width), w_out[0], preferred_element_type...]
    all_gather x9 -> x0, blocking collectives: 22.7 us -> none  [layer(): lax.all_gather(jnp.concatenate([key_rows, value_rows], axis=1), 'seq', ax...]
    select_n x17 -> x8, other arithmetic: 22.2 us -> 0.08 us  [tick(): held = jnp.where(section_rank == 0, following, moved)]
    reshape x29 -> x2, local copies, waits for them, and re-layouts: 19.1 us -> 0.3 us  [the longest x1 0.16 us: body(): record.reshape(CHUNKS, own, tensors, width_part)]
    while x2 -> x96, local copies, waits for them, and re-layouts: 9.37 us -> 24.9 us  [body(): lax.scan(tick, start, jnp.arange(tick_total - 1, dtype=jnp.int32))]
    ppermute x0 -> x9, starting transfers between devices: none -> 9.93 us  [work(): kv_other = lax.ppermute(kv_own, 'seq', [(0, 1), (1, 0)])]
    dot_general x2 -> x0, local copies, waits for them, and re-layouts: 9.27 us -> none  [the longest x1 6.75 us: layer(): queries = jnp.dot(normed, w_query[0], preferred_element_type=f32)]
  transfers between devices with their start and end apart: 27 -> 37, of which waited for: 26 -> 28; matrix products, arithmetic and copies ran while one was open for 4% -> 5% of each run, Pallas kernels for 0% -> 7%
where the time goes in v2:
time: 558 us; the launch traced here: 551 us
  waiting for transfers between devices  235 us (42%)
  Pallas kernels  140 us (25%)
  starting transfers between devices  93.8 us (17%)
  local copies, waits for them, and re-layouts  50.8 us (9%)
  loops' own time  9.87 us (2%)
  between operations  8.12 us (1%)
  other arithmetic  7.88 us (1%)
  blocking collectives  6.14 us (1%)
    all_to_all x20, waiting for transfers between devices, exchange(): lax.all_to_all(pieces, 'tensor', split_axis=0, concat_axis=0, tiled=True)  204 us
    all_to_all x20, starting transfers between devices, exchange(): lax.all_to_all(pieces, 'tensor', split_axis=0, concat_axis=0, tiled=True)  73.6 us
    pallas_call x9, Pallas kernels, work(): attention(place, queries, kv_own, kv_other, past_own, past_other, w_out)  41.8 us
    pallas_call x9, Pallas kernels, work(): key_value(place, full, pre_gain, cos_full, sin_full, w_key, w_value)  40.3 us
    pallas_call x9, Pallas kernels, work(): queries = query(place, normed, cos_full, sin_full, w_query)  40.3 us
    ppermute x8, waiting for transfers between devices, tick(): lax.ppermute(new_rows, 'section', [(i, i + 1) for i in range(sections - 1)])  30.4 us
    while x96, local copies, waits for them, and re-layouts  24.9 us
    pallas_call x9, Pallas kernels, work(): return (combine(exchange(terms), held, post_gain), kv_own, kv_other)  17.3 us
  transfers between devices with their start and end apart: 37, of which 28 were waited for; matrix products, arithmetic and copies ran while one was open for 5% of the time, Pallas kernels for 7%

profile of v2, /device:TPU:57, one launch (start us, length us, event | category | flops | bytes accessed | tf_op | source)
XLA Modules:
  0.0 550.9 jit_solution(1875320512309955496)
XLA Ops:
  9.1 6.4 %all-to-all-start.2 = ((bf16[8,2,8,576]{3,2,1,0:T(8,128)(2,1)}), bf16[8,2,8,576]{3,2,1,0:T(8,128)(2,1)S(1)}, u32[]{:S(2)}, u32[]{:S(2)}) async-start(bf16[8,2,8,576]{3,2,1,0:T(8,128)(2,1)} %copy.31), calls=%async_computation.2 | async-start | bytes 327680 | tf_op jit(solution)/shard_map/all_to_all | solution.py:24
  15.9 6.7 %all-to-all-done.2 = bf16[8,2,8,576]{3,2,1,0:T(8,128)(2,1)S(1)} async-done(((bf16[8,2,8,576]{3,2,1,0:T(8,128)(2,1)}), bf16[8,2,8,576]{3,2,1,0:T(8,128)(2,1)S(1)}, u32[]{:S(2)}, u32[]{:S(2)}) %all-to-all-start.2) | async-done | bytes 147488 | tf_op jit(solution)/shard_map/all_to_all | solution.py:24
  23.0 459.7 %while.17 = (s32[]{:T(128)}, bf16[8,4608]{1,0:T(8,128)(2,1)S(1)}, bf16[64,512]{1,0:T(8,128)(2,1)S(1)}, bf16[64,512]{1,0:T(8,128)(2,1)S(1)}, bf16[8,8,4608]{2,1,0...) while((s32[]{:T(128)}, bf16[8,4608]{1,0:T(8,128)(2,1)S(1)}, ...), condition=%wide.region_2.3_spmd, body=%wide.region_1.2_spmd.sunk | while | flops 36876 | bytes 10670692 | solution.py:268
  29.1 10.4 %all-to-all-done.x_ref = bf16[8,8,4608]{2,1,0:T(8,128)(2,1)S(1)} async-done(((bf16[8,8,4608]{2,1,0:T(8,128)(2,1)}), bf16[8,8,4608]{2,1,0:T(8,128)(2,1)S(1)}, u32[]{:S(2)}, u32[]{:S(2)}) %all-to-all-start) | async-done | bytes 589856 | tf_op jit(solution)/shard_map/while/body/eval_jaxpr/all_to_all | solution.py:24
  40.3 4.5 key_value.4
  46.0 4.5 query.3.q_ref
  51.1 4.6 attention.4
  55.8 3.5 all-to-all-start.1
  60.7 11.0 %all-to-all-done.1.arrived_ref = bf16[8,8,4608]{2,1,0:T(8,128)(2,1)S(1)} async-done(((bf16[8,8,4608]{2,1,0:T(8,128)(2,1)}), bf16[8,8,4608]{2,1,0:T(8,128)(2,1)S(1)}, u32[]{:S(2)}, u32[]{:S(2)}) %all-to-all-start.1) | async-done | bytes 589856 | tf_op jit(solution)/shard_map/while/body/eval_jaxpr/all_to_all | solution.py:24
  85.9 9.9 %all-to-all-done.x_ref = bf16[8,8,4608]{2,1,0:T(8,128)(2,1)S(1)} async-done(((bf16[8,8,4608]{2,1,0:T(8,128)(2,1)}), bf16[8,8,4608]{2,1,0:T(8,128)(2,1)S(1)}, u32[]{:S(2)}, u32[]{:S(2)}) %all-to-all-start) | async-done | bytes 589856 | tf_op jit(solution)/shard_map/while/body/eval_jaxpr/all_to_all | solution.py:24
  96.7 4.5 key_value.4
  102.8 4.5 query.3.q_ref
  107.9 4.6 attention.4
  112.5 3.5 all-to-all-start.1
  117.5 11.0 %all-to-all-done.1.arrived_ref = bf16[8,8,4608]{2,1,0:T(8,128)(2,1)S(1)} async-done(((bf16[8,8,4608]{2,1,0:T(8,128)(2,1)}), bf16[8,8,4608]{2,1,0:T(8,128)(2,1)S(1)}, u32[]{:S(2)}, u32[]{:S(2)}) %all-to-all-start.1) | async-done | bytes 589856 | tf_op jit(solution)/shard_map/while/body/eval_jaxpr/all_to_all | solution.py:24
  142.8 10.4 %all-to-all-done.x_ref = bf16[8,8,4608]{2,1,0:T(8,128)(2,1)S(1)} async-done(((bf16[8,8,4608]{2,1,0:T(8,128)(2,1)}), bf16[8,8,4608]{2,1,0:T(8,128)(2,1)S(1)}, u32[]{:S(2)}, u32[]{:S(2)}) %all-to-all-start) | async-done | bytes 589856 | tf_op jit(solution)/shard_map/while/body/eval_jaxpr/all_to_all | solution.py:24
  154.1 4.5 key_value.4
  159.7 4.5 query.3.q_ref
  164.8 4.6 attention.4
  169.5 3.5 all-to-all-start.1
  174.5 11.0 %all-to-all-done.1.arrived_ref = bf16[8,8,4608]{2,1,0:T(8,128)(2,1)S(1)} async-done(((bf16[8,8,4608]{2,1,0:T(8,128)(2,1)}), bf16[8,8,4608]{2,1,0:T(8,128)(2,1)S(1)}, u32[]{:S(2)}, u32[]{:S(2)}) %all-to-all-start.1) | async-done | bytes 589856 | tf_op jit(solution)/shard_map/while/body/eval_jaxpr/all_to_all | solution.py:24
  190.3 4.0 collective-permute-done.1
  200.5 10.5 %all-to-all-done.x_ref = bf16[8,8,4608]{2,1,0:T(8,128)(2,1)S(1)} async-done(((bf16[8,8,4608]{2,1,0:T(8,128)(2,1)}), bf16[8,8,4608]{2,1,0:T(8,128)(2,1)S(1)}, u32[]{:S(2)}, u32[]{:S(2)}) %all-to-all-start) | async-done | bytes 589856 | tf_op jit(solution)/shard_map/while/body/eval_jaxpr/all_to_all | solution.py:24
  211.9 4.5 key_value.4
  217.4 4.5 query.3.q_ref
  222.5 4.6 attention.4
  227.1 3.5 all-to-all-start.1
  232.1 11.0 %all-to-all-done.1.arrived_ref = bf16[8,8,4608]{2,1,0:T(8,128)(2,1)S(1)} async-done(((bf16[8,8,4608]{2,1,0:T(8,128)(2,1)}), bf16[8,8,4608]{2,1,0:T(8,128)(2,1)S(1)}, u32[]{:S(2)}, u32[]{:S(2)}) %all-to-all-start.1) | async-done | bytes 589856 | tf_op jit(solution)/shard_map/while/body/eval_jaxpr/all_to_all | solution.py:24
  248.0 4.0 collective-permute-done.1
  258.2 10.5 %all-to-all-done.x_ref = bf16[8,8,4608]{2,1,0:T(8,128)(2,1)S(1)} async-done(((bf16[8,8,4608]{2,1,0:T(8,128)(2,1)}), bf16[8,8,4608]{2,1,0:T(8,128)(2,1)S(1)}, u32[]{:S(2)}, u32[]{:S(2)}) %all-to-all-start) | async-done | bytes 589856 | tf_op jit(solution)/shard_map/while/body/eval_jaxpr/all_to_all | solution.py:24
  269.5 4.5 key_value.4
  275.0 4.5 query.3.q_ref
  280.2 4.6 attention.4
  284.8 3.5 all-to-all-start.1
  289.8 11.0 %all-to-all-done.1.arrived_ref = bf16[8,8,4608]{2,1,0:T(8,128)(2,1)S(1)} async-done(((bf16[8,8,4608]{2,1,0:T(8,128)(2,1)}), bf16[8,8,4608]{2,1,0:T(8,128)(2,1)S(1)}, u32[]{:S(2)}, u32[]{:S(2)}) %all-to-all-start.1) | async-done | bytes 589856 | tf_op jit(solution)/shard_map/while/body/eval_jaxpr/all_to_all | solution.py:24
  305.7 4.0 collective-permute-done.1
  315.9 10.5 %all-to-all-done.x_ref = bf16[8,8,4608]{2,1,0:T(8,128)(2,1)S(1)} async-done(((bf16[8,8,4608]{2,1,0:T(8,128)(2,1)}), bf16[8,8,4608]{2,1,0:T(8,128)(2,1)S(1)}, u32[]{:S(2)}, u32[]{:S(2)}) %all-to-all-start) | async-done | bytes 589856 | tf_op jit(solution)/shard_map/while/body/eval_jaxpr/all_to_all | solution.py:24
  327.2 4.5 key_value.4
  332.7 4.5 query.3.q_ref
  337.8 4.6 attention.4
  342.5 3.5 all-to-all-start.1
  347.5 11.0 %all-to-all-done.1.arrived_ref = bf16[8,8,4608]{2,1,0:T(8,128)(2,1)S(1)} async-done(((bf16[8,8,4608]{2,1,0:T(8,128)(2,1)}), bf16[8,8,4608]{2,1,0:T(8,128)(2,1)S(1)}, u32[]{:S(2)}, u32[]{:S(2)}) %all-to-all-start.1) | async-done | bytes 589856 | tf_op jit(solution)/shard_map/while/body/eval_jaxpr/all_to_all | solution.py:24
  363.4 4.0 collective-permute-done.1
  373.5 10.5 %all-to-all-done.x_ref = bf16[8,8,4608]{2,1,0:T(8,128)(2,1)S(1)} async-done(((bf16[8,8,4608]{2,1,0:T(8,128)(2,1)}), bf16[8,8,4608]{2,1,0:T(8,128)(2,1)S(1)}, u32[]{:S(2)}, u32[]{:S(2)}) %all-to-all-start) | async-done | bytes 589856 | tf_op jit(solution)/shard_map/while/body/eval_jaxpr/all_to_all | solution.py:24
  384.9 4.5 key_value.4
  390.4 4.5 query.3.q_ref
  395.5 4.6 attention.4
  400.2 3.5 all-to-all-start.1
  405.1 11.0 %all-to-all-done.1.arrived_ref = bf16[8,8,4608]{2,1,0:T(8,128)(2,1)S(1)} async-done(((bf16[8,8,4608]{2,1,0:T(8,128)(2,1)}), bf16[8,8,4608]{2,1,0:T(8,128)(2,1)S(1)}, u32[]{:S(2)}, u32[]{:S(2)}) %all-to-all-start.1) | async-done | bytes 589856 | tf_op jit(solution)/shard_map/while/body/eval_jaxpr/all_to_all | solution.py:24
  421.0 4.0 collective-permute-done.1
  431.2 10.5 %all-to-all-done.x_ref = bf16[8,8,4608]{2,1,0:T(8,128)(2,1)S(1)} async-done(((bf16[8,8,4608]{2,1,0:T(8,128)(2,1)}), bf16[8,8,4608]{2,1,0:T(8,128)(2,1)S(1)}, u32[]{:S(2)}, u32[]{:S(2)}) %all-to-all-start) | async-done | bytes 589856 | tf_op jit(solution)/shard_map/while/body/eval_jaxpr/all_to_all | solution.py:24
  442.6 4.5 key_value.4
  448.1 4.5 query.3.q_ref
  453.2 4.6 attention.4
  457.8 3.5 all-to-all-start.1
  462.8 11.0 %all-to-all-done.1.arrived_ref = bf16[8,8,4608]{2,1,0:T(8,128)(2,1)S(1)} async-done(((bf16[8,8,4608]{2,1,0:T(8,128)(2,1)}), bf16[8,8,4608]{2,1,0:T(8,128)(2,1)S(1)}, u32[]{:S(2)}, u32[]{:S(2)}) %all-to-all-start.1) | async-done | bytes 589856 | tf_op jit(solution)/shard_map/while/body/eval_jaxpr/all_to_all | solution.py:24
  478.7 4.0 collective-permute-done.1
  487.8 11.6 %all-to-all-done.3.x_ref = bf16[8,8,4608]{2,1,0:T(8,128)(2,1)S(1)} async-done(((bf16[8,8,4608]{2,1,0:T(8,128)(2,1)}), bf16[8,8,4608]{2,1,0:T(8,128)(2,1)S(1)}, u32[]{:S(2)}, u32[]{:S(2)}) %all-to-all-start.3) | async-done | bytes 589856 | tf_op jit(solution)/shard_map/all_to_all | solution.py:24
  500.2 4.5 key_value.3
  505.7 4.5 query.2.q_ref
  510.9 4.6 attention.3
  515.5 3.5 all-to-all-start.4
  519.1 12.4 %all-to-all-done.4.arrived_ref = bf16[8,8,4608]{2,1,0:T(8,128)(2,1)S(1)} async-done(((bf16[8,8,4608]{2,1,0:T(8,128)(2,1)}), bf16[8,8,4608]{2,1,0:T(8,128)(2,1)S(1)}, u32[]{:S(2)}, u32[]{:S(2)}) %all-to-all-start.4) | async-done | bytes 589856 | tf_op jit(solution)/shard_map/all_to_all | solution.py:24
  546.4 3.6 all_gather.7
  (227 shorter events, 142.7 us)
Async XLA Ops:
  9.1 13.5 %all-to-all-start.2 = ((bf16[8,2,8,576]{3,2,1,0:T(8,128)(2,1)}), bf16[8,2,8,576]{3,2,1,0:T(8,128)(2,1)S(1)}, u32[]{:S(2)}, u32[]{:S(2)}) async-start(bf16[8,2,8,576]{3,2,1,0:T(8,128)(2,1)} %copy.31), calls=%async_computation.2 | async-start | bytes 327680 | tf_op jit(solution)/shard_map/all_to_all | solution.py:24
  23.8 15.7 %all-to-all-start = ((bf16[8,8,4608]{2,1,0:T(8,128)(2,1)}), bf16[8,8,4608]{2,1,0:T(8,128)(2,1)S(1)}, u32[]{:S(2)}, u32[]{:S(2)}) async-start(bf16[8,8,4608]{2,1,0:T(8,128)(2,1)} %broadcast_in_dim.59), calls=%async_computation | async-start | bytes 1179648 | tf_op jit(solution)/shard_map/while/body/eval_jaxpr/all_to_all | solution.py:24
  39.5 0.8 copy-start.1
  44.8 5.7 %collective-permute-start = (bf16[64,512]{1,0:T(8,128)(2,1)}, bf16[64,512]{1,0:T(8,128)(2,1)S(1)}, u32[]{:S(2)}, u32[]{:S(2)}) collective-permute-start(bf16[64,512]{1,0:T(8,128)(2,1)} %get-tuple-element.373.own_ref), channel_id=1, source_target_pairs={{0,8},{8,0},{1,9},{9,1},{2,10},{10,2},{3,11},{11,3},{4,12},{12,4},... | collective-permute-start | bytes 196616 | tf_op jit(solution)/shard_map/while/body/eval_jaxpr/ppermute | solution.py:251
  50.5 9.4 %copy-start.2 = (bf16[64,512]{1,0:T(8,128)(2,1)S(1)}, bf16[64,512]{1,0:T(8,128)(2,1)}, u32[]{:S(2)}) copy-start(bf16[64,512]{1,0:T(8,128)(2,1)} %get-tuple-element.373.own_ref) | copy-start | bytes 196612 | tf_op jit(solution)/shard_map/while
  50.5 22.1 %copy-start.6 = (bf16[1,4608]{1,0:T(2,128)(2,1)S(1)}, bf16[1,4608]{1,0:T(2,128)(2,1)}, u32[]{:S(2)}) copy-start(bf16[1,4608]{1,0:T(2,128)(2,1)} %get-tuple-element.388.gain_ref) | copy-start | bytes 27652 | tf_op jit(solution)/shard_map/while
  55.8 16.0 %all-to-all-start.1 = ((bf16[8,8,4608]{2,1,0:T(8,128)(2,1)}), bf16[8,8,4608]{2,1,0:T(8,128)(2,1)S(1)}, u32[]{:S(2)}, u32[]{:S(2)}) async-start(bf16[8,8,4608]{2,1,0:T(8,128)(2,1)} %attention.4), calls=%async_computation.1 | async-start | bytes 1179648 | tf_op jit(solution)/shard_map/while/body/eval_jaxpr/all_to_all | solution.py:24
  74.4 5.3 collective-permute-start.1
  80.6 15.2 %all-to-all-start = ((bf16[8,8,4608]{2,1,0:T(8,128)(2,1)}), bf16[8,8,4608]{2,1,0:T(8,128)(2,1)S(1)}, u32[]{:S(2)}, u32[]{:S(2)}) async-start(bf16[8,8,4608]{2,1,0:T(8,128)(2,1)} %broadcast_in_dim.59), calls=%async_computation | async-start | bytes 1179648 | tf_op jit(solution)/shard_map/while/body/eval_jaxpr/all_to_all | solution.py:24
  95.8 0.8 copy-start.1
  101.2 6.1 %collective-permute-start = (bf16[64,512]{1,0:T(8,128)(2,1)}, bf16[64,512]{1,0:T(8,128)(2,1)S(1)}, u32[]{:S(2)}, u32[]{:S(2)}) collective-permute-start(bf16[64,512]{1,0:T(8,128)(2,1)} %get-tuple-element.373.own_ref), channel_id=1, source_target_pairs={{0,8},{8,0},{1,9},{9,1},{2,10},{10,2},{3,11},{11,3},{4,12},{12,4},... | collective-permute-start | bytes 196616 | tf_op jit(solution)/shard_map/while/body/eval_jaxpr/ppermute | solution.py:251
  107.2 9.4 %copy-start.2 = (bf16[64,512]{1,0:T(8,128)(2,1)S(1)}, bf16[64,512]{1,0:T(8,128)(2,1)}, u32[]{:S(2)}) copy-start(bf16[64,512]{1,0:T(8,128)(2,1)} %get-tuple-element.373.own_ref) | copy-start | bytes 196612 | tf_op jit(solution)/shard_map/while
  107.2 22.1 %copy-start.6 = (bf16[1,4608]{1,0:T(2,128)(2,1)S(1)}, bf16[1,4608]{1,0:T(2,128)(2,1)}, u32[]{:S(2)}) copy-start(bf16[1,4608]{1,0:T(2,128)(2,1)} %get-tuple-element.388.gain_ref) | copy-start | bytes 27652 | tf_op jit(solution)/shard_map/while
  112.5 16.0 %all-to-all-start.1 = ((bf16[8,8,4608]{2,1,0:T(8,128)(2,1)}), bf16[8,8,4608]{2,1,0:T(8,128)(2,1)S(1)}, u32[]{:S(2)}, u32[]{:S(2)}) async-start(bf16[8,8,4608]{2,1,0:T(8,128)(2,1)} %attention.4), calls=%async_computation.1 | async-start | bytes 1179648 | tf_op jit(solution)/shard_map/while/body/eval_jaxpr/all_to_all | solution.py:24
  131.2 5.5 collective-permute-start.1
  137.6 15.7 %all-to-all-start = ((bf16[8,8,4608]{2,1,0:T(8,128)(2,1)}), bf16[8,8,4608]{2,1,0:T(8,128)(2,1)S(1)}, u32[]{:S(2)}, u32[]{:S(2)}) async-start(bf16[8,8,4608]{2,1,0:T(8,128)(2,1)} %broadcast_in_dim.59), calls=%async_computation | async-start | bytes 1179648 | tf_op jit(solution)/shard_map/while/body/eval_jaxpr/all_to_all | solution.py:24
  153.3 0.8 copy-start.1
  158.6 5.6 %collective-permute-start = (bf16[64,512]{1,0:T(8,128)(2,1)}, bf16[64,512]{1,0:T(8,128)(2,1)S(1)}, u32[]{:S(2)}, u32[]{:S(2)}) collective-permute-start(bf16[64,512]{1,0:T(8,128)(2,1)} %get-tuple-element.373.own_ref), channel_id=1, source_target_pairs={{0,8},{8,0},{1,9},{9,1},{2,10},{10,2},{3,11},{11,3},{4,12},{12,4},... | collective-permute-start | bytes 196616 | tf_op jit(solution)/shard_map/while/body/eval_jaxpr/ppermute | solution.py:251
  164.2 9.4 %copy-start.2 = (bf16[64,512]{1,0:T(8,128)(2,1)S(1)}, bf16[64,512]{1,0:T(8,128)(2,1)}, u32[]{:S(2)}) copy-start(bf16[64,512]{1,0:T(8,128)(2,1)} %get-tuple-element.373.own_ref) | copy-start | bytes 196612 | tf_op jit(solution)/shard_map/while
  164.2 22.1 %copy-start.6 = (bf16[1,4608]{1,0:T(2,128)(2,1)S(1)}, bf16[1,4608]{1,0:T(2,128)(2,1)}, u32[]{:S(2)}) copy-start(bf16[1,4608]{1,0:T(2,128)(2,1)} %get-tuple-element.388.gain_ref) | copy-start | bytes 27652 | tf_op jit(solution)/shard_map/while
  169.5 16.0 %all-to-all-start.1 = ((bf16[8,8,4608]{2,1,0:T(8,128)(2,1)}), bf16[8,8,4608]{2,1,0:T(8,128)(2,1)S(1)}, u32[]{:S(2)}, u32[]{:S(2)}) async-start(bf16[8,8,4608]{2,1,0:T(8,128)(2,1)} %attention.4), calls=%async_computation.1 | async-start | bytes 1179648 | tf_op jit(solution)/shard_map/while/body/eval_jaxpr/all_to_all | solution.py:24
  188.2 6.2 %collective-permute-start.1 = (bf16[8,4608]{1,0:T(8,128)(2,1)}, bf16[8,4608]{1,0:T(8,128)(2,1)S(1)}, u32[]{:S(2)}, u32[]{:S(2)}) collective-permute-start(bf16[8,4608]{1,0:T(8,128)(2,1)} %combine.4), channel_id=1, source_target_pairs={{0,16},{16,32},{32,48},{48,64},{64,80},{80,96},{96,112},{1,17},{17... | collective-permute-start | bytes 221192 | tf_op jit(solution)/shard_map/while/body/eval_jaxpr/ppermute | solution.py:259
  195.2 15.8 %all-to-all-start = ((bf16[8,8,4608]{2,1,0:T(8,128)(2,1)}), bf16[8,8,4608]{2,1,0:T(8,128)(2,1)S(1)}, u32[]{:S(2)}, u32[]{:S(2)}) async-start(bf16[8,8,4608]{2,1,0:T(8,128)(2,1)} %broadcast_in_dim.59), calls=%async_computation | async-start | bytes 1179648 | tf_op jit(solution)/shard_map/while/body/eval_jaxpr/all_to_all | solution.py:24
  211.0 0.8 copy-start.1
  216.4 5.5 %collective-permute-start = (bf16[64,512]{1,0:T(8,128)(2,1)}, bf16[64,512]{1,0:T(8,128)(2,1)S(1)}, u32[]{:S(2)}, u32[]{:S(2)}) collective-permute-start(bf16[64,512]{1,0:T(8,128)(2,1)} %get-tuple-element.373.own_ref), channel_id=1, source_target_pairs={{0,8},{8,0},{1,9},{9,1},{2,10},{10,2},{3,11},{11,3},{4,12},{12,4},... | collective-permute-start | bytes 196616 | tf_op jit(solution)/shard_map/while/body/eval_jaxpr/ppermute | solution.py:251
  221.8 9.4 %copy-start.2 = (bf16[64,512]{1,0:T(8,128)(2,1)S(1)}, bf16[64,512]{1,0:T(8,128)(2,1)}, u32[]{:S(2)}) copy-start(bf16[64,512]{1,0:T(8,128)(2,1)} %get-tuple-element.373.own_ref) | copy-start | bytes 196612 | tf_op jit(solution)/shard_map/while
  221.9 22.1 %copy-start.6 = (bf16[1,4608]{1,0:T(2,128)(2,1)S(1)}, bf16[1,4608]{1,0:T(2,128)(2,1)}, u32[]{:S(2)}) copy-start(bf16[1,4608]{1,0:T(2,128)(2,1)} %get-tuple-element.388.gain_ref) | copy-start | bytes 27652 | tf_op jit(solution)/shard_map/while
  227.1 16.0 %all-to-all-start.1 = ((bf16[8,8,4608]{2,1,0:T(8,128)(2,1)}), bf16[8,8,4608]{2,1,0:T(8,128)(2,1)S(1)}, u32[]{:S(2)}, u32[]{:S(2)}) async-start(bf16[8,8,4608]{2,1,0:T(8,128)(2,1)} %attention.4), calls=%async_computation.1 | async-start | bytes 1179648 | tf_op jit(solution)/shard_map/while/body/eval_jaxpr/all_to_all | solution.py:24
  245.8 6.2 %collective-permute-start.1 = (bf16[8,4608]{1,0:T(8,128)(2,1)}, bf16[8,4608]{1,0:T(8,128)(2,1)S(1)}, u32[]{:S(2)}, u32[]{:S(2)}) collective-permute-start(bf16[8,4608]{1,0:T(8,128)(2,1)} %combine.4), channel_id=1, source_target_pairs={{0,16},{16,32},{32,48},{48,64},{64,80},{80,96},{96,112},{1,17},{17... | collective-permute-start | bytes 221192 | tf_op jit(solution)/shard_map/while/body/eval_jaxpr/ppermute | solution.py:259
  252.9 15.8 %all-to-all-start = ((bf16[8,8,4608]{2,1,0:T(8,128)(2,1)}), bf16[8,8,4608]{2,1,0:T(8,128)(2,1)S(1)}, u32[]{:S(2)}, u32[]{:S(2)}) async-start(bf16[8,8,4608]{2,1,0:T(8,128)(2,1)} %broadcast_in_dim.59), calls=%async_computation | async-start | bytes 1179648 | tf_op jit(solution)/shard_map/while/body/eval_jaxpr/all_to_all | solution.py:24
  268.7 0.8 copy-start.1
  274.0 5.5 %collective-permute-start = (bf16[64,512]{1,0:T(8,128)(2,1)}, bf16[64,512]{1,0:T(8,128)(2,1)S(1)}, u32[]{:S(2)}, u32[]{:S(2)}) collective-permute-start(bf16[64,512]{1,0:T(8,128)(2,1)} %get-tuple-element.373.own_ref), channel_id=1, source_target_pairs={{0,8},{8,0},{1,9},{9,1},{2,10},{10,2},{3,11},{11,3},{4,12},{12,4},... | collective-permute-start | bytes 196616 | tf_op jit(solution)/shard_map/while/body/eval_jaxpr/ppermute | solution.py:251
  279.5 9.4 %copy-start.2 = (bf16[64,512]{1,0:T(8,128)(2,1)S(1)}, bf16[64,512]{1,0:T(8,128)(2,1)}, u32[]{:S(2)}) copy-start(bf16[64,512]{1,0:T(8,128)(2,1)} %get-tuple-element.373.own_ref) | copy-start | bytes 196612 | tf_op jit(solution)/shard_map/while
  279.5 22.1 %copy-start.6 = (bf16[1,4608]{1,0:T(2,128)(2,1)S(1)}, bf16[1,4608]{1,0:T(2,128)(2,1)}, u32[]{:S(2)}) copy-start(bf16[1,4608]{1,0:T(2,128)(2,1)} %get-tuple-element.388.gain_ref) | copy-start | bytes 27652 | tf_op jit(solution)/shard_map/while
  284.8 16.0 %all-to-all-start.1 = ((bf16[8,8,4608]{2,1,0:T(8,128)(2,1)}), bf16[8,8,4608]{2,1,0:T(8,128)(2,1)S(1)}, u32[]{:S(2)}, u32[]{:S(2)}) async-start(bf16[8,8,4608]{2,1,0:T(8,128)(2,1)} %attention.4), calls=%async_computation.1 | async-start | bytes 1179648 | tf_op jit(solution)/shard_map/while/body/eval_jaxpr/all_to_all | solution.py:24
  303.5 6.2 %collective-permute-start.1 = (bf16[8,4608]{1,0:T(8,128)(2,1)}, bf16[8,4608]{1,0:T(8,128)(2,1)S(1)}, u32[]{:S(2)}, u32[]{:S(2)}) collective-permute-start(bf16[8,4608]{1,0:T(8,128)(2,1)} %combine.4), channel_id=1, source_target_pairs={{0,16},{16,32},{32,48},{48,64},{64,80},{80,96},{96,112},{1,17},{17... | collective-permute-start | bytes 221192 | tf_op jit(solution)/shard_map/while/body/eval_jaxpr/ppermute | solution.py:259
  310.6 15.8 %all-to-all-start = ((bf16[8,8,4608]{2,1,0:T(8,128)(2,1)}), bf16[8,8,4608]{2,1,0:T(8,128)(2,1)S(1)}, u32[]{:S(2)}, u32[]{:S(2)}) async-start(bf16[8,8,4608]{2,1,0:T(8,128)(2,1)} %broadcast_in_dim.59), calls=%async_computation | async-start | bytes 1179648 | tf_op jit(solution)/shard_map/while/body/eval_jaxpr/all_to_all | solution.py:24
  326.4 0.8 copy-start.1
  331.7 5.5 %collective-permute-start = (bf16[64,512]{1,0:T(8,128)(2,1)}, bf16[64,512]{1,0:T(8,128)(2,1)S(1)}, u32[]{:S(2)}, u32[]{:S(2)}) collective-permute-start(bf16[64,512]{1,0:T(8,128)(2,1)} %get-tuple-element.373.own_ref), channel_id=1, source_target_pairs={{0,8},{8,0},{1,9},{9,1},{2,10},{10,2},{3,11},{11,3},{4,12},{12,4},... | collective-permute-start | bytes 196616 | tf_op jit(solution)/shard_map/while/body/eval_jaxpr/ppermute | solution.py:251
  337.2 9.4 %copy-start.2 = (bf16[64,512]{1,0:T(8,128)(2,1)S(1)}, bf16[64,512]{1,0:T(8,128)(2,1)}, u32[]{:S(2)}) copy-start(bf16[64,512]{1,0:T(8,128)(2,1)} %get-tuple-element.373.own_ref) | copy-start | bytes 196612 | tf_op jit(solution)/shard_map/while
  337.2 22.1 %copy-start.6 = (bf16[1,4608]{1,0:T(2,128)(2,1)S(1)}, bf16[1,4608]{1,0:T(2,128)(2,1)}, u32[]{:S(2)}) copy-start(bf16[1,4608]{1,0:T(2,128)(2,1)} %get-tuple-element.388.gain_ref) | copy-start | bytes 27652 | tf_op jit(solution)/shard_map/while
  342.5 16.0 %all-to-all-start.1 = ((bf16[8,8,4608]{2,1,0:T(8,128)(2,1)}), bf16[8,8,4608]{2,1,0:T(8,128)(2,1)S(1)}, u32[]{:S(2)}, u32[]{:S(2)}) async-start(bf16[8,8,4608]{2,1,0:T(8,128)(2,1)} %attention.4), calls=%async_computation.1 | async-start | bytes 1179648 | tf_op jit(solution)/shard_map/while/body/eval_jaxpr/all_to_all | solution.py:24
  361.2 6.2 %collective-permute-start.1 = (bf16[8,4608]{1,0:T(8,128)(2,1)}, bf16[8,4608]{1,0:T(8,128)(2,1)S(1)}, u32[]{:S(2)}, u32[]{:S(2)}) collective-permute-start(bf16[8,4608]{1,0:T(8,128)(2,1)} %combine.4), channel_id=1, source_target_pairs={{0,16},{16,32},{32,48},{48,64},{64,80},{80,96},{96,112},{1,17},{17... | collective-permute-start | bytes 221192 | tf_op jit(solution)/shard_map/while/body/eval_jaxpr/ppermute | solution.py:259
  368.3 15.8 %all-to-all-start = ((bf16[8,8,4608]{2,1,0:T(8,128)(2,1)}), bf16[8,8,4608]{2,1,0:T(8,128)(2,1)S(1)}, u32[]{:S(2)}, u32[]{:S(2)}) async-start(bf16[8,8,4608]{2,1,0:T(8,128)(2,1)} %broadcast_in_dim.59), calls=%async_computation | async-start | bytes 1179648 | tf_op jit(solution)/shard_map/while/body/eval_jaxpr/all_to_all | solution.py:24
  384.0 0.8 copy-start.1
  389.4 5.5 %collective-permute-start = (bf16[64,512]{1,0:T(8,128)(2,1)}, bf16[64,512]{1,0:T(8,128)(2,1)S(1)}, u32[]{:S(2)}, u32[]{:S(2)}) collective-permute-start(bf16[64,512]{1,0:T(8,128)(2,1)} %get-tuple-element.373.own_ref), channel_id=1, source_target_pairs={{0,8},{8,0},{1,9},{9,1},{2,10},{10,2},{3,11},{11,3},{4,12},{12,4},... | collective-permute-start | bytes 196616 | tf_op jit(solution)/shard_map/while/body/eval_jaxpr/ppermute | solution.py:251
  394.9 9.4 %copy-start.2 = (bf16[64,512]{1,0:T(8,128)(2,1)S(1)}, bf16[64,512]{1,0:T(8,128)(2,1)}, u32[]{:S(2)}) copy-start(bf16[64,512]{1,0:T(8,128)(2,1)} %get-tuple-element.373.own_ref) | copy-start | bytes 196612 | tf_op jit(solution)/shard_map/while
  394.9 22.1 %copy-start.6 = (bf16[1,4608]{1,0:T(2,128)(2,1)S(1)}, bf16[1,4608]{1,0:T(2,128)(2,1)}, u32[]{:S(2)}) copy-start(bf16[1,4608]{1,0:T(2,128)(2,1)} %get-tuple-element.388.gain_ref) | copy-start | bytes 27652 | tf_op jit(solution)/shard_map/while
  400.2 16.0 %all-to-all-start.1 = ((bf16[8,8,4608]{2,1,0:T(8,128)(2,1)}), bf16[8,8,4608]{2,1,0:T(8,128)(2,1)S(1)}, u32[]{:S(2)}, u32[]{:S(2)}) async-start(bf16[8,8,4608]{2,1,0:T(8,128)(2,1)} %attention.4), calls=%async_computation.1 | async-start | bytes 1179648 | tf_op jit(solution)/shard_map/while/body/eval_jaxpr/all_to_all | solution.py:24
  418.9 6.2 %collective-permute-start.1 = (bf16[8,4608]{1,0:T(8,128)(2,1)}, bf16[8,4608]{1,0:T(8,128)(2,1)S(1)}, u32[]{:S(2)}, u32[]{:S(2)}) collective-permute-start(bf16[8,4608]{1,0:T(8,128)(2,1)} %combine.4), channel_id=1, source_target_pairs={{0,16},{16,32},{32,48},{48,64},{64,80},{80,96},{96,112},{1,17},{17... | collective-permute-start | bytes 221192 | tf_op jit(solution)/shard_map/while/body/eval_jaxpr/ppermute | solution.py:259
  425.9 15.8 %all-to-all-start = ((bf16[8,8,4608]{2,1,0:T(8,128)(2,1)}), bf16[8,8,4608]{2,1,0:T(8,128)(2,1)S(1)}, u32[]{:S(2)}, u32[]{:S(2)}) async-start(bf16[8,8,4608]{2,1,0:T(8,128)(2,1)} %broadcast_in_dim.59), calls=%async_computation | async-start | bytes 1179648 | tf_op jit(solution)/shard_map/while/body/eval_jaxpr/all_to_all | solution.py:24
  441.7 0.8 copy-start.1
  447.0 5.5 %collective-permute-start = (bf16[64,512]{1,0:T(8,128)(2,1)}, bf16[64,512]{1,0:T(8,128)(2,1)S(1)}, u32[]{:S(2)}, u32[]{:S(2)}) collective-permute-start(bf16[64,512]{1,0:T(8,128)(2,1)} %get-tuple-element.373.own_ref), channel_id=1, source_target_pairs={{0,8},{8,0},{1,9},{9,1},{2,10},{10,2},{3,11},{11,3},{4,12},{12,4},... | collective-permute-start | bytes 196616 | tf_op jit(solution)/shard_map/while/body/eval_jaxpr/ppermute | solution.py:251
  452.5 9.4 %copy-start.2 = (bf16[64,512]{1,0:T(8,128)(2,1)S(1)}, bf16[64,512]{1,0:T(8,128)(2,1)}, u32[]{:S(2)}) copy-start(bf16[64,512]{1,0:T(8,128)(2,1)} %get-tuple-element.373.own_ref) | copy-start | bytes 196612 | tf_op jit(solution)/shard_map/while
  452.5 22.1 %copy-start.6 = (bf16[1,4608]{1,0:T(2,128)(2,1)S(1)}, bf16[1,4608]{1,0:T(2,128)(2,1)}, u32[]{:S(2)}) copy-start(bf16[1,4608]{1,0:T(2,128)(2,1)} %get-tuple-element.388.gain_ref) | copy-start | bytes 27652 | tf_op jit(solution)/shard_map/while
  457.8 16.0 %all-to-all-start.1 = ((bf16[8,8,4608]{2,1,0:T(8,128)(2,1)}), bf16[8,8,4608]{2,1,0:T(8,128)(2,1)S(1)}, u32[]{:S(2)}, u32[]{:S(2)}) async-start(bf16[8,8,4608]{2,1,0:T(8,128)(2,1)} %attention.4), calls=%async_computation.1 | async-start | bytes 1179648 | tf_op jit(solution)/shard_map/while/body/eval_jaxpr/all_to_all | solution.py:24
  476.5 6.2 %collective-permute-start.1 = (bf16[8,4608]{1,0:T(8,128)(2,1)}, bf16[8,4608]{1,0:T(8,128)(2,1)S(1)}, u32[]{:S(2)}, u32[]{:S(2)}) collective-permute-start(bf16[8,4608]{1,0:T(8,128)(2,1)} %combine.4), channel_id=1, source_target_pairs={{0,16},{16,32},{32,48},{48,64},{64,80},{80,96},{96,112},{1,17},{17... | collective-permute-start | bytes 221192 | tf_op jit(solution)/shard_map/while/body/eval_jaxpr/ppermute | solution.py:259
  483.6 15.8 %all-to-all-start.3 = ((bf16[8,8,4608]{2,1,0:T(8,128)(2,1)}), bf16[8,8,4608]{2,1,0:T(8,128)(2,1)S(1)}, u32[]{:S(2)}, u32[]{:S(2)}) async-start(bf16[8,8,4608]{2,1,0:T(8,128)(2,1)} %broadcast_in_dim.53), calls=%async_computation.3 | async-start | bytes 1179648 | tf_op jit(solution)/shard_map/all_to_all | solution.py:24
  499.4 0.8 copy-start.5
  504.7 5.5 %collective-permute-start.2 = (bf16[64,512]{1,0:T(8,128)(2,1)}, bf16[64,512]{1,0:T(8,128)(2,1)S(1)}, u32[]{:S(2)}, u32[]{:S(2)}) collective-permute-start(bf16[64,512]{1,0:T(8,128)(2,1)} %get-tuple-element.164.own_ref), channel_id=1, source_target_pairs={{0,8},{8,0},{1,9},{9,1},{2,10},{10,2},{3,11},{11,3},{4,12},{12,4},... | collective-permute-start | bytes 196616 | tf_op jit(solution)/shard_map/ppermute | solution.py:251
  510.2 22.1 %copy-start.7 = (bf16[1,4608]{1,0:T(2,128)(2,1)S(1)}, bf16[1,4608]{1,0:T(2,128)(2,1)}, u32[]{:S(2)}) copy-start(bf16[1,4608]{1,0:T(2,128)(2,1)} %get-tuple-element.412) | copy-start | bytes 27652
  510.2 29.1 %copy-start.9 = (s32[4]{0:T(128)S(1)}, s32[4]{0:T(128)}, u32[]{:S(2)}) copy-start(s32[4]{0:T(128)} %param.11) | copy-start | bytes 52
  515.5 16.0 %all-to-all-start.4 = ((bf16[8,8,4608]{2,1,0:T(8,128)(2,1)}), bf16[8,8,4608]{2,1,0:T(8,128)(2,1)S(1)}, u32[]{:S(2)}, u32[]{:S(2)}) async-start(bf16[8,8,4608]{2,1,0:T(8,128)(2,1)} %attention.3), calls=%async_computation.4 | async-start | bytes 1179648 | tf_op jit(solution)/shard_map/all_to_all | solution.py:24
  536.0 10.4 %all-to-all-start.5 = ((bf16[8,2,8,576]{3,2,1,0:T(8,128)(2,1)}), bf16[8,2,8,576]{3,2,1,0:T(8,128)(2,1)S(1)}, u32[]{:S(2)}, u32[]{:S(2)}) async-start(bf16[8,2,8,576]{3,2,1,0:T(8,128)(2,1)} %copy.34), calls=%async_computation.5 | async-start | bytes 327680 | tf_op jit(solution)/shard_map/all_to_all | solution.py:24
  (18 other events, 12.8 us)

commit v3 on v2

v3 whole, which is shorter than its diff:
```python
import jax
import jax.numpy as jnp
from jax import lax
from jax.experimental import pallas as pl
from jax.experimental.pallas import tpu as pltpu
from jax.sharding import PartitionSpec as P

HEAD_DIM = 128
CHUNKS = 2

softcap_limit = 50.0
query_scale = 144.0 ** (-0.5)
epsilon = 1e-06
rotary_base = 10000.0
f32 = jnp.float32
bf16 = jnp.bfloat16

VMEM = pl.BlockSpec(memory_space=pltpu.VMEM)
SMEM = pl.BlockSpec(memory_space=pltpu.SMEM)
MIB = 1024 * 1024


def limit(mib):
    return pltpu.CompilerParams(vmem_limit_bytes=mib * MIB)


def exchange(pieces, axes):
    return lax.all_to_all(pieces, axes, split_axis=0, concat_axis=0, tiled=True)


def rope(u, cos_full, sin_full):
    return u * cos_full + pltpu.roll(u, HEAD_DIM // 2, 1) * sin_full


def key_value_kernel(place_ref, x_ref, gain_ref, cos_ref, sin_ref, wk_ref, wv_ref,
                     kv_ref, normed_ref):
    rows, width = normed_ref.shape
    kv_width = wk_ref.shape[2]
    x = x_ref[...].astype(f32).reshape(rows, width)
    scaling = lax.rsqrt(jnp.sum(x * x, axis=1, keepdims=True) / width + epsilon)
    normed_ref[...] = (x * scaling * gain_ref[...].astype(f32)).astype(bf16)
    slot = place_ref[0]
    cos_full, sin_full = cos_ref[slot], sin_ref[slot]
    keys = jnp.dot(normed_ref[...], wk_ref[0], preferred_element_type=f32)
    for head in range(kv_width // HEAD_DIM):
        at = slice(head * HEAD_DIM, (head + 1) * HEAD_DIM)
        kv_ref[:, at] = rope(keys[:, at], cos_full, sin_full).astype(bf16)
    values = jnp.dot(normed_ref[...], wv_ref[0], preferred_element_type=f32)
    kv_ref[:, kv_width:] = values.astype(bf16)


def query_kernel(place_ref, normed_ref, cos_ref, sin_ref, wq_ref, q_ref):
    q_width = q_ref.shape[1]
    slot = place_ref[0]
    cos_full, sin_full = cos_ref[slot], sin_ref[slot]
    queries = jnp.dot(normed_ref[...], wq_ref[0], preferred_element_type=f32)
    for head in range(q_width // HEAD_DIM):
        at = slice(head * HEAD_DIM, (head + 1) * HEAD_DIM)
        q_ref[:, at] = (rope(queries[:, at], cos_full, sin_full) * query_scale).astype(bf16)


def attention_kernel(place_ref, q_ref, own_ref, other_ref, past_own_ref, past_other_ref, wo_ref,
                     out_ref, attended_ref):
    rows, q_width = q_ref.shape
    kv_width = own_ref.shape[1] // 2
    kv_heads = kv_width // HEAD_DIM
    group = q_width // kv_width
    has_past = place_ref[0] > 0
    is_later = place_ref[1] > 0
    sources = (own_ref, other_ref, past_own_ref, past_other_ref)
    keys_seen = len(sources) * rows
    row = lax.broadcasted_iota(jnp.int32, (group * rows, keys_seen), 0) % rows
    col = lax.broadcasted_iota(jnp.int32, (group * rows, keys_seen), 1)
    other_to = jnp.where(is_later, 2 * rows, rows)
    past_to = jnp.where(has_past, keys_seen, 2 * rows)
    allowed = (
        ((col < rows) & (col <= row))
        | ((col >= rows) & (col < other_to))
        | ((col >= 2 * rows) & (col < past_to))
    )
    for head in range(kv_heads):
        at = slice(head * HEAD_DIM, (head + 1) * HEAD_DIM)
        value_at = slice(kv_width + head * HEAD_DIM, kv_width + (head + 1) * HEAD_DIM)
        keys = jnp.concatenate([s[:, at] for s in sources], axis=0)
        values = jnp.concatenate([s[:, value_at] for s in sources], axis=0)
        first = head * group * HEAD_DIM
        queries = jnp.concatenate(
            [q_ref[:, first + g * HEAD_DIM:first + (g + 1) * HEAD_DIM] for g in range(group)], axis=0
        )
        scores = lax.dot_general(
            queries, keys, (((1,), (1,)), ((), ())), preferred_element_type=f32
        )
        capped = softcap_limit * jnp.tanh(scores / softcap_limit)
        weight = jnp.where(allowed, jnp.exp(capped), f32(0.0))
        totals = jnp.sum(weight, axis=1, keepdims=True)
        numerator = jnp.dot(weight.astype(bf16), values, preferred_element_type=f32)
        attended = (numerator / totals).astype(bf16)
        for g in range(group):
            attended_ref[:, first + g * HEAD_DIM:first + (g + 1) * HEAD_DIM] = attended[
                g * rows:(g + 1) * rows
            ]
    terms = jnp.dot(attended_ref[...], wo_ref[0], preferred_element_type=f32)
    out_ref[...] = terms.reshape(out_ref.shape).astype(bf16)


def combine_kernel(arrived_ref, held_ref, gain_ref, out_ref):
    width = out_ref.shape[1]
    projected = jnp.sum(arrived_ref[...].astype(f32), axis=0)
    mean = jnp.sum(projected * projected, axis=1, keepdims=True) / width
    scaled = projected * lax.rsqrt(mean + epsilon) * gain_ref[...].astype(f32)
    out_ref[...] = (held_ref[...].astype(f32) + scaled).astype(bf16)


def pick_kernel(order_ref, place_ref, blocks_ref, out_ref):
    peers, _, _ = out_ref.shape
    spans, rows, _ = blocks_ref.shape
    own = rows // peers
    core = place_ref[1]
    block_of = []
    for chunk in range(CHUNKS):
        span = core + chunk * (spans // CHUNKS)
        at = jnp.int32(0)
        for j in range(1, spans):
            at = jnp.where(order_ref[j] == span, j, at)
        block_of.append(at)
    first = blocks_ref[block_of[0]]
    second = blocks_ref[block_of[1]].astype(f32)
    for t in range(peers):
        out_ref[t, :rows] = first
        out_ref[t, rows:] = second[t * own:(t + 1) * own].astype(bf16)


def gather_kernel(place_ref, arrived_ref, full_ref, held_ref, next_ref):
    peers, own, width = full_ref.shape
    rows = peers * own
    part = width // peers
    for t in range(peers):
        at = slice(t * part, (t + 1) * part)
        piece = arrived_ref[t].astype(f32)
        full_ref[:, :, at] = piece[:rows].reshape(peers, own, part).astype(bf16)
        next_ref[:, at] = piece[rows:].astype(bf16)
    held_ref[...] = full_ref[place_ref[2]]


def split_kernel(place_ref, *refs):
    *made_refs, out_ref = refs
    cores, peers, chunks, own, part = out_ref.shape
    section = place_ref[3]
    for chunk in range(chunks):
        rows = made_refs[chunk][...].astype(f32)
        for i in range(1, len(made_refs) - chunks + 1):
            rows = jnp.where(section == i, made_refs[i + chunk][...].astype(f32), rows)
        for t in range(peers):
            piece = rows[:, t * part:(t + 1) * part].astype(bf16)
            for core in range(cores):
                out_ref[core, t, chunk] = piece


def order_kernel(order_ref, place_ref, arrived_ref, out_ref):
    cores, peers, chunks, own, part = arrived_ref.shape
    rows = peers * own
    blocks = out_ref.shape[0] // rows
    for j in range(blocks):
        span = order_ref[place_ref[1] * blocks + j]
        chunk, core = lax.div(span, jnp.int32(cores)), lax.rem(span, jnp.int32(cores))
        piece = arrived_ref[core, :, chunk].astype(f32).reshape(rows, part)
        out_ref[j * rows:(j + 1) * rows] = piece.astype(bf16)


def body(states_in, span_order, pre_gain, w_query, w_key, w_value, w_out, post_gain):
    _, row_count, part = states_in.shape
    width = pre_gain.shape[1]
    q_width = w_query.shape[2]
    kv_width = w_key.shape[2]
    sections = lax.axis_size("section")
    tensors = lax.axis_size("tensor")
    seqs = lax.axis_size("seq")
    section_rank = lax.axis_index("section")
    seq_rank = lax.axis_index("seq")
    tensor_rank = lax.axis_index("tensor")
    spans = span_order.shape[0]
    rows = row_count // CHUNKS
    own = rows // tensors
    chunk_len = rows * seqs

    key_value = pl.pallas_call(
        key_value_kernel,
        out_shape=(
            jax.ShapeDtypeStruct((rows, 2 * kv_width), bf16),
            jax.ShapeDtypeStruct((rows, width), bf16),
        ),
        in_specs=[SMEM] + [VMEM] * 6,
        out_specs=(VMEM, VMEM),
        compiler_params=limit(10),
        name="key_value",
    )
    query = pl.pallas_call(
        query_kernel,
        out_shape=jax.ShapeDtypeStruct((rows, q_width), bf16),
        in_specs=[SMEM] + [VMEM] * 4,
        out_specs=VMEM,
        compiler_params=limit(8),
        name="query",
    )
    attention = pl.pallas_call(
        attention_kernel,
        out_shape=jax.ShapeDtypeStruct((tensors, own, width), bf16),
        in_specs=[SMEM] + [VMEM] * 6,
        out_specs=VMEM,
        scratch_shapes=[pltpu.VMEM((rows, q_width), bf16)],
        compiler_params=limit(10),
        name="attention",
    )
    combine = pl.pallas_call(
        combine_kernel,
        out_shape=jax.ShapeDtypeStruct((own, width), bf16),
        in_specs=[VMEM, VMEM, VMEM],
        out_specs=VMEM,
        compiler_params=limit(4),
        name="combine",
    )

    tick_total = sections + CHUNKS - 1
    slots = jnp.clip(jnp.arange(tick_total, dtype=jnp.int32) - section_rank, 0, CHUNKS - 1)
    ranks = jnp.stack([seq_rank, tensor_rank, section_rank]).astype(jnp.int32)
    place_all = jnp.concatenate(
        [slots[:, None], jnp.broadcast_to(ranks[None], (tick_total, 3))], axis=1
    )
    places = (
        jnp.arange(CHUNKS, dtype=jnp.int32)[:, None] * chunk_len
        + seq_rank * rows
        + jnp.arange(rows, dtype=jnp.int32)[None, :]
    )
    half = HEAD_DIM // 2
    inverse = rotary_base ** (-(jnp.arange(half, dtype=f32) * 2.0 / HEAD_DIM))
    angles = places.astype(f32)[..., None] * inverse
    cos_part, sin_part = jnp.cos(angles), jnp.sin(angles)
    cos_full = jnp.concatenate([cos_part, cos_part], axis=-1)
    sin_full = jnp.concatenate([-sin_part, sin_part], axis=-1)

    blocks = lax.all_gather(states_in[0], "seq", axis=0).reshape(spans, rows, part)
    pieces = pl.pallas_call(
        pick_kernel,
        out_shape=jax.ShapeDtypeStruct((tensors, rows + own, part), bf16),
        in_specs=[SMEM, SMEM, VMEM],
        out_specs=VMEM,
        compiler_params=limit(4),
        name="pick",
    )(span_order, place_all[0], blocks)
    pieces, place_all, cos_full, sin_full = lax.optimization_barrier(
        (pieces, place_all, cos_full, sin_full)
    )
    full, held, following = pl.pallas_call(
        gather_kernel,
        out_shape=(
            jax.ShapeDtypeStruct((tensors, own, width), bf16),
            jax.ShapeDtypeStruct((own, width), bf16),
            jax.ShapeDtypeStruct((own, width), bf16),
        ),
        in_specs=[SMEM, VMEM],
        out_specs=(VMEM, VMEM, VMEM),
        compiler_params=limit(6),
        name="gather",
    )(place_all[0], exchange(pieces, "tensor"))

    past = (jnp.zeros((rows, 2 * kv_width), bf16),) * 2
    made = []
    for tick in range(tick_total):
        place = place_all[tick]
        kv_own, normed = key_value(place, full, pre_gain, cos_full, sin_full, w_key, w_value)
        kv_other = lax.ppermute(kv_own, "seq", [(0, 1), (1, 0)])
        queries = query(place, normed, cos_full, sin_full, w_query)
        terms = attention(place, queries, kv_own, kv_other, *past, w_out)
        past = (kv_own, kv_other)
        made.append(combine(exchange(terms, "tensor"), held, post_gain))
        if tick + 1 < tick_total:
            busy = [i for i in range(sections - 1) if 0 <= tick - i < CHUNKS]
            held = lax.ppermute(made[-1], "section", [(i, i + 1) for i in busy])
            if tick + 1 < CHUNKS:
                held = jnp.where(section_rank == 0, following, held)
            full = exchange(jnp.broadcast_to(held[None], (tensors, own, width)), "tensor")

    made = lax.optimization_barrier(tuple(made))
    pieces = pl.pallas_call(
        split_kernel,
        out_shape=jax.ShapeDtypeStruct((seqs, tensors, CHUNKS, own, part), bf16),
        in_specs=[SMEM] + [VMEM] * tick_total,
        out_specs=VMEM,
        compiler_params=limit(6),
        name="split",
    )(place_all[0], *made)
    pieces = exchange(pieces.reshape(seqs * tensors, CHUNKS, own, part), ("seq", "tensor"))
    out = pl.pallas_call(
        order_kernel,
        out_shape=jax.ShapeDtypeStruct((row_count, part), bf16),
        in_specs=[SMEM, SMEM, VMEM],
        out_specs=VMEM,
        compiler_params=limit(4),
        name="order",
    )(span_order, place_all[0], pieces.reshape(seqs, tensors, CHUNKS, own, part))
    return out[None, None]


def solution(mesh):
    in_specs = (
        P(None, "seq", "tensor"),
        P(),
        P("section", None),
        P("section", None, "tensor"),
        P("section", None, "tensor"),
        P("section", None, "tensor"),
        P("section", "tensor", None),
        P("section", None),
    )
    out_specs = P("section", None, "seq", "tensor")
    return jax.shard_map(body, mesh=mesh, in_specs=in_specs, out_specs=out_specs, check_vma=False)
```

time: 558 us -> 400 us (0.72); the launches traced: 551 us -> 399 us
  blocking collectives: 6.14 us -> 256 us
  waiting for transfers between devices: 235 us -> 45.4 us
  Pallas kernels: 140 us -> 51.4 us
  starting transfers between devices: 93.8 us -> 33.6 us
  local copies, waits for them, and re-layouts: 50.8 us -> 11.8 us
  loops' own time: 9.87 us -> 0 us
  between operations: 8.12 us -> 0.59 us
  other arithmetic: 7.88 us -> 0.66 us
    all_to_all x0 -> x18, blocking collectives: none -> 253 us  [exchange(): return lax.all_to_all(pieces, axes, split_axis=0, concat_axis=0, tiled=True)]
    all_to_all x20 -> x1, waiting for transfers between devices: 204 us -> 13.7 us  [exchange(): return lax.all_to_all(pieces, axes, split_axis=0, concat_axis=0, tiled=True)]
    pallas_call x36 -> x40, Pallas kernels: 140 us -> 51.4 us  [the longest x9 17.1 us: body(): terms = attention(place, queries, kv_own, kv_other, *past, w_out)]
    all_to_all x20 -> x1, starting transfers between devices: 73.6 us -> 6.43 us  [exchange(): return lax.all_to_all(pieces, axes, split_axis=0, concat_axis=0, tiled=True)]
    while x96 -> x0, local copies, waits for them, and re-layouts: 24.9 us -> none
    another operation x1 -> x0, loops' own time: 9.87 us -> none  [body(): lax.scan(tick, (first_rows[0], no_past, no_past), jnp.arange(tick_total -...]
    unnamed x10 -> x34, local copies, waits for them, and re-layouts: 2.27 us -> 9.92 us
    broadcast_in_dim x12 -> x10, local copies, waits for them, and re-layouts: 8.45 us -> 1.12 us  [the longest x1 0.79 us: body(): return out[None, None]]
  transfers between devices with their start and end apart: 37 -> 18, of which waited for: 28 -> 3; matrix products, arithmetic and copies ran while one was open for 5% -> 0% of each run, Pallas kernels for 7% -> 4%
where the time goes in v3:
time: 400 us; the launch traced here: 399 us
  blocking collectives  256 us (64%)
  Pallas kernels  51.4 us (13%)
  waiting for transfers between devices  45.4 us (11%)
  starting transfers between devices  33.6 us (8%)
  local copies, waits for them, and re-layouts  11.8 us (3%)
    all_to_all x18, blocking collectives, exchange(): return lax.all_to_all(pieces, axes, split_axis=0, concat_axis=0, tiled=True)  253 us
    ppermute x8, waiting for transfers between devices, body(): held = lax.ppermute(made[-1], 'section', [(i, i + 1) for i in busy])  31.6 us
    ppermute x9, starting transfers between devices, body(): kv_other = lax.ppermute(kv_own, 'seq', [(0, 1), (1, 0)])  20.6 us
    pallas_call x9, Pallas kernels, body(): terms = attention(place, queries, kv_own, kv_other, *past, w_out)  17.1 us
    pallas_call x9, Pallas kernels, body(): key_value(place, full, pre_gain, cos_full, sin_full, w_key, w_value)  15.8 us
    pallas_call x9, Pallas kernels, body(): queries = query(place, normed, cos_full, sin_full, w_query)  14 us
    all_to_all x1, waiting for transfers between devices, exchange(): return lax.all_to_all(pieces, axes, split_axis=0, concat_axis=0, tiled=True)  13.7 us
    unnamed x34, local copies, waits for them, and re-layouts  9.92 us
  transfers between devices with their start and end apart: 18, of which 3 were waited for; matrix products, arithmetic and copies ran while one was open for 0% of the time, Pallas kernels for 4%

profile of v3, /device:TPU:57, one launch (start us, length us, event | category | flops | bytes accessed | tf_op | source)
XLA Modules:
  0.0 399.1 jit_solution(10628566229933595858)
XLA Ops:
  0.5 2.7 all_gather.3
  5.9 6.4 %all-to-all-start = ((bf16[8,72,576]{2,1,0:T(8,128)(2,1)}), bf16[8,72,576]{2,1,0:T(8,128)(2,1)S(1)}, u32[]{:S(2)}, u32[]{:S(2)}) async-start(bf16[8,72,576]{2,1,0:T(8,128)(2,1)} %copy-done.8), calls=%async_computation | async-start | bytes 1474560 | tf_op jit(solution)/shard_map/all_to_all | solution.py:28
  12.7 13.7 %all-to-all-done.arrived_ref = bf16[8,72,576]{2,1,0:T(8,128)(2,1)S(1)} async-done(((bf16[8,72,576]{2,1,0:T(8,128)(2,1)}), bf16[8,72,576]{2,1,0:T(8,128)(2,1)S(1)}, u32[]{:S(2)}, u32[]{:S(2)}) %all-to-all-start) | async-done | bytes 663584 | tf_op jit(solution)/shard_map/all_to_all | solution.py:28
  27.1 2.0 copy-done.5
  29.2 1.8 key_value.9
  31.8 1.6 query.9.q_ref
  33.4 1.9 attention.9
  35.3 14.7 %all_to_all.95.arrived_ref = bf16[8,8,4608]{2,1,0:T(8,128)(2,1)S(1)} all-to-all(bf16[8,8,4608]{2,1,0:T(8,128)(2,1)S(1)} %attention.9), channel_id=1, replica_groups=mesh['section'=8,'seq'=2,'tensor'=8] {'tensor'}, dimensions={0} | all-to-all | bytes 1179648 | tf_op jit(solution)/shard_map/all_to_all | solution.py:28
  50.9 13.4 %all_to_all.96.x_ref = bf16[8,8,4608]{2,1,0:T(8,128)(2,1)S(1)} all-to-all(bf16[8,8,4608]{2,1,0:T(8,128)(2,1)S(1)} %broadcast_in_dim.24), channel_id=1, replica_groups=mesh['section'=8,'seq'=2,'tensor'=8] {'tensor'}, dimensions={0} | all-to-all | bytes 1179648 | tf_op jit(solution)/shard_map/all_to_all | solution.py:28
  64.4 1.7 copy-done.6
  66.0 1.8 key_value.10
  67.8 2.4 collective-permute-start.2
  70.2 2.3 copy-done.1
  72.5 1.6 query.10.q_ref
  74.1 2.3 copy-done.3
  76.4 1.9 attention.10
  78.3 14.7 %all_to_all.97.arrived_ref = bf16[8,8,4608]{2,1,0:T(8,128)(2,1)S(1)} all-to-all(bf16[8,8,4608]{2,1,0:T(8,128)(2,1)S(1)} %attention.10), channel_id=1, replica_groups=mesh['section'=8,'seq'=2,'tensor'=8] {'tensor'}, dimensions={0} | all-to-all | bytes 1179648 | tf_op jit(solution)/shard_map/all_to_all | solution.py:28
  94.0 13.7 %all_to_all.98.x_ref = bf16[8,8,4608]{2,1,0:T(8,128)(2,1)S(1)} all-to-all(bf16[8,8,4608]{2,1,0:T(8,128)(2,1)S(1)} %broadcast_in_dim.25), channel_id=1, replica_groups=mesh['section'=8,'seq'=2,'tensor'=8] {'tensor'}, dimensions={0} | all-to-all | bytes 1179648 | tf_op jit(solution)/shard_map/all_to_all | solution.py:28
  107.7 1.8 key_value.11
  109.4 2.4 collective-permute-start.4
  111.8 1.6 query.11.q_ref
  113.4 1.9 attention.11
  115.3 14.7 %all_to_all.99.arrived_ref = bf16[8,8,4608]{2,1,0:T(8,128)(2,1)S(1)} all-to-all(bf16[8,8,4608]{2,1,0:T(8,128)(2,1)S(1)} %attention.11), channel_id=1, replica_groups=mesh['section'=8,'seq'=2,'tensor'=8] {'tensor'}, dimensions={0} | all-to-all | bytes 1179648 | tf_op jit(solution)/shard_map/all_to_all | solution.py:28
  131.0 13.4 %all_to_all.100.x_ref = bf16[8,8,4608]{2,1,0:T(8,128)(2,1)S(1)} all-to-all(bf16[8,8,4608]{2,1,0:T(8,128)(2,1)S(1)} %broadcast_in_dim.26), channel_id=1, replica_groups=mesh['section'=8,'seq'=2,'tensor'=8] {'tensor'}, dimensions={0} | all-to-all | bytes 1179648 | tf_op jit(solution)/shard_map/all_to_all | solution.py:28
  144.4 1.8 key_value.12
  146.1 2.6 collective-permute-start.6
  148.7 1.6 query.12.q_ref
  150.3 1.9 attention.12
  152.2 14.7 %all_to_all.101.arrived_ref = bf16[8,8,4608]{2,1,0:T(8,128)(2,1)S(1)} all-to-all(bf16[8,8,4608]{2,1,0:T(8,128)(2,1)S(1)} %attention.12), channel_id=1, replica_groups=mesh['section'=8,'seq'=2,'tensor'=8] {'tensor'}, dimensions={0} | all-to-all | bytes 1179648 | tf_op jit(solution)/shard_map/all_to_all | solution.py:28
  167.8 13.4 %all_to_all.102.x_ref = bf16[8,8,4608]{2,1,0:T(8,128)(2,1)S(1)} all-to-all(bf16[8,8,4608]{2,1,0:T(8,128)(2,1)S(1)} %broadcast_in_dim.27), channel_id=1, replica_groups=mesh['section'=8,'seq'=2,'tensor'=8] {'tensor'}, dimensions={0} | all-to-all | bytes 1179648 | tf_op jit(solution)/shard_map/all_to_all | solution.py:28
  181.2 1.8 key_value.13
  183.0 2.4 collective-permute-start.8
  185.4 1.6 query.13.q_ref
  187.0 1.9 attention.13
  188.9 14.7 %all_to_all.103.arrived_ref = bf16[8,8,4608]{2,1,0:T(8,128)(2,1)S(1)} all-to-all(bf16[8,8,4608]{2,1,0:T(8,128)(2,1)S(1)} %attention.13), channel_id=1, replica_groups=mesh['section'=8,'seq'=2,'tensor'=8] {'tensor'}, dimensions={0} | all-to-all | bytes 1179648 | tf_op jit(solution)/shard_map/all_to_all | solution.py:28
  204.5 13.4 %all_to_all.104.x_ref = bf16[8,8,4608]{2,1,0:T(8,128)(2,1)S(1)} all-to-all(bf16[8,8,4608]{2,1,0:T(8,128)(2,1)S(1)} %broadcast_in_dim.28), channel_id=1, replica_groups=mesh['section'=8,'seq'=2,'tensor'=8] {'tensor'}, dimensions={0} | all-to-all | bytes 1179648 | tf_op jit(solution)/shard_map/all_to_all | solution.py:28
  217.9 1.8 key_value.14
  219.7 2.4 collective-permute-start.10
  222.1 1.6 query.14.q_ref
  223.6 1.9 attention.14
  225.5 14.7 %all_to_all.105.arrived_ref = bf16[8,8,4608]{2,1,0:T(8,128)(2,1)S(1)} all-to-all(bf16[8,8,4608]{2,1,0:T(8,128)(2,1)S(1)} %attention.14), channel_id=1, replica_groups=mesh['section'=8,'seq'=2,'tensor'=8] {'tensor'}, dimensions={0} | all-to-all | bytes 1179648 | tf_op jit(solution)/shard_map/all_to_all | solution.py:28
  241.2 13.4 %all_to_all.106.x_ref = bf16[8,8,4608]{2,1,0:T(8,128)(2,1)S(1)} all-to-all(bf16[8,8,4608]{2,1,0:T(8,128)(2,1)S(1)} %broadcast_in_dim.29), channel_id=1, replica_groups=mesh['section'=8,'seq'=2,'tensor'=8] {'tensor'}, dimensions={0} | all-to-all | bytes 1179648 | tf_op jit(solution)/shard_map/all_to_all | solution.py:28
  254.6 1.8 key_value.15
  256.3 2.4 collective-permute-start.12
  258.7 1.6 query.15.q_ref
  260.3 1.9 attention.15
  262.2 14.7 %all_to_all.107.arrived_ref = bf16[8,8,4608]{2,1,0:T(8,128)(2,1)S(1)} all-to-all(bf16[8,8,4608]{2,1,0:T(8,128)(2,1)S(1)} %attention.15), channel_id=1, replica_groups=mesh['section'=8,'seq'=2,'tensor'=8] {'tensor'}, dimensions={0} | all-to-all | bytes 1179648 | tf_op jit(solution)/shard_map/all_to_all | solution.py:28
  277.1 1.3 collective-permute-start.13
  278.4 27.5 %collective-permute-done.13.held_ref = bf16[8,4608]{1,0:T(8,128)(2,1)S(1)} collective-permute-done((bf16[8,4608]{1,0:T(8,128)(2,1)S(1)}, bf16[8,4608]{1,0:T(8,128)(2,1)S(1)}, u32[]{:S(2)}, u32[]{:S(2)}) %collective-permute-start.13) | collective-permute-done | bytes 73760 | tf_op jit(solution)/shard_map/ppermute | solution.py:278
  306.0 13.4 %all_to_all.108.x_ref = bf16[8,8,4608]{2,1,0:T(8,128)(2,1)S(1)} all-to-all(bf16[8,8,4608]{2,1,0:T(8,128)(2,1)S(1)} %broadcast_in_dim.30), channel_id=1, replica_groups=mesh['section'=8,'seq'=2,'tensor'=8] {'tensor'}, dimensions={0} | all-to-all | bytes 1179648 | tf_op jit(solution)/shard_map/all_to_all | solution.py:28
  319.4 1.8 key_value.16
  321.1 2.7 collective-permute-start.14
  323.8 1.6 query.16.q_ref
  325.4 1.9 attention.16
  327.3 14.7 %all_to_all.109.arrived_ref = bf16[8,8,4608]{2,1,0:T(8,128)(2,1)S(1)} all-to-all(bf16[8,8,4608]{2,1,0:T(8,128)(2,1)S(1)} %attention.16), channel_id=1, replica_groups=mesh['section'=8,'seq'=2,'tensor'=8] {'tensor'}, dimensions={0} | all-to-all | bytes 1179648 | tf_op jit(solution)/shard_map/all_to_all | solution.py:28
  342.2 1.3 collective-permute-start.15
  343.5 4.1 %collective-permute-done.15.held_ref = bf16[8,4608]{1,0:T(8,128)(2,1)S(1)} collective-permute-done((bf16[8,4608]{1,0:T(8,128)(2,1)S(1)}, bf16[8,4608]{1,0:T(8,128)(2,1)S(1)}, u32[]{:S(2)}, u32[]{:S(2)}) %collective-permute-start.15) | collective-permute-done | bytes 73760 | tf_op jit(solution)/shard_map/ppermute | solution.py:278
  347.6 13.3 %all_to_all.110.x_ref = bf16[8,8,4608]{2,1,0:T(8,128)(2,1)S(1)} all-to-all(bf16[8,8,4608]{2,1,0:T(8,128)(2,1)S(1)} %broadcast_in_dim.31), channel_id=1, replica_groups=mesh['section'=8,'seq'=2,'tensor'=8] {'tensor'}, dimensions={0} | all-to-all | bytes 1179648 | tf_op jit(solution)/shard_map/all_to_all | solution.py:28
  360.9 1.8 key_value.17
  362.7 2.5 collective-permute-start.16
  365.2 1.6 query.17.q_ref
  366.7 1.9 attention.17
  368.6 14.7 %all_to_all.111.arrived_ref = bf16[8,8,4608]{2,1,0:T(8,128)(2,1)S(1)} all-to-all(bf16[8,8,4608]{2,1,0:T(8,128)(2,1)S(1)} %attention.17), channel_id=1, replica_groups=mesh['section'=8,'seq'=2,'tensor'=8] {'tensor'}, dimensions={0} | all-to-all | bytes 1179648 | tf_op jit(solution)/shard_map/all_to_all | solution.py:28
  384.3 13.5 %all_to_all.112 = bf16[16,2,8,576]{3,2,1,0:T(8,128)(2,1)S(1)} all-to-all(bf16[16,2,8,576]{3,2,1,0:T(8,128)(2,1)S(1)} %bitcast.12), channel_id=1, replica_groups=mesh['section'=8,'seq'=2,'tensor'=8] {'seq','tensor'}, dimensions={0} | all-to-all | bytes 589824 | tf_op jit(solution)/shard_map/all_to_all | solution.py:28
  (90 shorter events, 13.6 us)
Async XLA Ops:
  0.0 27.1 %copy-start.4 = (bf16[1,4608,256]{2,1,0:T(8,128)(2,1)S(1)}, bf16[1,4608,256]{2,1,0:T(8,128)(2,1)}, u32[]{:S(2)}) copy-start(bf16[1,4608,256]{2,1,0:T(8,128)(2,1)} %wk_ref.17) | copy-start | bytes 7077892
  0.0 27.1 %copy-start.9 = (bf16[1,4608]{1,0:T(2,128)(2,1)S(1)}, bf16[1,4608]{1,0:T(2,128)(2,1)}, u32[]{:S(2)}) copy-start(bf16[1,4608]{1,0:T(2,128)(2,1)} %gain_ref.34) | copy-start | bytes 27652
  3.8 0.7 copy-start.11
  5.0 0.9 copy-start.8
  5.9 20.5 %all-to-all-start = ((bf16[8,72,576]{2,1,0:T(8,128)(2,1)}), bf16[8,72,576]{2,1,0:T(8,128)(2,1)S(1)}, u32[]{:S(2)}, u32[]{:S(2)}) async-start(bf16[8,72,576]{2,1,0:T(8,128)(2,1)} %copy-done.8), calls=%async_computation | async-start | bytes 1474560 | tf_op jit(solution)/shard_map/all_to_all | solution.py:28
  26.4 5.4 %copy-start = (bf16[1,4608,512]{2,1,0:T(8,128)(2,1)S(1)}, bf16[1,4608,512]{2,1,0:T(8,128)(2,1)}, u32[]{:S(2)}) copy-start(bf16[1,4608,512]{2,1,0:T(8,128)(2,1)} %wq_ref.17) | copy-start | bytes 14155780
  27.1 2.0 copy-start.5
  29.2 4.2 %copy-start.2 = (bf16[1,512,4608]{2,1,0:T(8,128)(2,1)S(1)}, bf16[1,512,4608]{2,1,0:T(8,128)(2,1)}, u32[]{:S(2)}) copy-start(bf16[1,512,4608]{2,1,0:T(8,128)(2,1)} %wo_ref.17) | copy-start | bytes 14155780
  30.9 2.4 collective-permute-start
  33.3 16.6 %copy-start.10 = (bf16[1,4608]{1,0:T(2,128)(2,1)S(1)}, bf16[1,4608]{1,0:T(2,128)(2,1)}, u32[]{:S(2)}) copy-start(bf16[1,4608]{1,0:T(2,128)(2,1)} %gain_ref.35) | copy-start | bytes 27652
  50.2 0.7 collective-permute-start.1
  64.4 1.7 copy-start.6
  67.8 6.3 %collective-permute-start.2 = (bf16[64,512]{1,0:T(8,128)(2,1)S(1)}, bf16[64,512]{1,0:T(8,128)(2,1)S(1)}, u32[]{:S(2)}, u32[]{:S(2)}) collective-permute-start(bf16[64,512]{1,0:T(8,128)(2,1)S(1)} %get-tuple-element.49.own_ref.past_own_ref), channel_id=1, source_target_pairs={{0,8},{8,0},{1,9},{9,1},{2,10},{10,2},{3,11},{11,3},{4,12},{12,4},... | collective-permute-start | bytes 196616 | tf_op jit(solution)/shard_map/ppermute | solution.py:271
  70.2 2.3 copy-start.1
  74.1 2.3 copy-start.3
  76.4 31.2 %copy-start.7 = (bf16[1,4608,256]{2,1,0:T(8,128)(2,1)S(1)}, bf16[1,4608,256]{2,1,0:T(8,128)(2,1)}, u32[]{:S(2)}) copy-start(bf16[1,4608,256]{2,1,0:T(8,128)(2,1)} %wv_ref.17) | copy-start | bytes 7077892
  76.4 35.4 %slice-start = ((s8[4718592]{0:T(1024)(128)(4,1)}), s8[4194304]{0:T(1024)(128)(4,1)S(1)}, s32[]{:S(2)}) async-start(s8[4718592]{0:T(1024)(128)(4,1)} %bitcast.7), calls=%async_computation.19 | async-start | bytes 8388608
  93.0 18.8 %slice-start.1 = ((s8[4718592]{0:T(1024)(128)(4,1)}), s8[524288]{0:T(1024)(128)(4,1)S(1)}, s32[]{:S(2)}) async-start(s8[4718592]{0:T(1024)(128)(4,1)} %bitcast.7), calls=%async_computation.20 | async-start | bytes 1048576
  93.2 0.7 collective-permute-start.3
  94.0 19.4 %slice-start.2 = ((s8[4718592]{0:T(1024)(128)(4,1)}), s8[4194304]{0:T(1024)(128)(4,1)S(1)}, s32[]{:S(2)}) async-start(s8[4718592]{0:T(1024)(128)(4,1)} %bitcast.9), calls=%async_computation.21 | async-start | bytes 8388608
  107.7 5.8 %slice-start.3 = ((s8[4718592]{0:T(1024)(128)(4,1)}), s8[524288]{0:T(1024)(128)(4,1)S(1)}, s32[]{:S(2)}) async-start(s8[4718592]{0:T(1024)(128)(4,1)} %bitcast.9), calls=%async_computation.22 | async-start | bytes 1048576
  109.4 4.0 collective-permute-start.4
  130.2 0.7 collective-permute-start.5
  146.1 4.2 %collective-permute-start.6 = (bf16[64,512]{1,0:T(8,128)(2,1)S(1)}, bf16[64,512]{1,0:T(8,128)(2,1)S(1)}, u32[]{:S(2)}, u32[]{:S(2)}) collective-permute-start(bf16[64,512]{1,0:T(8,128)(2,1)S(1)} %get-tuple-element.53.own_ref.past_own_ref), channel_id=1, source_target_pairs={{0,8},{8,0},{1,9},{9,1},{2,10},{10,2},{3,11},{11,3},{4,12},{12,4},... | collective-permute-start | bytes 196616 | tf_op jit(solution)/shard_map/ppermute | solution.py:271
  167.1 0.7 collective-permute-start.7
  183.0 4.0 collective-permute-start.8
  203.8 0.7 collective-permute-start.9
  219.7 4.0 collective-permute-start.10
  240.4 0.7 collective-permute-start.11
  256.3 4.0 collective-permute-start.12
  277.1 28.8 %collective-permute-start.13 = (bf16[8,4608]{1,0:T(8,128)(2,1)S(1)}, bf16[8,4608]{1,0:T(8,128)(2,1)S(1)}, u32[]{:S(2)}, u32[]{:S(2)}) collective-permute-start(bf16[8,4608]{1,0:T(8,128)(2,1)S(1)} %combine.15.refs_6_), channel_id=1, source_target_pairs={{80,96},{96,112},{81,97},{97,113},{82,98},{98,114},{83,99},{99,115... | collective-permute-start | bytes 221192 | tf_op jit(solution)/shard_map/ppermute | solution.py:278
  321.1 4.2 %collective-permute-start.14 = (bf16[64,512]{1,0:T(8,128)(2,1)S(1)}, bf16[64,512]{1,0:T(8,128)(2,1)S(1)}, u32[]{:S(2)}, u32[]{:S(2)}) collective-permute-start(bf16[64,512]{1,0:T(8,128)(2,1)S(1)} %get-tuple-element.61.own_ref.past_own_ref), channel_id=1, source_target_pairs={{0,8},{8,0},{1,9},{9,1},{2,10},{10,2},{3,11},{11,3},{4,12},{12,4},... | collective-permute-start | bytes 196616 | tf_op jit(solution)/shard_map/ppermute | solution.py:271
  342.2 5.4 %collective-permute-start.15 = (bf16[8,4608]{1,0:T(8,128)(2,1)S(1)}, bf16[8,4608]{1,0:T(8,128)(2,1)S(1)}, u32[]{:S(2)}, u32[]{:S(2)}) collective-permute-start(bf16[8,4608]{1,0:T(8,128)(2,1)S(1)} %combine.16.refs_7_), channel_id=1, source_target_pairs={{96,112},{97,113},{98,114},{99,115},{100,116},{101,117},{102,118},... | collective-permute-start | bytes 221192 | tf_op jit(solution)/shard_map/ppermute | solution.py:278
  362.7 4.1 %collective-permute-start.16 = (bf16[64,512]{1,0:T(8,128)(2,1)S(1)}, bf16[64,512]{1,0:T(8,128)(2,1)S(1)}, u32[]{:S(2)}, u32[]{:S(2)}) collective-permute-start(bf16[64,512]{1,0:T(8,128)(2,1)S(1)} %get-tuple-element.63.own_ref), channel_id=1, source_target_pairs={{0,8},{8,0},{1,9},{9,1},{2,10},{10,2},{3,11},{11,3},{4,12},{12,4},... | collective-permute-start | bytes 196616 | tf_op jit(solution)/shard_map/ppermute | solution.py:271
  366.7 31.1 %copy-start.12 = (s32[4]{0:T(128)S(1)}, s32[4]{0:T(128)}, u32[]{:S(2)}) copy-start(s32[4]{0:T(128)} %order_ref.3) | copy-start | bytes 52

commit v4 on v3

v4 whole, which is shorter than its diff:
```python
import functools

import jax
import jax.numpy as jnp
from jax import lax
from jax.experimental import pallas as pl
from jax.experimental.pallas import tpu as pltpu
from jax.sharding import PartitionSpec as P

HEAD_DIM = 128
CHUNKS = 2
LANES = 128
OWN = 8

softcap_limit = 50.0
query_scale = 144.0 ** (-0.5)
epsilon = 1e-06
rotary_base = 10000.0
f32 = jnp.float32
bf16 = jnp.bfloat16

VMEM = pl.BlockSpec(memory_space=pltpu.VMEM)

FIRST_FROM, SECOND_FROM, GIVEN_AS = 0, 4, 8
SECTION, CORE, OWNER, FACTS = 16, 17, 18, 24
MIB = 1024 * 1024


def limit(mib):
    return pltpu.CompilerParams(vmem_limit_bytes=mib * MIB)


def exchange(pieces, axes):
    return lax.all_to_all(pieces, axes, split_axis=0, concat_axis=0, tiled=True)


def tiles(ref_shape):
    return range(ref_shape[-2] // OWN)


def tile(c):
    return slice(c * OWN, (c + 1) * OWN)


def fact(facts_ref, row):
    return facts_ref[row:row + 1, :]


def one_of(facts_ref, first, choices):
    picked = choices[0]
    for i in range(1, len(choices)):
        picked = jnp.where(facts_ref[first + i:first + i + 1, :1] > 0, choices[i], picked)
    return picked


def is_later(facts_ref, tick):
    return fact(facts_ref, SECTION) <= tick - 1


def lanes(c):
    return slice(c * LANES, (c + 1) * LANES)


def rope(u, cos_full, sin_full):
    return u * cos_full + pltpu.roll(u, HEAD_DIM // 2, 1) * sin_full


def key_value_kernel(tick, facts_ref, x_ref, gain_ref, cos_ref, sin_ref, wk_ref, wv_ref,
                     kv_ref, normed_ref):
    rows, width = normed_ref.shape
    kv_width = wk_ref.shape[2]
    squares = jnp.zeros((rows, LANES), f32)
    for c in tiles(x_ref.shape):
        x = x_ref[:, tile(c)].astype(f32).reshape(rows, LANES)
        squares += x * x
    scaling = lax.rsqrt(jnp.sum(squares, axis=1, keepdims=True) / width + epsilon)
    for c in tiles(x_ref.shape):
        x = x_ref[:, tile(c)].astype(f32).reshape(rows, LANES)
        normed_ref[:, lanes(c)] = (x * scaling * gain_ref[:, lanes(c)].astype(f32)).astype(bf16)
    later = is_later(facts_ref, tick)
    cos_full = jnp.where(later, cos_ref[1], cos_ref[0])
    sin_full = jnp.where(later, sin_ref[1], sin_ref[0])
    keys = jnp.dot(normed_ref[...], wk_ref[0], preferred_element_type=f32)
    for head in range(kv_width // HEAD_DIM):
        at = slice(head * HEAD_DIM, (head + 1) * HEAD_DIM)
        kv_ref[:, at] = rope(keys[:, at], cos_full, sin_full).astype(bf16)
    values = jnp.dot(normed_ref[...], wv_ref[0], preferred_element_type=f32)
    kv_ref[:, kv_width:] = values.astype(bf16)


def query_kernel(tick, facts_ref, normed_ref, cos_ref, sin_ref, wq_ref, q_ref):
    q_width = q_ref.shape[1]
    later = is_later(facts_ref, tick)
    cos_full = jnp.where(later, cos_ref[1], cos_ref[0])
    sin_full = jnp.where(later, sin_ref[1], sin_ref[0])
    queries = jnp.dot(normed_ref[...], wq_ref[0], preferred_element_type=f32)
    for head in range(q_width // HEAD_DIM):
        at = slice(head * HEAD_DIM, (head + 1) * HEAD_DIM)
        q_ref[:, at] = (rope(queries[:, at], cos_full, sin_full) * query_scale).astype(bf16)


def attention_kernel(tick, facts_ref, q_ref, own_ref, other_ref, past_own_ref, past_other_ref, wo_ref,
                     out_ref, attended_ref):
    rows, q_width = q_ref.shape
    kv_width = own_ref.shape[1] // 2
    kv_heads = kv_width // HEAD_DIM
    group = q_width // kv_width
    sources = (own_ref, other_ref, past_own_ref, past_other_ref)
    half = 2 * rows
    row = lax.broadcasted_iota(jnp.int32, (group * rows, half), 0) % rows
    col = lax.broadcasted_iota(jnp.int32, (group * rows, half), 1)
    after = jnp.broadcast_to(fact(facts_ref, CORE) > 0, (group * rows, half))
    has_past = jnp.broadcast_to(is_later(facts_ref, tick), (group * rows, half))
    now = ((col < rows) & (col <= row)) | ((col >= rows) & after)
    for head in range(kv_heads):
        at = slice(head * HEAD_DIM, (head + 1) * HEAD_DIM)
        value_at = slice(kv_width + head * HEAD_DIM, kv_width + (head + 1) * HEAD_DIM)
        keys = jnp.concatenate([s[:, at] for s in sources], axis=0)
        values = jnp.concatenate([s[:, value_at] for s in sources], axis=0)
        first = head * group * HEAD_DIM
        queries = jnp.concatenate(
            [q_ref[:, first + g * HEAD_DIM:first + (g + 1) * HEAD_DIM] for g in range(group)], axis=0
        )
        scores = lax.dot_general(
            queries, keys, (((1,), (1,)), ((), ())), preferred_element_type=f32
        )
        capped = softcap_limit * jnp.tanh(scores / softcap_limit)
        weight = jnp.exp(capped)
        weight = jnp.concatenate(
            [
                jnp.where(now, weight[:, :half], f32(0.0)),
                jnp.where(has_past, weight[:, half:], f32(0.0)),
            ],
            axis=1,
        )
        totals = jnp.sum(weight, axis=1, keepdims=True)
        numerator = jnp.dot(weight.astype(bf16), values, preferred_element_type=f32)
        attended = (numerator / totals).astype(bf16)
        for g in range(group):
            attended_ref[:, first + g * HEAD_DIM:first + (g + 1) * HEAD_DIM] = attended[
                g * rows:(g + 1) * rows
            ]
    terms = jnp.dot(attended_ref[...], wo_ref[0], preferred_element_type=f32)
    for c in tiles(out_ref.shape):
        out_ref[:, tile(c)] = terms[:, lanes(c)].reshape(-1, OWN, LANES).astype(bf16)


def combine_kernel(arrived_ref, held_ref, gain_ref, out_ref, sum_ref):
    width = gain_ref.shape[1]
    squares = jnp.zeros((OWN, LANES), f32)
    for c in tiles(out_ref.shape):
        projected = jnp.sum(arrived_ref[:, tile(c)].astype(f32), axis=0)
        sum_ref[tile(c)] = projected
        squares += projected * projected
    scaling = lax.rsqrt(jnp.sum(squares, axis=1, keepdims=True) / width + epsilon)
    for c in tiles(out_ref.shape):
        scaled = sum_ref[tile(c)] * scaling * gain_ref[:, lanes(c)].astype(f32)
        out_ref[tile(c)] = (held_ref[tile(c)].astype(f32) + scaled).astype(bf16)


def choose_kernel(facts_ref, moved_ref, following_ref, held_ref):
    is_first = fact(facts_ref, SECTION) < 1
    moved, following = moved_ref[...].astype(f32), following_ref[...].astype(f32)
    held_ref[...] = jnp.where(is_first, following, moved).astype(bf16)


def pick_kernel(facts_ref, blocks_ref, out_ref):
    peers = out_ref.shape[0]
    spans, rows, _ = blocks_ref.shape
    blocks = [blocks_ref[j].astype(f32) for j in range(spans)]
    first = one_of(facts_ref, FIRST_FROM, blocks).astype(bf16)
    second = one_of(facts_ref, SECOND_FROM, blocks)
    for t in range(peers):
        out_ref[t, :rows] = first
        out_ref[t, rows:] = second[t * OWN:(t + 1) * OWN].astype(bf16)


def gather_kernel(facts_ref, arrived_ref, full_ref, held_ref, next_ref, flat_ref):
    peers = full_ref.shape[0]
    rows = peers * OWN
    part = flat_ref.shape[1] // peers
    for t in range(peers):
        flat_ref[:, t * part:(t + 1) * part] = arrived_ref[t].astype(f32)
    owner = fact(facts_ref, OWNER)
    for c in tiles(next_ref.shape):
        blocks = flat_ref[:rows, lanes(c)].reshape(peers, OWN, LANES)
        full_ref[:, tile(c)] = blocks.astype(bf16)
        held = blocks[0]
        for t in range(1, peers):
            held = jnp.where(owner == t, blocks[t], held)
        held_ref[tile(c)] = held.astype(bf16)
        next_ref[tile(c)] = flat_ref[rows:, lanes(c)].astype(bf16)


def split_kernel(facts_ref, *refs):
    *made_refs, out_ref, flat_ref = refs
    cores, peers, chunks, _, part = out_ref.shape
    section = fact(facts_ref, SECTION)
    for chunk in range(chunks):
        rows = made_refs[chunk][...].astype(f32)
        for i in range(1, len(made_refs) - chunks + 1):
            rows = jnp.where(section == i, made_refs[i + chunk][...].astype(f32), rows)
        for c in tiles(rows.shape):
            flat_ref[:, lanes(c)] = rows[tile(c)]
        for t in range(peers):
            piece = flat_ref[:, t * part:(t + 1) * part].astype(bf16)
            for core in range(cores):
                out_ref[core, t, chunk] = piece


def order_kernel(facts_ref, arrived_ref, out_ref):
    cores, peers, chunks, _, part = arrived_ref.shape
    rows = peers * OWN
    spans = [
        arrived_ref[core, :, chunk].astype(f32).reshape(rows, part)
        for chunk in range(chunks)
        for core in range(cores)
    ]
    for j in range(out_ref.shape[0] // rows):
        piece = one_of(facts_ref, GIVEN_AS + j * len(spans), spans)
        out_ref[j * rows:(j + 1) * rows] = piece.astype(bf16)


def body(states_in, span_order, pre_gain, w_query, w_key, w_value, w_out, post_gain):
    _, row_count, part = states_in.shape
    width = pre_gain.shape[1]
    q_width = w_query.shape[2]
    kv_width = w_key.shape[2]
    sections = lax.axis_size("section")
    tensors = lax.axis_size("tensor")
    seqs = lax.axis_size("seq")
    section_rank = lax.axis_index("section")
    seq_rank = lax.axis_index("seq")
    tensor_rank = lax.axis_index("tensor")
    spans = span_order.shape[0]
    rows = row_count // CHUNKS
    own = rows // tensors
    assert own == OWN
    chunk_len = rows * seqs
    block = (own * width // LANES, LANES)

    key_value = lambda tick: pl.pallas_call(
        functools.partial(key_value_kernel, tick),
        out_shape=(
            jax.ShapeDtypeStruct((rows, 2 * kv_width), bf16),
            jax.ShapeDtypeStruct((rows, width), bf16),
        ),
        in_specs=[VMEM] * 7,
        out_specs=(VMEM, VMEM),
        compiler_params=limit(10),
        name="key_value",
    )
    query = lambda tick: pl.pallas_call(
        functools.partial(query_kernel, tick),
        out_shape=jax.ShapeDtypeStruct((rows, q_width), bf16),
        in_specs=[VMEM] * 5,
        out_specs=VMEM,
        compiler_params=limit(8),
        name="query",
    )
    attention = lambda tick: pl.pallas_call(
        functools.partial(attention_kernel, tick),
        out_shape=jax.ShapeDtypeStruct((tensors, *block), bf16),
        in_specs=[VMEM] * 7,
        out_specs=VMEM,
        scratch_shapes=[pltpu.VMEM((rows, q_width), bf16)],
        compiler_params=limit(10),
        name="attention",
    )
    combine = pl.pallas_call(
        combine_kernel,
        out_shape=jax.ShapeDtypeStruct(block, bf16),
        in_specs=[VMEM, VMEM, VMEM],
        out_specs=VMEM,
        scratch_shapes=[pltpu.VMEM(block, f32)],
        compiler_params=limit(4),
        name="combine",
    )

    tick_total = sections + CHUNKS - 1
    ids = jnp.arange(spans, dtype=jnp.int32)
    given = lax.dynamic_slice_in_dim(span_order, seq_rank * (spans // seqs), spans // seqs, 0)
    rows_of_facts = [span_order == chunk * seqs + seq_rank for chunk in range(CHUNKS)]
    rows_of_facts += [(given[:, None] == ids[None, :]).reshape(-1)]
    rows_of_facts += [jnp.stack([section_rank, seq_rank, tensor_rank])]
    facts = jnp.concatenate([r.astype(f32) for r in rows_of_facts])
    facts = jnp.pad(facts, (0, FACTS - facts.shape[0]))
    facts = jnp.broadcast_to(facts[:, None], (FACTS, LANES))
    places = (
        jnp.arange(CHUNKS, dtype=jnp.int32)[:, None] * chunk_len
        + seq_rank * rows
        + jnp.arange(rows, dtype=jnp.int32)[None, :]
    )
    half = HEAD_DIM // 2
    inverse = rotary_base ** (-(jnp.arange(half, dtype=f32) * 2.0 / HEAD_DIM))
    angles = places.astype(f32)[..., None] * inverse
    cos_part, sin_part = jnp.cos(angles), jnp.sin(angles)
    cos_full = jnp.concatenate([cos_part, cos_part], axis=-1)
    sin_full = jnp.concatenate([-sin_part, sin_part], axis=-1)

    blocks = lax.all_gather(states_in[0], "seq", axis=0).reshape(spans, rows, part)
    pieces = pl.pallas_call(
        pick_kernel,
        out_shape=jax.ShapeDtypeStruct((tensors, rows + own, part), bf16),
        in_specs=[VMEM, VMEM],
        out_specs=VMEM,
        compiler_params=limit(4),
        name="pick",
    )(facts, blocks)
    no_past = jnp.zeros((rows, 2 * kv_width), bf16)
    pieces, facts, cos_full, sin_full, no_past = lax.optimization_barrier(
        (pieces, facts, cos_full, sin_full, no_past)
    )
    full, held, following = pl.pallas_call(
        gather_kernel,
        out_shape=(
            jax.ShapeDtypeStruct((tensors, *block), bf16),
            jax.ShapeDtypeStruct(block, bf16),
            jax.ShapeDtypeStruct(block, bf16),
        ),
        in_specs=[VMEM, VMEM],
        out_specs=(VMEM, VMEM, VMEM),
        scratch_shapes=[pltpu.VMEM((rows + own, width), f32)],
        compiler_params=limit(6),
        name="gather",
    )(facts, exchange(pieces, "tensor"))

    past = (no_past, no_past)
    made = []
    for tick in range(tick_total):
        kv_own, normed = key_value(tick)(facts, full, pre_gain, cos_full, sin_full, w_key, w_value)
        kv_other = lax.ppermute(kv_own, "seq", [(0, 1), (1, 0)])
        queries = query(tick)(facts, normed, cos_full, sin_full, w_query)
        terms = attention(tick)(facts, queries, kv_own, kv_other, *past, w_out)
        past = (kv_own, kv_other)
        made.append(combine(exchange(terms, "tensor"), held, post_gain))
        if tick + 1 < tick_total:
            busy = [i for i in range(sections - 1) if 0 <= tick - i < CHUNKS]
            held = lax.ppermute(made[-1], "section", [(i, i + 1) for i in busy])
            if tick + 1 < CHUNKS:
                held = pl.pallas_call(
                    choose_kernel,
                    out_shape=jax.ShapeDtypeStruct(block, bf16),
                    in_specs=[VMEM] * 3,
                    out_specs=VMEM,
                    compiler_params=limit(2),
                    name="choose",
                )(facts, held, following)
            full = exchange(jnp.broadcast_to(held[None], (tensors, *block)), "tensor")

    made = lax.optimization_barrier(tuple(made))
    pieces = pl.pallas_call(
        split_kernel,
        out_shape=jax.ShapeDtypeStruct((seqs, tensors, CHUNKS, own, part), bf16),
        in_specs=[VMEM] * (tick_total + 1),
        out_specs=VMEM,
        scratch_shapes=[pltpu.VMEM((own, width), f32)],
        compiler_params=limit(6),
        name="split",
    )(facts, *made)
    pieces = exchange(pieces.reshape(seqs * tensors, CHUNKS, own, part), ("seq", "tensor"))
    out = pl.pallas_call(
        order_kernel,
        out_shape=jax.ShapeDtypeStruct((row_count, part), bf16),
        in_specs=[VMEM, VMEM],
        out_specs=VMEM,
        compiler_params=limit(4),
        name="order",
    )(facts, pieces.reshape(seqs, tensors, CHUNKS, own, part))
    return out[None, None]


def solution(mesh):
    in_specs = (
        P(None, "seq", "tensor"),
        P(),
        P("section", None),
        P("section", None, "tensor"),
        P("section", None, "tensor"),
        P("section", None, "tensor"),
        P("section", "tensor", None),
        P("section", None),
    )
    out_specs = P("section", None, "seq", "tensor")
    return jax.shard_map(body, mesh=mesh, in_specs=in_specs, out_specs=out_specs, check_vma=False)
```

time: 400 us -> 377 us (0.943)
  blocking collectives: 256 us -> 275 us
  Pallas kernels: 51.4 us -> 34.7 us
  waiting for transfers between devices: 45.4 us -> 31.6 us
  local copies, waits for them, and re-layouts: 11.8 us -> 5.24 us
  starting transfers between devices: 33.6 us -> 28.1 us
    all_to_all x18 -> x19, blocking collectives: 253 us -> 272 us  [exchange(): return lax.all_to_all(pieces, axes, split_axis=0, concat_axis=0, tiled=True)]
    pallas_call x28 -> x29, Pallas kernels: 47.6 us -> 32.4 us  [the longest x9 12.3 us: body(): terms = attention(tick)(facts, queries, kv_own, kv_other, *past, w_out)]
    all_to_all x1 -> x0, waiting for transfers between devices: 13.7 us -> none  [exchange(): return lax.all_to_all(pieces, axes, split_axis=0, concat_axis=0, tiled=True)]
    unnamed x34 -> x18, local copies, waits for them, and re-layouts: 9.92 us -> 2.57 us
    all_to_all x1 -> x0, starting transfers between devices: 6.43 us -> none  [exchange(): return lax.all_to_all(pieces, axes, split_axis=0, concat_axis=0, tiled=True)]
  transfers between devices with their start and end apart: 18 -> 17, of which waited for: 3 -> 2; matrix products, arithmetic and copies ran while one was open for 0% -> 0% of each run, Pallas kernels for 4% -> 2%
where the time goes in v4:
time: 377 us; the launch traced here: 376 us
  blocking collectives  275 us (73%)
  Pallas kernels  34.7 us (9%)
  waiting for transfers between devices  31.6 us (8%)
  starting transfers between devices  28.1 us (7%)
  local copies, waits for them, and re-layouts  5.24 us (1%)
    all_to_all x19, blocking collectives, exchange(): return lax.all_to_all(pieces, axes, split_axis=0, concat_axis=0, tiled=True)  272 us
    ppermute x8, waiting for transfers between devices, body(): held = lax.ppermute(made[-1], 'section', [(i, i + 1) for i in busy])  31.6 us
    ppermute x9, starting transfers between devices, body(): kv_other = lax.ppermute(kv_own, 'seq', [(0, 1), (1, 0)])  21.5 us
    pallas_call x9, Pallas kernels, body(): terms = attention(tick)(facts, queries, kv_own, kv_other, *past, w_out)  12.3 us
    pallas_call x9, Pallas kernels, body(): key_value(tick)(facts, full, pre_gain, cos_full, sin_full, w_key, w_value)  10.8 us
    pallas_call x9, Pallas kernels, body(): queries = query(tick)(facts, normed, cos_full, sin_full, w_query)  9.1 us
  transfers between devices with their start and end apart: 17, of which 2 were waited for; matrix products, arithmetic and copies ran while one was open for 0% of the time, Pallas kernels for 2%

profile of v4, /device:TPU:57, one launch (start us, length us, event | category | flops | bytes accessed | tf_op | source)
XLA Modules:
  0.0 376.3 jit_solution(12016260028615730237)
XLA Ops:
  0.0 0.9 dynamic_slice.3
  1.8 2.5 all_gather.3
  5.4 19.5 %all_to_all.95.arrived_ref = bf16[8,72,576]{2,1,0:T(8,128)(2,1)S(1)} all-to-all(bf16[8,72,576]{2,1,0:T(8,128)(2,1)S(1)} %pick.1), channel_id=1, replica_groups=mesh['section'=8,'seq'=2,'tensor'=8] {'tensor'}, dimensions={0} | all-to-all | bytes 1327104 | tf_op jit(solution)/shard_map/all_to_all | solution.py:34
  25.2 1.8 copy-done.2
  27.0 0.7 copy-done.4
  27.7 1.2 key_value.9
  28.9 1.7 collective-permute-start
  30.6 1.0 query.9.q_ref
  31.7 1.4 attention.9
  33.1 14.7 %all_to_all.96.arrived_ref = bf16[8,288,128]{2,1,0:T(8,128)(2,1)S(1)} all-to-all(bf16[8,288,128]{2,1,0:T(8,128)(2,1)S(1)} %attention.9), channel_id=1, replica_groups=mesh['section'=8,'seq'=2,'tensor'=8] {'tensor'}, dimensions={0} | all-to-all | bytes 1179648 | tf_op jit(solution)/shard_map/all_to_all | solution.py:34
  48.8 13.4 %all_to_all.97.x_ref = bf16[8,288,128]{2,1,0:T(8,128)(2,1)S(1)} all-to-all(bf16[8,288,128]{2,1,0:T(8,128)(2,1)S(1)} %broadcast_in_dim.24), channel_id=1, replica_groups=mesh['section'=8,'seq'=2,'tensor'=8] {'tensor'}, dimensions={0} | all-to-all | bytes 1179648 | tf_op jit(solution)/shard_map/all_to_all | solution.py:34
  62.2 1.2 key_value.10
  63.4 2.4 collective-permute-start.2
  65.8 1.0 query.10.q_ref
  66.8 1.4 attention.10
  68.2 14.7 %all_to_all.98.arrived_ref = bf16[8,288,128]{2,1,0:T(8,128)(2,1)S(1)} all-to-all(bf16[8,288,128]{2,1,0:T(8,128)(2,1)S(1)} %attention.10), channel_id=1, replica_groups=mesh['section'=8,'seq'=2,'tensor'=8] {'tensor'}, dimensions={0} | all-to-all | bytes 1179648 | tf_op jit(solution)/shard_map/all_to_all | solution.py:34
  83.8 13.4 %all_to_all.99.x_ref = bf16[8,288,128]{2,1,0:T(8,128)(2,1)S(1)} all-to-all(bf16[8,288,128]{2,1,0:T(8,128)(2,1)S(1)} %broadcast_in_dim.25), channel_id=1, replica_groups=mesh['section'=8,'seq'=2,'tensor'=8] {'tensor'}, dimensions={0} | all-to-all | bytes 1179648 | tf_op jit(solution)/shard_map/all_to_all | solution.py:34
  97.3 1.2 key_value.11
  98.5 2.4 collective-permute-start.4
  100.9 1.0 query.11.q_ref
  101.9 1.4 attention.11
  103.3 14.7 %all_to_all.100.arrived_ref = bf16[8,288,128]{2,1,0:T(8,128)(2,1)S(1)} all-to-all(bf16[8,288,128]{2,1,0:T(8,128)(2,1)S(1)} %attention.11), channel_id=1, replica_groups=mesh['section'=8,'seq'=2,'tensor'=8] {'tensor'}, dimensions={0} | all-to-all | bytes 1179648 | tf_op jit(solution)/shard_map/all_to_all | solution.py:34
  118.9 13.4 %all_to_all.101.x_ref = bf16[8,288,128]{2,1,0:T(8,128)(2,1)S(1)} all-to-all(bf16[8,288,128]{2,1,0:T(8,128)(2,1)S(1)} %broadcast_in_dim.26), channel_id=1, replica_groups=mesh['section'=8,'seq'=2,'tensor'=8] {'tensor'}, dimensions={0} | all-to-all | bytes 1179648 | tf_op jit(solution)/shard_map/all_to_all | solution.py:34
  132.3 1.2 key_value.12
  133.5 2.6 collective-permute-start.6
  136.1 1.0 query.12.q_ref
  137.1 1.4 attention.12
  138.5 14.7 %all_to_all.102.arrived_ref = bf16[8,288,128]{2,1,0:T(8,128)(2,1)S(1)} all-to-all(bf16[8,288,128]{2,1,0:T(8,128)(2,1)S(1)} %attention.12), channel_id=1, replica_groups=mesh['section'=8,'seq'=2,'tensor'=8] {'tensor'}, dimensions={0} | all-to-all | bytes 1179648 | tf_op jit(solution)/shard_map/all_to_all | solution.py:34
  154.1 13.4 %all_to_all.103.x_ref = bf16[8,288,128]{2,1,0:T(8,128)(2,1)S(1)} all-to-all(bf16[8,288,128]{2,1,0:T(8,128)(2,1)S(1)} %broadcast_in_dim.27), channel_id=1, replica_groups=mesh['section'=8,'seq'=2,'tensor'=8] {'tensor'}, dimensions={0} | all-to-all | bytes 1179648 | tf_op jit(solution)/shard_map/all_to_all | solution.py:34
  167.6 1.2 key_value.13
  168.8 2.4 collective-permute-start.8
  171.2 1.0 query.13.q_ref
  172.2 1.4 attention.13
  173.5 14.7 %all_to_all.104.arrived_ref = bf16[8,288,128]{2,1,0:T(8,128)(2,1)S(1)} all-to-all(bf16[8,288,128]{2,1,0:T(8,128)(2,1)S(1)} %attention.13), channel_id=1, replica_groups=mesh['section'=8,'seq'=2,'tensor'=8] {'tensor'}, dimensions={0} | all-to-all | bytes 1179648 | tf_op jit(solution)/shard_map/all_to_all | solution.py:34
  189.2 13.4 %all_to_all.105.x_ref = bf16[8,288,128]{2,1,0:T(8,128)(2,1)S(1)} all-to-all(bf16[8,288,128]{2,1,0:T(8,128)(2,1)S(1)} %broadcast_in_dim.28), channel_id=1, replica_groups=mesh['section'=8,'seq'=2,'tensor'=8] {'tensor'}, dimensions={0} | all-to-all | bytes 1179648 | tf_op jit(solution)/shard_map/all_to_all | solution.py:34
  202.6 1.2 key_value.14
  203.8 2.4 collective-permute-start.10
  206.2 1.0 query.14.q_ref
  207.2 1.4 attention.14
  208.6 14.7 %all_to_all.106.arrived_ref = bf16[8,288,128]{2,1,0:T(8,128)(2,1)S(1)} all-to-all(bf16[8,288,128]{2,1,0:T(8,128)(2,1)S(1)} %attention.14), channel_id=1, replica_groups=mesh['section'=8,'seq'=2,'tensor'=8] {'tensor'}, dimensions={0} | all-to-all | bytes 1179648 | tf_op jit(solution)/shard_map/all_to_all | solution.py:34
  224.2 13.4 %all_to_all.107.x_ref = bf16[8,288,128]{2,1,0:T(8,128)(2,1)S(1)} all-to-all(bf16[8,288,128]{2,1,0:T(8,128)(2,1)S(1)} %broadcast_in_dim.29), channel_id=1, replica_groups=mesh['section'=8,'seq'=2,'tensor'=8] {'tensor'}, dimensions={0} | all-to-all | bytes 1179648 | tf_op jit(solution)/shard_map/all_to_all | solution.py:34
  237.7 1.2 key_value.15
  238.9 2.4 collective-permute-start.12
  241.3 1.0 query.15.q_ref
  242.3 1.4 attention.15
  243.7 14.7 %all_to_all.108.arrived_ref = bf16[8,288,128]{2,1,0:T(8,128)(2,1)S(1)} all-to-all(bf16[8,288,128]{2,1,0:T(8,128)(2,1)S(1)} %attention.15), channel_id=1, replica_groups=mesh['section'=8,'seq'=2,'tensor'=8] {'tensor'}, dimensions={0} | all-to-all | bytes 1179648 | tf_op jit(solution)/shard_map/all_to_all | solution.py:34
  258.5 1.3 collective-permute-start.13
  259.8 27.5 %collective-permute-done.13.held_ref = bf16[288,128]{1,0:T(8,128)(2,1)S(1)} collective-permute-done((bf16[288,128]{1,0:T(8,128)(2,1)S(1)}, bf16[288,128]{1,0:T(8,128)(2,1)S(1)}, u32[]{:S(2)}, u32[]{:S(2)}) %collective-permute-start.13) | collective-permute-done | bytes 73760 | tf_op jit(solution)/shard_map/ppermute | solution.py:339
  287.5 13.4 %all_to_all.109.x_ref = bf16[8,288,128]{2,1,0:T(8,128)(2,1)S(1)} all-to-all(bf16[8,288,128]{2,1,0:T(8,128)(2,1)S(1)} %broadcast_in_dim.30), channel_id=1, replica_groups=mesh['section'=8,'seq'=2,'tensor'=8] {'tensor'}, dimensions={0} | all-to-all | bytes 1179648 | tf_op jit(solution)/shard_map/all_to_all | solution.py:34
  300.8 1.2 key_value.16
  302.0 2.7 collective-permute-start.14
  304.7 1.0 query.16.q_ref
  305.7 1.4 attention.16
  307.1 14.7 %all_to_all.110.arrived_ref = bf16[8,288,128]{2,1,0:T(8,128)(2,1)S(1)} all-to-all(bf16[8,288,128]{2,1,0:T(8,128)(2,1)S(1)} %attention.16), channel_id=1, replica_groups=mesh['section'=8,'seq'=2,'tensor'=8] {'tensor'}, dimensions={0} | all-to-all | bytes 1179648 | tf_op jit(solution)/shard_map/all_to_all | solution.py:34
  322.0 1.3 collective-permute-start.15
  323.3 4.1 %collective-permute-done.15.held_ref = bf16[288,128]{1,0:T(8,128)(2,1)S(1)} collective-permute-done((bf16[288,128]{1,0:T(8,128)(2,1)S(1)}, bf16[288,128]{1,0:T(8,128)(2,1)S(1)}, u32[]{:S(2)}, u32[]{:S(2)}) %collective-permute-start.15) | collective-permute-done | bytes 73760 | tf_op jit(solution)/shard_map/ppermute | solution.py:339
  327.4 13.3 %all_to_all.111.x_ref = bf16[8,288,128]{2,1,0:T(8,128)(2,1)S(1)} all-to-all(bf16[8,288,128]{2,1,0:T(8,128)(2,1)S(1)} %broadcast_in_dim.31), channel_id=1, replica_groups=mesh['section'=8,'seq'=2,'tensor'=8] {'tensor'}, dimensions={0} | all-to-all | bytes 1179648 | tf_op jit(solution)/shard_map/all_to_all | solution.py:34
  340.7 1.2 key_value.17
  341.9 2.5 collective-permute-start.16
  344.4 1.0 query.17.q_ref
  345.5 1.4 attention.17
  346.8 14.7 %all_to_all.112.arrived_ref = bf16[8,288,128]{2,1,0:T(8,128)(2,1)S(1)} all-to-all(bf16[8,288,128]{2,1,0:T(8,128)(2,1)S(1)} %attention.17), channel_id=1, replica_groups=mesh['section'=8,'seq'=2,'tensor'=8] {'tensor'}, dimensions={0} | all-to-all | bytes 1179648 | tf_op jit(solution)/shard_map/all_to_all | solution.py:34
  361.9 13.5 %all_to_all.113 = bf16[16,2,8,576]{3,2,1,0:T(8,128)(2,1)S(1)} all-to-all(bf16[16,2,8,576]{3,2,1,0:T(8,128)(2,1)S(1)} %bitcast.10), channel_id=1, replica_groups=mesh['section'=8,'seq'=2,'tensor'=8] {'seq','tensor'}, dimensions={0} | all-to-all | bytes 589824 | tf_op jit(solution)/shard_map/all_to_all | solution.py:34
  375.6 0.8 copy.12
  (73 shorter events, 9.0 us)
Async XLA Ops:
  0.0 25.2 %copy-start.1 = (bf16[1,4608,256]{2,1,0:T(8,128)(2,1)S(1)}, bf16[1,4608,256]{2,1,0:T(8,128)(2,1)}, u32[]{:S(2)}) copy-start(bf16[1,4608,256]{2,1,0:T(8,128)(2,1)} %wk_ref.17) | copy-start | bytes 7077892
  4.5 26.1 %copy-start = (bf16[1,4608,512]{2,1,0:T(8,128)(2,1)S(1)}, bf16[1,4608,512]{2,1,0:T(8,128)(2,1)}, u32[]{:S(2)}) copy-start(bf16[1,4608,512]{2,1,0:T(8,128)(2,1)} %wq_ref.17) | copy-start | bytes 14155780
  24.9 6.8 %slice-start = ((s8[4718592]{0:T(1024)(128)(4,1)}), s8[4194304]{0:T(1024)(128)(4,1)S(1)}, s32[]{:S(2)}) async-start(s8[4718592]{0:T(1024)(128)(4,1)} %bitcast.7), calls=%async_computation.19 | async-start | bytes 8388608
  25.2 1.8 copy-start.2
  27.0 0.7 copy-start.4
  27.7 4.0 %slice-start.1 = ((s8[4718592]{0:T(1024)(128)(4,1)}), s8[524288]{0:T(1024)(128)(4,1)S(1)}, s32[]{:S(2)}) async-start(s8[4718592]{0:T(1024)(128)(4,1)} %bitcast.7), calls=%async_computation.20 | async-start | bytes 1048576
  28.9 2.8 collective-permute-start
  31.6 16.1 %copy-start.6 = (bf16[1,4608]{1,0:T(2,128)(2,1)S(1)}, bf16[1,4608]{1,0:T(2,128)(2,1)}, u32[]{:S(2)}) copy-start(bf16[1,4608]{1,0:T(2,128)(2,1)} %gain_ref.35) | copy-start | bytes 27652
  31.7 30.5 %copy-start.3 = (bf16[1,4608,256]{2,1,0:T(8,128)(2,1)S(1)}, bf16[1,4608,256]{2,1,0:T(8,128)(2,1)}, u32[]{:S(2)}) copy-start(bf16[1,4608,256]{2,1,0:T(8,128)(2,1)} %wv_ref.17) | copy-start | bytes 7077892
  31.7 30.5 %copy-start.5 = (bf16[1,4608]{1,0:T(2,128)(2,1)S(1)}, bf16[1,4608]{1,0:T(2,128)(2,1)}, u32[]{:S(2)}) copy-start(bf16[1,4608]{1,0:T(2,128)(2,1)} %gain_ref.34) | copy-start | bytes 27652
  48.0 0.7 collective-permute-start.1
  63.4 3.4 collective-permute-start.2
  83.1 0.7 collective-permute-start.3
  98.5 3.4 collective-permute-start.4
  118.1 0.7 collective-permute-start.5
  133.5 3.6 collective-permute-start.6
  153.4 0.7 collective-permute-start.7
  168.8 3.4 collective-permute-start.8
  188.4 0.7 collective-permute-start.9
  203.8 3.4 collective-permute-start.10
  223.5 0.7 collective-permute-start.11
  238.9 3.4 collective-permute-start.12
  258.5 28.8 %collective-permute-start.13 = (bf16[288,128]{1,0:T(8,128)(2,1)S(1)}, bf16[288,128]{1,0:T(8,128)(2,1)S(1)}, u32[]{:S(2)}, u32[]{:S(2)}) collective-permute-start(bf16[288,128]{1,0:T(8,128)(2,1)S(1)} %combine.15.refs_6_), channel_id=1, source_target_pairs={{80,96},{96,112},{81,97},{97,113},{82,98},{98,114},{83,99},{99,115... | collective-permute-start | bytes 221192 | tf_op jit(solution)/shard_map/ppermute | solution.py:339
  302.0 3.7 collective-permute-start.14
  322.0 5.4 %collective-permute-start.15 = (bf16[288,128]{1,0:T(8,128)(2,1)S(1)}, bf16[288,128]{1,0:T(8,128)(2,1)S(1)}, u32[]{:S(2)}, u32[]{:S(2)}) collective-permute-start(bf16[288,128]{1,0:T(8,128)(2,1)S(1)} %combine.16.refs_7_), channel_id=1, source_target_pairs={{96,112},{97,113},{98,114},{99,115},{100,116},{101,117},{102,118},... | collective-permute-start | bytes 221192 | tf_op jit(solution)/shard_map/ppermute | solution.py:339
  341.9 3.5 collective-permute-start.16

commit v5 on v4

--- a/solution.py
+++ b/solution.py
@@ -11,6 +11,7 @@
 CHUNKS = 2
 LANES = 128
 OWN = 8
+FOLD = 5
 
 softcap_limit = 50.0
 query_scale = 144.0 ** (-0.5)
@@ -164,23 +165,42 @@
     held_ref[...] = jnp.where(is_first, following, moved).astype(bf16)
 
 
-def pick_kernel(facts_ref, blocks_ref, out_ref):
+def pick_kernel(facts_ref, mine_ref, theirs_ref, out_ref):
     peers = out_ref.shape[0]
-    spans, rows, _ = blocks_ref.shape
-    blocks = [blocks_ref[j].astype(f32) for j in range(spans)]
-    first = one_of(facts_ref, FIRST_FROM, blocks).astype(bf16)
+    both = [jnp.transpose(ref[...].astype(f32)) for ref in (mine_ref, theirs_ref)]
+    rows = both[0].shape[0] // CHUNKS
+    part = both[0].shape[1]
+    blocks = [b[i * rows:(i + 1) * rows] for b in both for i in range(CHUNKS)]
+    first = one_of(facts_ref, FIRST_FROM, blocks)
     second = one_of(facts_ref, SECOND_FROM, blocks)
+    sent, whole = rows + OWN, part // LANES
+    kept = FOLD * OWN
     for t in range(peers):
-        out_ref[t, :rows] = first
-        out_ref[t, rows:] = second[t * OWN:(t + 1) * OWN].astype(bf16)
+        own = second[t * OWN:(t + 1) * OWN]
+        for c in range(whole):
+            out_ref[t, c * sent:c * sent + rows] = first[:, lanes(c)].astype(bf16)
+            out_ref[t, c * sent + rows:(c + 1) * sent] = own[:, lanes(c)].astype(bf16)
+        rest = slice(whole * LANES, part)
+        upper = jnp.concatenate([first[kept:, rest], own[:, rest], own[:, rest]], axis=0)
+        fold = jnp.concatenate([first[:kept, rest], upper], axis=1)
+        out_ref[t, whole * sent:] = fold.astype(bf16)
 
 
 def gather_kernel(facts_ref, arrived_ref, full_ref, held_ref, next_ref, flat_ref):
     peers = full_ref.shape[0]
     rows = peers * OWN
     part = flat_ref.shape[1] // peers
+    sent, whole = rows + OWN, part // LANES
+    kept = FOLD * OWN
+    rest = part - whole * LANES
     for t in range(peers):
-        flat_ref[:, t * part:(t + 1) * part] = arrived_ref[t].astype(f32)
+        for c in range(whole):
+            piece = arrived_ref[t, c * sent:(c + 1) * sent].astype(f32)
+            flat_ref[:, t * part + c * LANES:t * part + (c + 1) * LANES] = piece
+        fold = arrived_ref[t, whole * sent:].astype(f32)
+        at = slice((t + 1) * part - rest, (t + 1) * part)
+        flat_ref[:kept, at] = fold[:, :rest]
+        flat_ref[kept:, at] = fold[:sent - kept, rest:]
     owner = fact(facts_ref, OWNER)
     for c in tiles(next_ref.shape):
         blocks = flat_ref[:rows, lanes(c)].reshape(peers, OWN, LANES)
@@ -216,9 +236,9 @@
         for chunk in range(chunks)
         for core in range(cores)
     ]
-    for j in range(out_ref.shape[0] // rows):
-        piece = one_of(facts_ref, GIVEN_AS + j * len(spans), spans)
-        out_ref[j * rows:(j + 1) * rows] = piece.astype(bf16)
+    blocks = out_ref.shape[1] // rows
+    given = [one_of(facts_ref, GIVEN_AS + j * len(spans), spans) for j in range(blocks)]
+    out_ref[...] = jnp.transpose(jnp.concatenate(given, axis=0)).astype(bf16)
 
 
 def body(states_in, span_order, pre_gain, w_query, w_key, w_value, w_out, post_gain):
@@ -278,10 +298,12 @@
     )
 
     tick_total = sections + CHUNKS - 1
+    half_spans = spans // seqs
+    twin_first = jnp.concatenate([span_order[half_spans:], span_order[:half_spans]])
+    near_first = jnp.where(seq_rank == 0, span_order, twin_first)
     ids = jnp.arange(spans, dtype=jnp.int32)
-    given = lax.dynamic_slice_in_dim(span_order, seq_rank * (spans // seqs), spans // seqs, 0)
-    rows_of_facts = [span_order == chunk * seqs + seq_rank for chunk in range(CHUNKS)]
-    rows_of_facts += [(given[:, None] == ids[None, :]).reshape(-1)]
+    rows_of_facts = [near_first == chunk * seqs + seq_rank for chunk in range(CHUNKS)]
+    rows_of_facts += [(near_first[:half_spans, None] == ids[None, :]).reshape(-1)]
     rows_of_facts += [jnp.stack([section_rank, seq_rank, tensor_rank])]
     facts = jnp.concatenate([r.astype(f32) for r in rows_of_facts])
     facts = jnp.pad(facts, (0, FACTS - facts.shape[0]))
@@ -298,15 +320,17 @@
     cos_full = jnp.concatenate([cos_part, cos_part], axis=-1)
     sin_full = jnp.concatenate([-sin_part, sin_part], axis=-1)
 
-    blocks = lax.all_gather(states_in[0], "seq", axis=0).reshape(spans, rows, part)
+    mine = jnp.transpose(states_in[0])
+    theirs = lax.ppermute(mine, "seq", [(0, 1), (1, 0)])
+    sent = (rows + own) * (part // LANES) + FOLD * own
     pieces = pl.pallas_call(
         pick_kernel,
-        out_shape=jax.ShapeDtypeStruct((tensors, rows + own, part), bf16),
-        in_specs=[VMEM, VMEM],
+        out_shape=jax.ShapeDtypeStruct((tensors, sent, LANES), bf16),
+        in_specs=[VMEM, VMEM, VMEM],
         out_specs=VMEM,
         compiler_params=limit(4),
         name="pick",
-    )(facts, blocks)
+    )(facts, mine, theirs)
     no_past = jnp.zeros((rows, 2 * kv_width), bf16)
     pieces, facts, cos_full, sin_full, no_past = lax.optimization_barrier(
         (pieces, facts, cos_full, sin_full, no_past)
@@ -361,13 +385,13 @@
     pieces = exchange(pieces.reshape(seqs * tensors, CHUNKS, own, part), ("seq", "tensor"))
     out = pl.pallas_call(
         order_kernel,
-        out_shape=jax.ShapeDtypeStruct((row_count, part), bf16),
+        out_shape=jax.ShapeDtypeStruct((part, row_count), bf16),
         in_specs=[VMEM, VMEM],
         out_specs=VMEM,
         compiler_params=limit(4),
         name="order",
     )(facts, pieces.reshape(seqs, tensors, CHUNKS, own, part))
-    return out[None, None]
+    return jnp.transpose(out)[None, None]
 
 
 def solution(mesh):

time: 377 us -> 375 us (level)
  blocking collectives: 275 us -> 271 us
  transfers between devices with their start and end apart: 17 -> 18, of which waited for: 2 -> 2; matrix products, arithmetic and copies ran while one was open for 0% -> 0% of each run, Pallas kernels for 2% -> 2%
where the time goes in v5:
time: 375 us; the launch traced here: 374 us
  blocking collectives  271 us (72%)
  Pallas kernels  35.6 us (9%)
  waiting for transfers between devices  31.6 us (8%)
  starting transfers between devices  28.7 us (8%)
  local copies, waits for them, and re-layouts  5.41 us (1%)
    all_to_all x19, blocking collectives, exchange(): return lax.all_to_all(pieces, axes, split_axis=0, concat_axis=0, tiled=True)  271 us
    ppermute x8, waiting for transfers between devices, body(): held = lax.ppermute(made[-1], 'section', [(i, i + 1) for i in busy])  31.6 us
    ppermute x9, starting transfers between devices, body(): kv_other = lax.ppermute(kv_own, 'seq', [(0, 1), (1, 0)])  21.4 us
    pallas_call x9, Pallas kernels, body(): terms = attention(tick)(facts, queries, kv_own, kv_other, *past, w_out)  12.3 us
    pallas_call x9, Pallas kernels, body(): key_value(tick)(facts, full, pre_gain, cos_full, sin_full, w_key, w_value)  10.8 us
    pallas_call x9, Pallas kernels, body(): queries = query(tick)(facts, normed, cos_full, sin_full, w_query)  9.1 us
  transfers between devices with their start and end apart: 18, of which 2 were waited for; matrix products, arithmetic and copies ran while one was open for 0% of the time, Pallas kernels for 2%

profile of v5, /device:TPU:57, one launch (start us, length us, event | category | flops | bytes accessed | tf_op | source)
XLA Modules:
  0.0 374.1 jit_solution(7527144324031213350)
XLA Ops:
  0.8 0.8 fusion.1
  2.5 1.2 copy-done.7
  4.0 18.8 %all_to_all.95.arrived_ref = bf16[8,328,128]{2,1,0:T(8,128)(2,1)S(1)} all-to-all(bf16[8,328,128]{2,1,0:T(8,128)(2,1)S(1)} %pick.1), channel_id=1, replica_groups=mesh['section'=8,'seq'=2,'tensor'=8] {'tensor'}, dimensions={0} | all-to-all | bytes 1343488 | tf_op jit(solution)/shard_map/all_to_all | solution.py:35
  23.1 1.8 copy-done.2
  24.9 0.7 copy-done.4
  25.6 1.2 key_value.9
  26.8 1.7 collective-permute-start.1
  28.4 1.0 query.9.q_ref
  29.6 1.4 attention.9
  30.9 14.7 %all_to_all.96.arrived_ref = bf16[8,288,128]{2,1,0:T(8,128)(2,1)S(1)} all-to-all(bf16[8,288,128]{2,1,0:T(8,128)(2,1)S(1)} %attention.9), channel_id=1, replica_groups=mesh['section'=8,'seq'=2,'tensor'=8] {'tensor'}, dimensions={0} | all-to-all | bytes 1179648 | tf_op jit(solution)/shard_map/all_to_all | solution.py:35
  46.6 13.4 %all_to_all.97.x_ref = bf16[8,288,128]{2,1,0:T(8,128)(2,1)S(1)} all-to-all(bf16[8,288,128]{2,1,0:T(8,128)(2,1)S(1)} %broadcast_in_dim.24), channel_id=1, replica_groups=mesh['section'=8,'seq'=2,'tensor'=8] {'tensor'}, dimensions={0} | all-to-all | bytes 1179648 | tf_op jit(solution)/shard_map/all_to_all | solution.py:35
  60.0 1.2 key_value.10
  61.2 2.4 collective-permute-start.3
  63.6 1.0 query.10.q_ref
  64.7 1.4 attention.10
  66.0 14.7 %all_to_all.98.arrived_ref = bf16[8,288,128]{2,1,0:T(8,128)(2,1)S(1)} all-to-all(bf16[8,288,128]{2,1,0:T(8,128)(2,1)S(1)} %attention.10), channel_id=1, replica_groups=mesh['section'=8,'seq'=2,'tensor'=8] {'tensor'}, dimensions={0} | all-to-all | bytes 1179648 | tf_op jit(solution)/shard_map/all_to_all | solution.py:35
  81.7 13.4 %all_to_all.99.x_ref = bf16[8,288,128]{2,1,0:T(8,128)(2,1)S(1)} all-to-all(bf16[8,288,128]{2,1,0:T(8,128)(2,1)S(1)} %broadcast_in_dim.25), channel_id=1, replica_groups=mesh['section'=8,'seq'=2,'tensor'=8] {'tensor'}, dimensions={0} | all-to-all | bytes 1179648 | tf_op jit(solution)/shard_map/all_to_all | solution.py:35
  95.1 1.2 key_value.11
  96.3 2.4 collective-permute-start.5
  98.7 1.0 query.11.q_ref
  99.7 1.4 attention.11
  101.1 14.7 %all_to_all.100.arrived_ref = bf16[8,288,128]{2,1,0:T(8,128)(2,1)S(1)} all-to-all(bf16[8,288,128]{2,1,0:T(8,128)(2,1)S(1)} %attention.11), channel_id=1, replica_groups=mesh['section'=8,'seq'=2,'tensor'=8] {'tensor'}, dimensions={0} | all-to-all | bytes 1179648 | tf_op jit(solution)/shard_map/all_to_all | solution.py:35
  116.7 13.4 %all_to_all.101.x_ref = bf16[8,288,128]{2,1,0:T(8,128)(2,1)S(1)} all-to-all(bf16[8,288,128]{2,1,0:T(8,128)(2,1)S(1)} %broadcast_in_dim.26), channel_id=1, replica_groups=mesh['section'=8,'seq'=2,'tensor'=8] {'tensor'}, dimensions={0} | all-to-all | bytes 1179648 | tf_op jit(solution)/shard_map/all_to_all | solution.py:35
  130.1 1.2 key_value.12
  131.3 2.6 collective-permute-start.7
  133.9 1.0 query.12.q_ref
  134.9 1.4 attention.12
  136.3 14.7 %all_to_all.102.arrived_ref = bf16[8,288,128]{2,1,0:T(8,128)(2,1)S(1)} all-to-all(bf16[8,288,128]{2,1,0:T(8,128)(2,1)S(1)} %attention.12), channel_id=1, replica_groups=mesh['section'=8,'seq'=2,'tensor'=8] {'tensor'}, dimensions={0} | all-to-all | bytes 1179648 | tf_op jit(solution)/shard_map/all_to_all | solution.py:35
  152.0 13.4 %all_to_all.103.x_ref = bf16[8,288,128]{2,1,0:T(8,128)(2,1)S(1)} all-to-all(bf16[8,288,128]{2,1,0:T(8,128)(2,1)S(1)} %broadcast_in_dim.27), channel_id=1, replica_groups=mesh['section'=8,'seq'=2,'tensor'=8] {'tensor'}, dimensions={0} | all-to-all | bytes 1179648 | tf_op jit(solution)/shard_map/all_to_all | solution.py:35
  165.4 1.2 key_value.13
  166.6 2.4 collective-permute-start.9
  169.0 1.0 query.13.q_ref
  170.0 1.4 attention.13
  171.4 14.7 %all_to_all.104.arrived_ref = bf16[8,288,128]{2,1,0:T(8,128)(2,1)S(1)} all-to-all(bf16[8,288,128]{2,1,0:T(8,128)(2,1)S(1)} %attention.13), channel_id=1, replica_groups=mesh['section'=8,'seq'=2,'tensor'=8] {'tensor'}, dimensions={0} | all-to-all | bytes 1179648 | tf_op jit(solution)/shard_map/all_to_all | solution.py:35
  187.0 13.4 %all_to_all.105.x_ref = bf16[8,288,128]{2,1,0:T(8,128)(2,1)S(1)} all-to-all(bf16[8,288,128]{2,1,0:T(8,128)(2,1)S(1)} %broadcast_in_dim.28), channel_id=1, replica_groups=mesh['section'=8,'seq'=2,'tensor'=8] {'tensor'}, dimensions={0} | all-to-all | bytes 1179648 | tf_op jit(solution)/shard_map/all_to_all | solution.py:35
  200.4 1.2 key_value.14
  201.6 2.4 collective-permute-start.11
  204.0 1.0 query.14.q_ref
  205.1 1.4 attention.14
  206.4 14.7 %all_to_all.106.arrived_ref = bf16[8,288,128]{2,1,0:T(8,128)(2,1)S(1)} all-to-all(bf16[8,288,128]{2,1,0:T(8,128)(2,1)S(1)} %attention.14), channel_id=1, replica_groups=mesh['section'=8,'seq'=2,'tensor'=8] {'tensor'}, dimensions={0} | all-to-all | bytes 1179648 | tf_op jit(solution)/shard_map/all_to_all | solution.py:35
  222.1 13.4 %all_to_all.107.x_ref = bf16[8,288,128]{2,1,0:T(8,128)(2,1)S(1)} all-to-all(bf16[8,288,128]{2,1,0:T(8,128)(2,1)S(1)} %broadcast_in_dim.29), channel_id=1, replica_groups=mesh['section'=8,'seq'=2,'tensor'=8] {'tensor'}, dimensions={0} | all-to-all | bytes 1179648 | tf_op jit(solution)/shard_map/all_to_all | solution.py:35
  235.5 1.2 key_value.15
  236.7 2.4 collective-permute-start.13
  239.1 1.0 query.15.q_ref
  240.1 1.4 attention.15
  241.5 14.7 %all_to_all.108.arrived_ref = bf16[8,288,128]{2,1,0:T(8,128)(2,1)S(1)} all-to-all(bf16[8,288,128]{2,1,0:T(8,128)(2,1)S(1)} %attention.15), channel_id=1, replica_groups=mesh['section'=8,'seq'=2,'tensor'=8] {'tensor'}, dimensions={0} | all-to-all | bytes 1179648 | tf_op jit(solution)/shard_map/all_to_all | solution.py:35
  256.3 1.3 collective-permute-start.14
  257.6 27.5 %collective-permute-done.14.held_ref = bf16[288,128]{1,0:T(8,128)(2,1)S(1)} collective-permute-done((bf16[288,128]{1,0:T(8,128)(2,1)S(1)}, bf16[288,128]{1,0:T(8,128)(2,1)S(1)}, u32[]{:S(2)}, u32[]{:S(2)}) %collective-permute-start.14) | collective-permute-done | bytes 73760 | tf_op jit(solution)/shard_map/ppermute | solution.py:363
  285.3 13.4 %all_to_all.109.x_ref = bf16[8,288,128]{2,1,0:T(8,128)(2,1)S(1)} all-to-all(bf16[8,288,128]{2,1,0:T(8,128)(2,1)S(1)} %broadcast_in_dim.30), channel_id=1, replica_groups=mesh['section'=8,'seq'=2,'tensor'=8] {'tensor'}, dimensions={0} | all-to-all | bytes 1179648 | tf_op jit(solution)/shard_map/all_to_all | solution.py:35
  298.6 1.2 key_value.16
  299.8 2.7 collective-permute-start.15
  302.5 1.0 query.16.q_ref
  303.5 1.4 attention.16
  304.9 14.7 %all_to_all.110.arrived_ref = bf16[8,288,128]{2,1,0:T(8,128)(2,1)S(1)} all-to-all(bf16[8,288,128]{2,1,0:T(8,128)(2,1)S(1)} %attention.16), channel_id=1, replica_groups=mesh['section'=8,'seq'=2,'tensor'=8] {'tensor'}, dimensions={0} | all-to-all | bytes 1179648 | tf_op jit(solution)/shard_map/all_to_all | solution.py:35
  319.8 1.3 collective-permute-start.16
  321.1 4.1 %collective-permute-done.16.held_ref = bf16[288,128]{1,0:T(8,128)(2,1)S(1)} collective-permute-done((bf16[288,128]{1,0:T(8,128)(2,1)S(1)}, bf16[288,128]{1,0:T(8,128)(2,1)S(1)}, u32[]{:S(2)}, u32[]{:S(2)}) %collective-permute-start.16) | collective-permute-done | bytes 73760 | tf_op jit(solution)/shard_map/ppermute | solution.py:363
  325.2 13.3 %all_to_all.111.x_ref = bf16[8,288,128]{2,1,0:T(8,128)(2,1)S(1)} all-to-all(bf16[8,288,128]{2,1,0:T(8,128)(2,1)S(1)} %broadcast_in_dim.31), channel_id=1, replica_groups=mesh['section'=8,'seq'=2,'tensor'=8] {'tensor'}, dimensions={0} | all-to-all | bytes 1179648 | tf_op jit(solution)/shard_map/all_to_all | solution.py:35
  338.6 1.2 key_value.17
  339.8 2.5 collective-permute-start.17
  342.2 1.0 query.17.q_ref
  343.3 1.4 attention.17
  344.6 14.7 %all_to_all.112.arrived_ref = bf16[8,288,128]{2,1,0:T(8,128)(2,1)S(1)} all-to-all(bf16[8,288,128]{2,1,0:T(8,128)(2,1)S(1)} %attention.17), channel_id=1, replica_groups=mesh['section'=8,'seq'=2,'tensor'=8] {'tensor'}, dimensions={0} | all-to-all | bytes 1179648 | tf_op jit(solution)/shard_map/all_to_all | solution.py:35
  359.7 13.5 %all_to_all.113 = bf16[16,2,8,576]{3,2,1,0:T(8,128)(2,1)S(1)} all-to-all(bf16[16,2,8,576]{3,2,1,0:T(8,128)(2,1)S(1)} %bitcast.14), channel_id=1, replica_groups=mesh['section'=8,'seq'=2,'tensor'=8] {'seq','tensor'}, dimensions={0} | all-to-all | bytes 589824 | tf_op jit(solution)/shard_map/all_to_all | solution.py:35
  373.2 0.8 order.1
  (75 shorter events, 8.9 us)
Async XLA Ops:
  0.0 23.0 %copy-start.1 = (bf16[1,4608,256]{2,1,0:T(8,128)(2,1)S(1)}, bf16[1,4608,256]{2,1,0:T(8,128)(2,1)}, u32[]{:S(2)}) copy-start(bf16[1,4608,256]{2,1,0:T(8,128)(2,1)} %wk_ref.17) | copy-start | bytes 7077892
  0.0 2.4 collective-permute-start
  1.8 26.6 %copy-start = (bf16[1,4608,512]{2,1,0:T(8,128)(2,1)S(1)}, bf16[1,4608,512]{2,1,0:T(8,128)(2,1)}, u32[]{:S(2)}) copy-start(bf16[1,4608,512]{2,1,0:T(8,128)(2,1)} %wq_ref.17) | copy-start | bytes 14155780
  2.5 1.2 copy-start.7
  22.7 6.8 %slice-start = ((s8[4718592]{0:T(1024)(128)(4,1)}), s8[4194304]{0:T(1024)(128)(4,1)S(1)}, s32[]{:S(2)}) async-start(s8[4718592]{0:T(1024)(128)(4,1)} %bitcast.12), calls=%async_computation.19 | async-start | bytes 8388608
  23.0 1.8 copy-start.2
  24.9 0.7 copy-start.4
  25.6 3.9 %slice-start.1 = ((s8[4718592]{0:T(1024)(128)(4,1)}), s8[524288]{0:T(1024)(128)(4,1)S(1)}, s32[]{:S(2)}) async-start(s8[4718592]{0:T(1024)(128)(4,1)} %bitcast.12), calls=%async_computation.20 | async-start | bytes 1048576
  26.8 2.7 collective-permute-start.1
  29.5 16.1 %copy-start.6 = (bf16[1,4608]{1,0:T(2,128)(2,1)S(1)}, bf16[1,4608]{1,0:T(2,128)(2,1)}, u32[]{:S(2)}) copy-start(bf16[1,4608]{1,0:T(2,128)(2,1)} %gain_ref.35) | copy-start | bytes 27652
  29.5 30.5 %copy-start.3 = (bf16[1,4608,256]{2,1,0:T(8,128)(2,1)S(1)}, bf16[1,4608,256]{2,1,0:T(8,128)(2,1)}, u32[]{:S(2)}) copy-start(bf16[1,4608,256]{2,1,0:T(8,128)(2,1)} %wv_ref.17) | copy-start | bytes 7077892
  29.5 30.5 %copy-start.5 = (bf16[1,4608]{1,0:T(2,128)(2,1)S(1)}, bf16[1,4608]{1,0:T(2,128)(2,1)}, u32[]{:S(2)}) copy-start(bf16[1,4608]{1,0:T(2,128)(2,1)} %gain_ref.34) | copy-start | bytes 27652
  45.8 0.7 collective-permute-start.2
  61.2 3.4 collective-permute-start.3
  80.9 0.7 collective-permute-start.4
  96.3 3.4 collective-permute-start.5
  115.9 0.7 collective-permute-start.6
  131.3 3.6 collective-permute-start.7
  151.2 0.7 collective-permute-start.8
  166.6 3.4 collective-permute-start.9
  186.2 0.7 collective-permute-start.10
  201.6 3.4 collective-permute-start.11
  221.3 0.7 collective-permute-start.12
  236.7 3.4 collective-permute-start.13
  256.3 28.8 %collective-permute-start.14 = (bf16[288,128]{1,0:T(8,128)(2,1)S(1)}, bf16[288,128]{1,0:T(8,128)(2,1)S(1)}, u32[]{:S(2)}, u32[]{:S(2)}) collective-permute-start(bf16[288,128]{1,0:T(8,128)(2,1)S(1)} %combine.15.refs_6_), channel_id=1, source_target_pairs={{80,96},{96,112},{81,97},{97,113},{82,98},{98,114},{83,99},{99,115... | collective-permute-start | bytes 221192 | tf_op jit(solution)/shard_map/ppermute | solution.py:363
  299.8 3.7 collective-permute-start.15
  319.8 5.4 %collective-permute-start.16 = (bf16[288,128]{1,0:T(8,128)(2,1)S(1)}, bf16[288,128]{1,0:T(8,128)(2,1)S(1)}, u32[]{:S(2)}, u32[]{:S(2)}) collective-permute-start(bf16[288,128]{1,0:T(8,128)(2,1)S(1)} %combine.16.refs_7_), channel_id=1, source_target_pairs={{96,112},{97,113},{98,114},{99,115},{100,116},{101,117},{102,118},... | collective-permute-start | bytes 221192 | tf_op jit(solution)/shard_map/ppermute | solution.py:363
  339.8 3.5 collective-permute-start.17

commit v6 on v5

--- a/solution.py
+++ b/solution.py
@@ -11,6 +11,7 @@
 CHUNKS = 2
 LANES = 128
 OWN = 8
+OUT_STEPS = 3
 FOLD = 5
 
 softcap_limit = 50.0
@@ -89,19 +90,56 @@
     kv_ref[:, kv_width:] = values.astype(bf16)
 
 
-def query_kernel(tick, facts_ref, normed_ref, cos_ref, sin_ref, wq_ref, q_ref):
+def early_kernel(tick, facts_ref, normed_ref, cos_ref, sin_ref, wq_ref, own_ref,
+                 past_own_ref, past_other_ref, wo_ref, out_ref, q_ref, attended_ref):
+    @pl.when(jnp.max(fact(facts_ref, CORE)) < 1)
+    def _():
+        query_part(tick, facts_ref, normed_ref, cos_ref, sin_ref, wq_ref, q_ref)
+        attention_part(
+            tick, facts_ref, q_ref, own_ref, own_ref, past_own_ref, past_other_ref, wo_ref,
+            out_ref, attended_ref,
+        )
+
+
+def late_query_kernel(tick, facts_ref, normed_ref, cos_ref, sin_ref, wq_ref, q_ref):
+    @pl.when(jnp.max(fact(facts_ref, CORE)) > 0)
+    def _():
+        query_part(tick, facts_ref, normed_ref, cos_ref, sin_ref, wq_ref, q_ref)
+
+
+def late_kernel(tick, facts_ref, q_ref, own_ref, other_ref, past_own_ref, past_other_ref, wo_ref,
+                done_ref, out_ref, attended_ref):
+    is_late = jnp.max(fact(facts_ref, CORE)) > 0
+
+    @pl.when(is_late)
+    def _():
+        attention_part(
+            tick, facts_ref, q_ref, own_ref, other_ref, past_own_ref, past_other_ref, wo_ref,
+            out_ref, attended_ref,
+        )
+
+    @pl.when(jnp.logical_not(is_late))
+    def _():
+        out_ref[...] = done_ref[...]
+
+
+def query_part(tick, facts_ref, normed_ref, cos_ref, sin_ref, wq_ref, q_ref):
     q_width = q_ref.shape[1]
     later = is_later(facts_ref, tick)
     cos_full = jnp.where(later, cos_ref[1], cos_ref[0])
     sin_full = jnp.where(later, sin_ref[1], sin_ref[0])
-    queries = jnp.dot(normed_ref[...], wq_ref[0], preferred_element_type=f32)
-    for head in range(q_width // HEAD_DIM):
-        at = slice(head * HEAD_DIM, (head + 1) * HEAD_DIM)
-        q_ref[:, at] = (rope(queries[:, at], cos_full, sin_full) * query_scale).astype(bf16)
-
-
-def attention_kernel(tick, facts_ref, q_ref, own_ref, other_ref, past_own_ref, past_other_ref, wo_ref,
-                     out_ref, attended_ref):
+    pair = 2 * HEAD_DIM
+
+    @pl.loop(0, q_width // pair)
+    def _(p):
+        at = pl.ds(pl.multiple_of(p * pair, pair), pair)
+        queries = jnp.dot(normed_ref[...], wq_ref[0, :, at], preferred_element_type=f32)
+        turned = [rope(queries[:, lanes(h)], cos_full, sin_full) * query_scale for h in range(2)]
+        q_ref[:, at] = jnp.concatenate(turned, axis=1).astype(bf16)
+
+
+def attention_part(tick, facts_ref, q_ref, own_ref, other_ref, past_own_ref, past_other_ref, wo_ref,
+                   out_ref, attended_ref):
     rows, q_width = q_ref.shape
     kv_width = own_ref.shape[1] // 2
     kv_heads = kv_width // HEAD_DIM
@@ -141,9 +179,15 @@
             attended_ref[:, first + g * HEAD_DIM:first + (g + 1) * HEAD_DIM] = attended[
                 g * rows:(g + 1) * rows
             ]
-    terms = jnp.dot(attended_ref[...], wo_ref[0], preferred_element_type=f32)
-    for c in tiles(out_ref.shape):
-        out_ref[:, tile(c)] = terms[:, lanes(c)].reshape(-1, OWN, LANES).astype(bf16)
+    count = out_ref.shape[1] // OWN // OUT_STEPS
+
+    @pl.loop(0, OUT_STEPS)
+    def _(n):
+        at = pl.ds(pl.multiple_of(n * count * LANES, LANES), count * LANES)
+        terms = jnp.dot(attended_ref[...], wo_ref[0, :, at], preferred_element_type=f32)
+        blocks = [terms[:, lanes(c)].reshape(-1, OWN, LANES).astype(bf16) for c in range(count)]
+        to = pl.ds(pl.multiple_of(n * count * OWN, 2 * OWN), count * OWN)
+        out_ref[:, to] = jnp.concatenate(blocks, axis=1)
 
 
 def combine_kernel(arrived_ref, held_ref, gain_ref, out_ref, sum_ref):
@@ -234,7 +278,7 @@
     spans = [
         arrived_ref[core, :, chunk].astype(f32).reshape(rows, part)
         for chunk in range(chunks)
-        for core in range(cores)
+        for core in reversed(range(cores))
     ]
     blocks = out_ref.shape[1] // rows
     given = [one_of(facts_ref, GIVEN_AS + j * len(spans), spans) for j in range(blocks)]
@@ -253,6 +297,7 @@
     seq_rank = lax.axis_index("seq")
     tensor_rank = lax.axis_index("tensor")
     spans = span_order.shape[0]
+    place = seqs - 1 - seq_rank
     rows = row_count // CHUNKS
     own = rows // tensors
     assert own == OWN
@@ -270,22 +315,34 @@
         compiler_params=limit(10),
         name="key_value",
     )
-    query = lambda tick: pl.pallas_call(
-        functools.partial(query_kernel, tick),
-        out_shape=jax.ShapeDtypeStruct((rows, q_width), bf16),
+
+    terms_shape = jax.ShapeDtypeStruct((tensors, *block), bf16)
+    q_shape = (rows, q_width)
+    early = lambda tick: pl.pallas_call(
+        functools.partial(early_kernel, tick),
+        out_shape=terms_shape,
+        in_specs=[VMEM] * 9,
+        out_specs=VMEM,
+        scratch_shapes=[pltpu.VMEM(q_shape, bf16)] * 2,
+        compiler_params=limit(16),
+        name="early",
+    )
+    late_query = lambda tick: pl.pallas_call(
+        functools.partial(late_query_kernel, tick),
+        out_shape=jax.ShapeDtypeStruct(q_shape, bf16),
         in_specs=[VMEM] * 5,
         out_specs=VMEM,
         compiler_params=limit(8),
-        name="query",
-    )
-    attention = lambda tick: pl.pallas_call(
-        functools.partial(attention_kernel, tick),
-        out_shape=jax.ShapeDtypeStruct((tensors, *block), bf16),
-        in_specs=[VMEM] * 7,
-        out_specs=VMEM,
-        scratch_shapes=[pltpu.VMEM((rows, q_width), bf16)],
-        compiler_params=limit(10),
-        name="attention",
+        name="late_query",
+    )
+    late = lambda tick: pl.pallas_call(
+        functools.partial(late_kernel, tick),
+        out_shape=terms_shape,
+        in_specs=[VMEM] * 8,
+        out_specs=VMEM,
+        scratch_shapes=[pltpu.VMEM(q_shape, bf16)],
+        compiler_params=limit(12),
+        name="late",
     )
     combine = pl.pallas_call(
         combine_kernel,
@@ -302,15 +359,15 @@
     twin_first = jnp.concatenate([span_order[half_spans:], span_order[:half_spans]])
     near_first = jnp.where(seq_rank == 0, span_order, twin_first)
     ids = jnp.arange(spans, dtype=jnp.int32)
-    rows_of_facts = [near_first == chunk * seqs + seq_rank for chunk in range(CHUNKS)]
+    rows_of_facts = [near_first == chunk * seqs + place for chunk in range(CHUNKS)]
     rows_of_facts += [(near_first[:half_spans, None] == ids[None, :]).reshape(-1)]
-    rows_of_facts += [jnp.stack([section_rank, seq_rank, tensor_rank])]
+    rows_of_facts += [jnp.stack([section_rank, place, tensor_rank])]
     facts = jnp.concatenate([r.astype(f32) for r in rows_of_facts])
     facts = jnp.pad(facts, (0, FACTS - facts.shape[0]))
     facts = jnp.broadcast_to(facts[:, None], (FACTS, LANES))
     places = (
         jnp.arange(CHUNKS, dtype=jnp.int32)[:, None] * chunk_len
-        + seq_rank * rows
+        + place * rows
         + jnp.arange(rows, dtype=jnp.int32)[None, :]
     )
     half = HEAD_DIM // 2
@@ -353,9 +410,11 @@
     made = []
     for tick in range(tick_total):
         kv_own, normed = key_value(tick)(facts, full, pre_gain, cos_full, sin_full, w_key, w_value)
+        terms = early(tick)(facts, normed, cos_full, sin_full, w_query, kv_own, *past, w_out)
+        kv_own, normed, terms = lax.optimization_barrier((kv_own, normed, terms))
         kv_other = lax.ppermute(kv_own, "seq", [(0, 1), (1, 0)])
-        queries = query(tick)(facts, normed, cos_full, sin_full, w_query)
-        terms = attention(tick)(facts, queries, kv_own, kv_other, *past, w_out)
+        queries = late_query(tick)(facts, normed, cos_full, sin_full, w_query)
+        terms = late(tick)(facts, queries, kv_own, kv_other, *past, w_out, terms)
         past = (kv_own, kv_other)
         made.append(combine(exchange(terms, "tensor"), held, post_gain))
         if tick + 1 < tick_total:

time: 375 us -> 364 us (0.971)
  blocking collectives: 271 us -> 247 us
  waiting for transfers between devices: 31.6 us -> 45.3 us
  starting transfers between devices: 28.7 us -> 18.4 us
  Pallas kernels: 35.6 us -> 43.9 us
    all_to_all x19, blocking collectives: 271 us -> 247 us  [exchange(): return lax.all_to_all(pieces, axes, split_axis=0, concat_axis=0, tiled=True)]
    ppermute x9, starting transfers between devices: 21.4 us -> 11.2 us  [body(): kv_other = lax.ppermute(kv_own, 'seq', [(0, 1), (1, 0)])]
    pallas_call x18 -> x27, Pallas kernels: 21.4 us -> 29.8 us  [the longest x9 27 us: body(): early(tick)]
    ppermute x9, waiting for transfers between devices: 0.02 us -> 7.05 us  [body(): kv_other = lax.ppermute(kv_own, 'seq', [(0, 1), (1, 0)])]
    ppermute x8, waiting for transfers between devices: 31.6 us -> 38.2 us  [body(): held = lax.ppermute(made[-1], 'section', [(i, i + 1) for i in busy])]
  transfers between devices with their start and end apart: 18 -> 18, of which waited for: 2 -> 11; matrix products, arithmetic and copies ran while one was open for 0% -> 0% of each run, Pallas kernels for 2% -> 0%
where the time goes in v6:
time: 364 us; the launch traced here: 363 us
  blocking collectives  247 us (68%)
  waiting for transfers between devices  45.3 us (12%)
  Pallas kernels  43.9 us (12%)
  starting transfers between devices  18.4 us (5%)
  local copies, waits for them, and re-layouts  7.57 us (2%)
    all_to_all x19, blocking collectives, exchange(): return lax.all_to_all(pieces, axes, split_axis=0, concat_axis=0, tiled=True)  247 us
    ppermute x8, waiting for transfers between devices, body(): held = lax.ppermute(made[-1], 'section', [(i, i + 1) for i in busy])  38.2 us
    pallas_call x9, Pallas kernels, body(): early(tick)  27 us
    ppermute x9, starting transfers between devices, body(): kv_other = lax.ppermute(kv_own, 'seq', [(0, 1), (1, 0)])  11.2 us
    pallas_call x9, Pallas kernels, body(): key_value(tick)(facts, full, pre_gain, cos_full, sin_full, w_key, w_value)  10.8 us
  transfers between devices with their start and end apart: 18, of which 11 were waited for; matrix products, arithmetic and copies ran while one was open for 0% of the time, Pallas kernels for 0%

profile of v6, /device:TPU:57, one launch (start us, length us, event | category | flops | bytes accessed | tf_op | source)
XLA Modules:
  0.0 363.3 jit_solution(8418487018059951726)
XLA Ops:
  0.0 0.7 collective-permute-start
  0.8 0.8 fusion.1
  2.5 1.2 copy-done.7
  4.0 18.8 %all_to_all.95.arrived_ref = bf16[8,328,128]{2,1,0:T(8,128)(2,1)S(1)} all-to-all(bf16[8,328,128]{2,1,0:T(8,128)(2,1)S(1)} %pick.1), channel_id=1, replica_groups=mesh['section'=8,'seq'=2,'tensor'=8] {'tensor'}, dimensions={0} | all-to-all | bytes 1343488 | tf_op jit(solution)/shard_map/all_to_all | solution.py:36
  23.1 1.7 copy-done.3
  24.7 0.7 copy-done.5
  25.4 1.2 key_value.9
  26.7 2.3 copy-done.1
  29.0 3.0 early.9.done_ref
  32.3 1.1 collective-permute-done.1.other_ref.past_other_ref
  33.5 12.7 %all_to_all.96.arrived_ref = bf16[8,288,128]{2,1,0:T(8,128)(2,1)S(1)} all-to-all(bf16[8,288,128]{2,1,0:T(8,128)(2,1)S(1)} %late.9), channel_id=1, replica_groups=mesh['section'=8,'seq'=2,'tensor'=8] {'tensor'}, dimensions={0} | all-to-all | bytes 1179648 | tf_op jit(solution)/shard_map/all_to_all | solution.py:36
  47.2 12.0 %all_to_all.97.x_ref = bf16[8,288,128]{2,1,0:T(8,128)(2,1)S(1)} all-to-all(bf16[8,288,128]{2,1,0:T(8,128)(2,1)S(1)} %broadcast_in_dim.24), channel_id=1, replica_groups=mesh['section'=8,'seq'=2,'tensor'=8] {'tensor'}, dimensions={0} | all-to-all | bytes 1179648 | tf_op jit(solution)/shard_map/all_to_all | solution.py:36
  59.2 1.2 key_value.10
  60.4 3.0 early.10.done_ref
  63.4 1.4 collective-permute-start.3
  64.9 0.8 collective-permute-done.3.other_ref.past_other_ref
  65.8 13.2 %all_to_all.98.arrived_ref = bf16[8,288,128]{2,1,0:T(8,128)(2,1)S(1)} all-to-all(bf16[8,288,128]{2,1,0:T(8,128)(2,1)S(1)} %late.10), channel_id=1, replica_groups=mesh['section'=8,'seq'=2,'tensor'=8] {'tensor'}, dimensions={0} | all-to-all | bytes 1179648 | tf_op jit(solution)/shard_map/all_to_all | solution.py:36
  80.0 11.9 %all_to_all.99.x_ref = bf16[8,288,128]{2,1,0:T(8,128)(2,1)S(1)} all-to-all(bf16[8,288,128]{2,1,0:T(8,128)(2,1)S(1)} %broadcast_in_dim.25), channel_id=1, replica_groups=mesh['section'=8,'seq'=2,'tensor'=8] {'tensor'}, dimensions={0} | all-to-all | bytes 1179648 | tf_op jit(solution)/shard_map/all_to_all | solution.py:36
  91.9 1.2 key_value.11
  93.1 3.0 early.11.done_ref
  96.1 1.0 collective-permute-start.5
  97.3 0.8 collective-permute-done.5.other_ref.past_other_ref
  98.2 13.2 %all_to_all.100.arrived_ref = bf16[8,288,128]{2,1,0:T(8,128)(2,1)S(1)} all-to-all(bf16[8,288,128]{2,1,0:T(8,128)(2,1)S(1)} %late.11), channel_id=1, replica_groups=mesh['section'=8,'seq'=2,'tensor'=8] {'tensor'}, dimensions={0} | all-to-all | bytes 1179648 | tf_op jit(solution)/shard_map/all_to_all | solution.py:36
  112.4 11.9 %all_to_all.101.x_ref = bf16[8,288,128]{2,1,0:T(8,128)(2,1)S(1)} all-to-all(bf16[8,288,128]{2,1,0:T(8,128)(2,1)S(1)} %broadcast_in_dim.26), channel_id=1, replica_groups=mesh['section'=8,'seq'=2,'tensor'=8] {'tensor'}, dimensions={0} | all-to-all | bytes 1179648 | tf_op jit(solution)/shard_map/all_to_all | solution.py:36
  124.3 1.2 key_value.12
  125.5 3.0 early.12.done_ref
  128.5 1.0 collective-permute-start.7
  129.7 0.8 collective-permute-done.7.other_ref.past_other_ref
  130.6 13.2 %all_to_all.102.arrived_ref = bf16[8,288,128]{2,1,0:T(8,128)(2,1)S(1)} all-to-all(bf16[8,288,128]{2,1,0:T(8,128)(2,1)S(1)} %late.12), channel_id=1, replica_groups=mesh['section'=8,'seq'=2,'tensor'=8] {'tensor'}, dimensions={0} | all-to-all | bytes 1179648 | tf_op jit(solution)/shard_map/all_to_all | solution.py:36
  144.8 11.9 %all_to_all.103.x_ref = bf16[8,288,128]{2,1,0:T(8,128)(2,1)S(1)} all-to-all(bf16[8,288,128]{2,1,0:T(8,128)(2,1)S(1)} %broadcast_in_dim.27), channel_id=1, replica_groups=mesh['section'=8,'seq'=2,'tensor'=8] {'tensor'}, dimensions={0} | all-to-all | bytes 1179648 | tf_op jit(solution)/shard_map/all_to_all | solution.py:36
  156.7 1.2 key_value.13
  157.9 3.0 early.13.done_ref
  160.9 1.0 collective-permute-start.9
  162.0 0.8 collective-permute-done.9.other_ref.past_other_ref
  163.0 13.2 %all_to_all.104.arrived_ref = bf16[8,288,128]{2,1,0:T(8,128)(2,1)S(1)} all-to-all(bf16[8,288,128]{2,1,0:T(8,128)(2,1)S(1)} %late.13), channel_id=1, replica_groups=mesh['section'=8,'seq'=2,'tensor'=8] {'tensor'}, dimensions={0} | all-to-all | bytes 1179648 | tf_op jit(solution)/shard_map/all_to_all | solution.py:36
  177.1 11.9 %all_to_all.105.x_ref = bf16[8,288,128]{2,1,0:T(8,128)(2,1)S(1)} all-to-all(bf16[8,288,128]{2,1,0:T(8,128)(2,1)S(1)} %broadcast_in_dim.28), channel_id=1, replica_groups=mesh['section'=8,'seq'=2,'tensor'=8] {'tensor'}, dimensions={0} | all-to-all | bytes 1179648 | tf_op jit(solution)/shard_map/all_to_all | solution.py:36
  189.0 1.2 key_value.14
  190.2 3.0 early.14.done_ref
  193.2 1.0 collective-permute-start.11
  194.4 0.8 collective-permute-done.11.other_ref.past_other_ref
  195.4 13.2 %all_to_all.106.arrived_ref = bf16[8,288,128]{2,1,0:T(8,128)(2,1)S(1)} all-to-all(bf16[8,288,128]{2,1,0:T(8,128)(2,1)S(1)} %late.14), channel_id=1, replica_groups=mesh['section'=8,'seq'=2,'tensor'=8] {'tensor'}, dimensions={0} | all-to-all | bytes 1179648 | tf_op jit(solution)/shard_map/all_to_all | solution.py:36
  209.5 11.9 %all_to_all.107.x_ref = bf16[8,288,128]{2,1,0:T(8,128)(2,1)S(1)} all-to-all(bf16[8,288,128]{2,1,0:T(8,128)(2,1)S(1)} %broadcast_in_dim.29), channel_id=1, replica_groups=mesh['section'=8,'seq'=2,'tensor'=8] {'tensor'}, dimensions={0} | all-to-all | bytes 1179648 | tf_op jit(solution)/shard_map/all_to_all | solution.py:36
  221.4 1.2 key_value.15
  222.6 3.0 early.15.done_ref
  225.6 1.0 collective-permute-start.13
  227.7 12.6 %all_to_all.108.arrived_ref = bf16[8,288,128]{2,1,0:T(8,128)(2,1)S(1)} all-to-all(bf16[8,288,128]{2,1,0:T(8,128)(2,1)S(1)} %late.15), channel_id=1, replica_groups=mesh['section'=8,'seq'=2,'tensor'=8] {'tensor'}, dimensions={0} | all-to-all | bytes 1179648 | tf_op jit(solution)/shard_map/all_to_all | solution.py:36
  240.6 1.3 collective-permute-start.14
  241.9 33.7 %collective-permute-done.14.held_ref = bf16[288,128]{1,0:T(8,128)(2,1)S(1)} collective-permute-done((bf16[288,128]{1,0:T(8,128)(2,1)S(1)}, bf16[288,128]{1,0:T(8,128)(2,1)S(1)}, u32[]{:S(2)}, u32[]{:S(2)}) %collective-permute-start.14) | collective-permute-done | bytes 73760 | tf_op jit(solution)/shard_map/ppermute | solution.py:422
  275.7 11.9 %all_to_all.109.x_ref = bf16[8,288,128]{2,1,0:T(8,128)(2,1)S(1)} all-to-all(bf16[8,288,128]{2,1,0:T(8,128)(2,1)S(1)} %broadcast_in_dim.30), channel_id=1, replica_groups=mesh['section'=8,'seq'=2,'tensor'=8] {'tensor'}, dimensions={0} | all-to-all | bytes 1179648 | tf_op jit(solution)/shard_map/all_to_all | solution.py:36
  287.6 1.2 key_value.16
  288.8 3.0 early.16.done_ref
  291.8 2.8 collective-permute-start.15
  294.7 0.8 collective-permute-done.15.other_ref.past_other_ref
  295.6 13.2 %all_to_all.110.arrived_ref = bf16[8,288,128]{2,1,0:T(8,128)(2,1)S(1)} all-to-all(bf16[8,288,128]{2,1,0:T(8,128)(2,1)S(1)} %late.16), channel_id=1, replica_groups=mesh['section'=8,'seq'=2,'tensor'=8] {'tensor'}, dimensions={0} | all-to-all | bytes 1179648 | tf_op jit(solution)/shard_map/all_to_all | solution.py:36
  309.0 1.3 collective-permute-start.16
  310.3 4.5 %collective-permute-done.16.held_ref = bf16[288,128]{1,0:T(8,128)(2,1)S(1)} collective-permute-done((bf16[288,128]{1,0:T(8,128)(2,1)S(1)}, bf16[288,128]{1,0:T(8,128)(2,1)S(1)}, u32[]{:S(2)}, u32[]{:S(2)}) %collective-permute-start.16) | collective-permute-done | bytes 73760 | tf_op jit(solution)/shard_map/ppermute | solution.py:422
  314.8 12.0 %all_to_all.111.x_ref = bf16[8,288,128]{2,1,0:T(8,128)(2,1)S(1)} all-to-all(bf16[8,288,128]{2,1,0:T(8,128)(2,1)S(1)} %broadcast_in_dim.31), channel_id=1, replica_groups=mesh['section'=8,'seq'=2,'tensor'=8] {'tensor'}, dimensions={0} | all-to-all | bytes 1179648 | tf_op jit(solution)/shard_map/all_to_all | solution.py:36
  326.8 1.2 key_value.17
  328.0 3.0 early.17.done_ref
  331.0 1.7 collective-permute-start.17
  332.9 0.8 collective-permute-done.17.other_ref
  333.8 13.2 %all_to_all.112.arrived_ref = bf16[8,288,128]{2,1,0:T(8,128)(2,1)S(1)} all-to-all(bf16[8,288,128]{2,1,0:T(8,128)(2,1)S(1)} %late.17), channel_id=1, replica_groups=mesh['section'=8,'seq'=2,'tensor'=8] {'tensor'}, dimensions={0} | all-to-all | bytes 1179648 | tf_op jit(solution)/shard_map/all_to_all | solution.py:36
  347.4 15.0 %all_to_all.113 = bf16[16,2,8,576]{3,2,1,0:T(8,128)(2,1)S(1)} all-to-all(bf16[16,2,8,576]{3,2,1,0:T(8,128)(2,1)S(1)} %bitcast.14), channel_id=1, replica_groups=mesh['section'=8,'seq'=2,'tensor'=8] {'seq','tensor'}, dimensions={0} | all-to-all | bytes 589824 | tf_op jit(solution)/shard_map/all_to_all | solution.py:36
  362.4 0.8 order.1
  (84 shorter events, 11.6 us)
Async XLA Ops:
  0.0 23.0 %copy-start.2 = (bf16[1,4608,256]{2,1,0:T(8,128)(2,1)S(1)}, bf16[1,4608,256]{2,1,0:T(8,128)(2,1)}, u32[]{:S(2)}) copy-start(bf16[1,4608,256]{2,1,0:T(8,128)(2,1)} %wk_ref.17) | copy-start | bytes 7077892
  0.0 2.4 collective-permute-start
  0.7 32.7 %slice-start = ((s8[4718592]{0:T(1024)(128)(4,1)}), s8[524288]{0:T(1024)(128)(4,1)S(1)}, s32[]{:S(2)}) async-start(s8[4718592]{0:T(1024)(128)(4,1)} %bitcast.12), calls=%async_computation.19 | async-start | bytes 1048576
  1.8 24.8 %copy-start = (bf16[1,4608,512]{2,1,0:T(8,128)(2,1)S(1)}, bf16[1,4608,512]{2,1,0:T(8,128)(2,1)}, u32[]{:S(2)}) copy-start(bf16[1,4608,512]{2,1,0:T(8,128)(2,1)} %wq_ref.35) | copy-start | bytes 14155780
  2.5 1.2 copy-start.7
  23.0 1.7 copy-start.3
  24.7 0.7 copy-start.5
  26.7 2.3 copy-start.1
  29.0 4.4 %slice-start.1 = ((s8[4718592]{0:T(1024)(128)(4,1)}), s8[4194304]{0:T(1024)(128)(4,1)S(1)}, s32[]{:S(2)}) async-start(s8[4718592]{0:T(1024)(128)(4,1)} %bitcast.12), calls=%async_computation.20 | async-start | bytes 8388608
  32.0 1.3 collective-permute-start.1
  32.2 14.0 %copy-start.6 = (bf16[1,4608]{1,0:T(2,128)(2,1)S(1)}, bf16[1,4608]{1,0:T(2,128)(2,1)}, u32[]{:S(2)}) copy-start(bf16[1,4608]{1,0:T(2,128)(2,1)} %gain_ref.35) | copy-start | bytes 27652
  32.2 26.9 %copy-start.4 = (bf16[1,4608,256]{2,1,0:T(8,128)(2,1)S(1)}, bf16[1,4608,256]{2,1,0:T(8,128)(2,1)}, u32[]{:S(2)}) copy-start(bf16[1,4608,256]{2,1,0:T(8,128)(2,1)} %wv_ref.17) | copy-start | bytes 7077892
  46.4 0.7 collective-permute-start.2
  63.4 2.3 collective-permute-start.3
  79.2 0.7 collective-permute-start.4
  96.1 1.9 collective-permute-start.5
  111.6 0.7 collective-permute-start.6
  128.5 2.0 collective-permute-start.7
  144.0 0.7 collective-permute-start.8
  160.9 1.9 collective-permute-start.9
  176.4 0.7 collective-permute-start.10
  193.2 2.0 collective-permute-start.11
  208.7 0.7 collective-permute-start.12
  225.6 1.9 collective-permute-start.13
  240.6 35.0 %collective-permute-start.14 = (bf16[288,128]{1,0:T(8,128)(2,1)S(1)}, bf16[288,128]{1,0:T(8,128)(2,1)S(1)}, u32[]{:S(2)}, u32[]{:S(2)}) collective-permute-start(bf16[288,128]{1,0:T(8,128)(2,1)S(1)} %combine.15.refs_6_), channel_id=1, source_target_pairs={{80,96},{96,112},{81,97},{97,113},{82,98},{98,114},{83,99},{99,115... | collective-permute-start | bytes 221192 | tf_op jit(solution)/shard_map/ppermute | solution.py:422
  291.8 3.7 %collective-permute-start.15 = (bf16[64,512]{1,0:T(8,128)(2,1)S(1)}, bf16[64,512]{1,0:T(8,128)(2,1)S(1)}, u32[]{:S(2)}, u32[]{:S(2)}) collective-permute-start(bf16[64,512]{1,0:T(8,128)(2,1)S(1)} %get-tuple-element.113.own_ref.past_own_ref), channel_id=1, source_target_pairs={{0,8},{8,0},{1,9},{9,1},{2,10},{10,2},{3,11},{11,3},{4,12},{12,4},... | collective-permute-start | bytes 196616 | tf_op jit(solution)/shard_map/ppermute | solution.py:415
  309.0 5.8 %collective-permute-start.16 = (bf16[288,128]{1,0:T(8,128)(2,1)S(1)}, bf16[288,128]{1,0:T(8,128)(2,1)S(1)}, u32[]{:S(2)}, u32[]{:S(2)}) collective-permute-start(bf16[288,128]{1,0:T(8,128)(2,1)S(1)} %combine.16.refs_7_), channel_id=1, source_target_pairs={{96,112},{97,113},{98,114},{99,115},{100,116},{101,117},{102,118},... | collective-permute-start | bytes 221192 | tf_op jit(solution)/shard_map/ppermute | solution.py:422
  331.0 2.6 collective-permute-start.17

commit v7 on v6

--- a/solution.py
+++ b/solution.py
@@ -230,7 +230,8 @@
         out_ref[t, whole * sent:] = fold.astype(bf16)
 
 
-def gather_kernel(facts_ref, arrived_ref, full_ref, held_ref, next_ref, flat_ref):
+def gather_kernel(facts_ref, arrived_ref, *refs):
+    full_ref, held_ref, next_ref, flat_ref = refs[-4:]
     peers = full_ref.shape[0]
     rows = peers * OWN
     part = flat_ref.shape[1] // peers
@@ -399,12 +400,12 @@
             jax.ShapeDtypeStruct(block, bf16),
             jax.ShapeDtypeStruct(block, bf16),
         ),
-        in_specs=[VMEM, VMEM],
+        in_specs=[VMEM] * 5,
         out_specs=(VMEM, VMEM, VMEM),
         scratch_shapes=[pltpu.VMEM((rows + own, width), f32)],
-        compiler_params=limit(6),
+        compiler_params=limit(16),
         name="gather",
-    )(facts, exchange(pieces, "tensor"))
+    )(facts, exchange(pieces, "tensor"), w_value, pre_gain, w_out)
 
     past = (no_past, no_past)
     made = []

time: 364 us -> 366 us (level)
  no operation moved by 1% of the time
where the time goes in v7:
time: 366 us; the launch traced here: 365 us
  blocking collectives  247 us (67%)
  waiting for transfers between devices  45.4 us (12%)
  Pallas kernels  43.8 us (12%)
  starting transfers between devices  18.3 us (5%)
  local copies, waits for them, and re-layouts  9.62 us (3%)
    all_to_all x19, blocking collectives, exchange(): return lax.all_to_all(pieces, axes, split_axis=0, concat_axis=0, tiled=True)  247 us
    ppermute x8, waiting for transfers between devices, body(): held = lax.ppermute(made[-1], 'section', [(i, i + 1) for i in busy])  38.3 us
    pallas_call x9, Pallas kernels, body(): early(tick)  27.1 us
    ppermute x9, starting transfers between devices, body(): kv_other = lax.ppermute(kv_own, 'seq', [(0, 1), (1, 0)])  11.1 us
    pallas_call x9, Pallas kernels, body(): key_value(tick)(facts, full, pre_gain, cos_full, sin_full, w_key, w_value)  10.6 us
    unnamed x20, local copies, waits for them, and re-layouts  8.03 us
  transfers between devices with their start and end apart: 18, of which 11 were waited for; matrix products, arithmetic and copies ran while one was open for 0% of the time, Pallas kernels for 0%

profile of v7, /device:TPU:57, one launch (start us, length us, event | category | flops | bytes accessed | tf_op | source)
XLA Modules:
  0.0 365.2 jit_solution(8879969287112031229)
XLA Ops:
  0.8 0.8 fusion.1
  2.5 1.0 copy-done.9
  3.8 18.9 %all_to_all.95.arrived_ref = bf16[8,328,128]{2,1,0:T(8,128)(2,1)S(1)} all-to-all(bf16[8,328,128]{2,1,0:T(8,128)(2,1)S(1)} %pick.1), channel_id=1, replica_groups=mesh['section'=8,'seq'=2,'tensor'=8] {'tensor'}, dimensions={0} | all-to-all | bytes 1343488 | tf_op jit(solution)/shard_map/all_to_all | solution.py:36
  22.6 2.3 copy-done
  25.0 1.7 copy-done.3
  27.7 1.2 key_value.9
  28.9 0.8 copy-done.1
  29.7 1.4 copy-done.2
  31.1 3.0 early.9.done_ref
  34.4 1.1 collective-permute-done.1.other_ref.past_other_ref
  35.6 12.7 %all_to_all.96.arrived_ref = bf16[8,288,128]{2,1,0:T(8,128)(2,1)S(1)} all-to-all(bf16[8,288,128]{2,1,0:T(8,128)(2,1)S(1)} %late.9), channel_id=1, replica_groups=mesh['section'=8,'seq'=2,'tensor'=8] {'tensor'}, dimensions={0} | all-to-all | bytes 1179648 | tf_op jit(solution)/shard_map/all_to_all | solution.py:36
  49.3 12.0 %all_to_all.97.x_ref = bf16[8,288,128]{2,1,0:T(8,128)(2,1)S(1)} all-to-all(bf16[8,288,128]{2,1,0:T(8,128)(2,1)S(1)} %broadcast_in_dim.24), channel_id=1, replica_groups=mesh['section'=8,'seq'=2,'tensor'=8] {'tensor'}, dimensions={0} | all-to-all | bytes 1179648 | tf_op jit(solution)/shard_map/all_to_all | solution.py:36
  61.3 1.2 key_value.10
  62.5 3.0 early.10.done_ref
  65.5 1.4 collective-permute-start.3
  67.0 0.8 collective-permute-done.3.other_ref.past_other_ref
  67.9 13.2 %all_to_all.98.arrived_ref = bf16[8,288,128]{2,1,0:T(8,128)(2,1)S(1)} all-to-all(bf16[8,288,128]{2,1,0:T(8,128)(2,1)S(1)} %late.10), channel_id=1, replica_groups=mesh['section'=8,'seq'=2,'tensor'=8] {'tensor'}, dimensions={0} | all-to-all | bytes 1179648 | tf_op jit(solution)/shard_map/all_to_all | solution.py:36
  82.1 11.9 %all_to_all.99.x_ref = bf16[8,288,128]{2,1,0:T(8,128)(2,1)S(1)} all-to-all(bf16[8,288,128]{2,1,0:T(8,128)(2,1)S(1)} %broadcast_in_dim.25), channel_id=1, replica_groups=mesh['section'=8,'seq'=2,'tensor'=8] {'tensor'}, dimensions={0} | all-to-all | bytes 1179648 | tf_op jit(solution)/shard_map/all_to_all | solution.py:36
  94.0 1.2 key_value.11
  95.2 3.0 early.11.done_ref
  98.2 1.0 collective-permute-start.5
  99.3 0.8 collective-permute-done.5.other_ref.past_other_ref
  100.3 13.2 %all_to_all.100.arrived_ref = bf16[8,288,128]{2,1,0:T(8,128)(2,1)S(1)} all-to-all(bf16[8,288,128]{2,1,0:T(8,128)(2,1)S(1)} %late.11), channel_id=1, replica_groups=mesh['section'=8,'seq'=2,'tensor'=8] {'tensor'}, dimensions={0} | all-to-all | bytes 1179648 | tf_op jit(solution)/shard_map/all_to_all | solution.py:36
  114.4 11.9 %all_to_all.101.x_ref = bf16[8,288,128]{2,1,0:T(8,128)(2,1)S(1)} all-to-all(bf16[8,288,128]{2,1,0:T(8,128)(2,1)S(1)} %broadcast_in_dim.26), channel_id=1, replica_groups=mesh['section'=8,'seq'=2,'tensor'=8] {'tensor'}, dimensions={0} | all-to-all | bytes 1179648 | tf_op jit(solution)/shard_map/all_to_all | solution.py:36
  126.3 1.2 key_value.12
  127.5 3.0 early.12.done_ref
  130.5 1.0 collective-permute-start.7
  131.7 0.8 collective-permute-done.7.other_ref.past_other_ref
  132.6 13.2 %all_to_all.102.arrived_ref = bf16[8,288,128]{2,1,0:T(8,128)(2,1)S(1)} all-to-all(bf16[8,288,128]{2,1,0:T(8,128)(2,1)S(1)} %late.12), channel_id=1, replica_groups=mesh['section'=8,'seq'=2,'tensor'=8] {'tensor'}, dimensions={0} | all-to-all | bytes 1179648 | tf_op jit(solution)/shard_map/all_to_all | solution.py:36
  146.8 11.9 %all_to_all.103.x_ref = bf16[8,288,128]{2,1,0:T(8,128)(2,1)S(1)} all-to-all(bf16[8,288,128]{2,1,0:T(8,128)(2,1)S(1)} %broadcast_in_dim.27), channel_id=1, replica_groups=mesh['section'=8,'seq'=2,'tensor'=8] {'tensor'}, dimensions={0} | all-to-all | bytes 1179648 | tf_op jit(solution)/shard_map/all_to_all | solution.py:36
  158.7 1.2 key_value.13
  159.8 3.0 early.13.done_ref
  162.9 1.0 collective-permute-start.9
  164.0 0.8 collective-permute-done.9.other_ref.past_other_ref
  165.0 13.2 %all_to_all.104.arrived_ref = bf16[8,288,128]{2,1,0:T(8,128)(2,1)S(1)} all-to-all(bf16[8,288,128]{2,1,0:T(8,128)(2,1)S(1)} %late.13), channel_id=1, replica_groups=mesh['section'=8,'seq'=2,'tensor'=8] {'tensor'}, dimensions={0} | all-to-all | bytes 1179648 | tf_op jit(solution)/shard_map/all_to_all | solution.py:36
  179.1 11.9 %all_to_all.105.x_ref = bf16[8,288,128]{2,1,0:T(8,128)(2,1)S(1)} all-to-all(bf16[8,288,128]{2,1,0:T(8,128)(2,1)S(1)} %broadcast_in_dim.28), channel_id=1, replica_groups=mesh['section'=8,'seq'=2,'tensor'=8] {'tensor'}, dimensions={0} | all-to-all | bytes 1179648 | tf_op jit(solution)/shard_map/all_to_all | solution.py:36
  191.0 1.2 key_value.14
  192.2 3.0 early.14.done_ref
  195.2 1.0 collective-permute-start.11
  196.4 0.8 collective-permute-done.11.other_ref.past_other_ref
  197.3 13.2 %all_to_all.106.arrived_ref = bf16[8,288,128]{2,1,0:T(8,128)(2,1)S(1)} all-to-all(bf16[8,288,128]{2,1,0:T(8,128)(2,1)S(1)} %late.14), channel_id=1, replica_groups=mesh['section'=8,'seq'=2,'tensor'=8] {'tensor'}, dimensions={0} | all-to-all | bytes 1179648 | tf_op jit(solution)/shard_map/all_to_all | solution.py:36
  211.5 11.9 %all_to_all.107.x_ref = bf16[8,288,128]{2,1,0:T(8,128)(2,1)S(1)} all-to-all(bf16[8,288,128]{2,1,0:T(8,128)(2,1)S(1)} %broadcast_in_dim.29), channel_id=1, replica_groups=mesh['section'=8,'seq'=2,'tensor'=8] {'tensor'}, dimensions={0} | all-to-all | bytes 1179648 | tf_op jit(solution)/shard_map/all_to_all | solution.py:36
  223.4 1.2 key_value.15
  224.5 3.0 early.15.done_ref
  227.6 1.0 collective-permute-start.13
  229.7 12.5 %all_to_all.108.arrived_ref = bf16[8,288,128]{2,1,0:T(8,128)(2,1)S(1)} all-to-all(bf16[8,288,128]{2,1,0:T(8,128)(2,1)S(1)} %late.15), channel_id=1, replica_groups=mesh['section'=8,'seq'=2,'tensor'=8] {'tensor'}, dimensions={0} | all-to-all | bytes 1179648 | tf_op jit(solution)/shard_map/all_to_all | solution.py:36
  242.4 1.3 collective-permute-start.14
  243.7 33.9 %collective-permute-done.14.held_ref = bf16[288,128]{1,0:T(8,128)(2,1)S(1)} collective-permute-done((bf16[288,128]{1,0:T(8,128)(2,1)S(1)}, bf16[288,128]{1,0:T(8,128)(2,1)S(1)}, u32[]{:S(2)}, u32[]{:S(2)}) %collective-permute-start.14) | collective-permute-done | bytes 73760 | tf_op jit(solution)/shard_map/ppermute | solution.py:423
  277.6 11.9 %all_to_all.109.x_ref = bf16[8,288,128]{2,1,0:T(8,128)(2,1)S(1)} all-to-all(bf16[8,288,128]{2,1,0:T(8,128)(2,1)S(1)} %broadcast_in_dim.30), channel_id=1, replica_groups=mesh['section'=8,'seq'=2,'tensor'=8] {'tensor'}, dimensions={0} | all-to-all | bytes 1179648 | tf_op jit(solution)/shard_map/all_to_all | solution.py:36
  289.5 1.2 key_value.16
  290.7 3.0 early.16.done_ref
  293.7 2.8 collective-permute-start.15
  296.6 0.8 collective-permute-done.15.other_ref.past_other_ref
  297.6 13.2 %all_to_all.110.arrived_ref = bf16[8,288,128]{2,1,0:T(8,128)(2,1)S(1)} all-to-all(bf16[8,288,128]{2,1,0:T(8,128)(2,1)S(1)} %late.16), channel_id=1, replica_groups=mesh['section'=8,'seq'=2,'tensor'=8] {'tensor'}, dimensions={0} | all-to-all | bytes 1179648 | tf_op jit(solution)/shard_map/all_to_all | solution.py:36
  310.9 1.3 collective-permute-start.16
  312.2 4.4 %collective-permute-done.16.held_ref = bf16[288,128]{1,0:T(8,128)(2,1)S(1)} collective-permute-done((bf16[288,128]{1,0:T(8,128)(2,1)S(1)}, bf16[288,128]{1,0:T(8,128)(2,1)S(1)}, u32[]{:S(2)}, u32[]{:S(2)}) %collective-permute-start.16) | collective-permute-done | bytes 73760 | tf_op jit(solution)/shard_map/ppermute | solution.py:423
  316.8 12.0 %all_to_all.111.x_ref = bf16[8,288,128]{2,1,0:T(8,128)(2,1)S(1)} all-to-all(bf16[8,288,128]{2,1,0:T(8,128)(2,1)S(1)} %broadcast_in_dim.31), channel_id=1, replica_groups=mesh['section'=8,'seq'=2,'tensor'=8] {'tensor'}, dimensions={0} | all-to-all | bytes 1179648 | tf_op jit(solution)/shard_map/all_to_all | solution.py:36
  328.7 1.2 key_value.17
  329.9 3.0 early.17.done_ref
  332.9 1.7 collective-permute-start.17
  334.8 0.8 collective-permute-done.17.other_ref
  335.7 13.2 %all_to_all.112.arrived_ref = bf16[8,288,128]{2,1,0:T(8,128)(2,1)S(1)} all-to-all(bf16[8,288,128]{2,1,0:T(8,128)(2,1)S(1)} %late.17), channel_id=1, replica_groups=mesh['section'=8,'seq'=2,'tensor'=8] {'tensor'}, dimensions={0} | all-to-all | bytes 1179648 | tf_op jit(solution)/shard_map/all_to_all | solution.py:36
  349.3 15.0 %all_to_all.113 = bf16[16,2,8,576]{3,2,1,0:T(8,128)(2,1)S(1)} all-to-all(bf16[16,2,8,576]{3,2,1,0:T(8,128)(2,1)S(1)} %bitcast.12), channel_id=1, replica_groups=mesh['section'=8,'seq'=2,'tensor'=8] {'seq','tensor'}, dimensions={0} | all-to-all | bytes 589824 | tf_op jit(solution)/shard_map/all_to_all | solution.py:36
  364.3 0.8 order.1
  (83 shorter events, 13.0 us)
Async XLA Ops:
  0.0 2.4 collective-permute-start
  2.3 25.4 %copy-start.5 = (bf16[1,4608,256]{2,1,0:T(8,128)(2,1)S(1)}, bf16[1,4608,256]{2,1,0:T(8,128)(2,1)}, u32[]{:S(2)}) copy-start(bf16[1,4608,256]{2,1,0:T(8,128)(2,1)} %wk_ref.17) | copy-start | bytes 7077892
  2.5 1.0 copy-start.9
  22.6 2.3 copy-start
  25.0 1.7 copy-start.3
  26.6 0.7 copy-start.6
  27.3 2.3 copy-start.1
  27.3 3.8 %copy-start.2 = (bf16[1,4608,512]{2,1,0:T(8,128)(2,1)S(1)}, bf16[1,4608,512]{2,1,0:T(8,128)(2,1)}, u32[]{:S(2)}) copy-start(bf16[1,4608,512]{2,1,0:T(8,128)(2,1)} %wq_ref.35) | copy-start | bytes 14155780
  34.1 1.3 collective-permute-start.1
  34.4 14.0 %copy-start.8 = (bf16[1,4608]{1,0:T(2,128)(2,1)S(1)}, bf16[1,4608]{1,0:T(2,128)(2,1)}, u32[]{:S(2)}) copy-start(bf16[1,4608]{1,0:T(2,128)(2,1)} %gain_ref.35) | copy-start | bytes 27652
  34.4 26.9 %copy-start.4 = (bf16[1,4608,256]{2,1,0:T(8,128)(2,1)S(1)}, bf16[1,4608,256]{2,1,0:T(8,128)(2,1)}, u32[]{:S(2)}) copy-start(bf16[1,4608,256]{2,1,0:T(8,128)(2,1)} %wv_ref.17) | copy-start | bytes 7077892
  34.4 26.9 %copy-start.7 = (bf16[1,4608]{1,0:T(2,128)(2,1)S(1)}, bf16[1,4608]{1,0:T(2,128)(2,1)}, u32[]{:S(2)}) copy-start(bf16[1,4608]{1,0:T(2,128)(2,1)} %gain_ref.34) | copy-start | bytes 27652
  48.5 0.7 collective-permute-start.2
  65.5 2.3 collective-permute-start.3
  81.3 0.7 collective-permute-start.4
  98.2 1.9 collective-permute-start.5
  113.6 0.7 collective-permute-start.6
  130.5 1.9 collective-permute-start.7
  146.0 0.7 collective-permute-start.8
  162.9 1.9 collective-permute-start.9
  178.3 0.7 collective-permute-start.10
  195.2 1.9 collective-permute-start.11
  210.7 0.7 collective-permute-start.12
  227.6 1.9 collective-permute-start.13
  242.4 35.2 %collective-permute-start.14 = (bf16[288,128]{1,0:T(8,128)(2,1)S(1)}, bf16[288,128]{1,0:T(8,128)(2,1)S(1)}, u32[]{:S(2)}, u32[]{:S(2)}) collective-permute-start(bf16[288,128]{1,0:T(8,128)(2,1)S(1)} %combine.15.refs_6_), channel_id=1, source_target_pairs={{80,96},{96,112},{81,97},{97,113},{82,98},{98,114},{83,99},{99,115... | collective-permute-start | bytes 221192 | tf_op jit(solution)/shard_map/ppermute | solution.py:423
  293.7 3.7 %collective-permute-start.15 = (bf16[64,512]{1,0:T(8,128)(2,1)S(1)}, bf16[64,512]{1,0:T(8,128)(2,1)S(1)}, u32[]{:S(2)}, u32[]{:S(2)}) collective-permute-start(bf16[64,512]{1,0:T(8,128)(2,1)S(1)} %get-tuple-element.113.own_ref.past_own_ref), channel_id=1, source_target_pairs={{0,8},{8,0},{1,9},{9,1},{2,10},{10,2},{3,11},{11,3},{4,12},{12,4},... | collective-permute-start | bytes 196616 | tf_op jit(solution)/shard_map/ppermute | solution.py:416
  310.9 5.7 %collective-permute-start.16 = (bf16[288,128]{1,0:T(8,128)(2,1)S(1)}, bf16[288,128]{1,0:T(8,128)(2,1)S(1)}, u32[]{:S(2)}, u32[]{:S(2)}) collective-permute-start(bf16[288,128]{1,0:T(8,128)(2,1)S(1)} %combine.16.refs_7_), channel_id=1, source_target_pairs={{96,112},{97,113},{98,114},{99,115},{100,116},{101,117},{102,118},... | collective-permute-start | bytes 221192 | tf_op jit(solution)/shard_map/ppermute | solution.py:423
  332.9 2.6 collective-permute-start.17
